TPU v7x, 16 devices: a whole 2x2x2 slice. The times are simulated.
16 devices in a mesh: tp: 4 (over z, y), cp: 4 (over x, core).
Axes of the slice: x: 2, y: 2, z: 2, core: 2. Of those that a mesh axis runs over, the one named last changes fastest.
Arguments:
- x_in: bfloat16 [32, 512, 3072], P(None, 'cp')
- grad_z: bfloat16 [32, 512, 3072], P(None, 'cp')
- seg_pos: int32 [32, 512], P(None, 'cp')
- norm_scale: bfloat16 [3072], replicated
- w_x: bfloat16 [3072, 3072], P(None, 'tp')
- b_x: bfloat16 [3072], P('tp')
- w_y: bfloat16 [3072, 3072], P(None, 'tp')
- b_y: bfloat16 [3072], P('tp')
- conv_w: bfloat16 [4, 3072], P(None, 'tp')
- conv_b: bfloat16 [3072], P('tp')
- w_a: bfloat16 [24, 128, 128], P('tp')
- b_a: bfloat16 [3072], P('tp')
- w_i: bfloat16 [24, 128, 128], P('tp')
- b_i: bfloat16 [3072], P('tp')
- a_param: float32 [3072], P('tp')
- w_out: bfloat16 [3072, 3072], P('tp')
- b_out: bfloat16 [3072], replicated
Outputs:
- output 1: bfloat16 [32, 512, 3072], P(None, 'cp')
- output 2: bfloat16 [32, 512, 3072], P(None, 'cp')
- output 3: float32 [3072], replicated
- output 4: float32 [3072, 3072], P(None, 'tp')
- output 5: float32 [3072], P('tp')
- output 6: float32 [3072, 3072], P(None, 'tp')
- output 7: float32 [3072], P('tp')
- output 8: float32 [4, 3072], P(None, 'tp')
- output 9: float32 [3072], P('tp')
- output 10: float32 [24, 128, 128], P('tp')
- output 11: float32 [3072], P('tp')
- output 12: float32 [24, 128, 128], P('tp')
- output 13: float32 [3072], P('tp')
- output 14: float32 [3072], P('tp')
- output 15: float32 [3072, 3072], P('tp')
- output 16: float32 [3072], replicated
All inputs are finite; a program needn't handle non-finite values.
Results may differ from a plain program's by a relative error of at most 0.00700116.
Values sent between devices are 32-bit elements.
A program may use at most 1 GiB of HBM per device.

v0:
```python
import functools
import jax
import jax.numpy as jnp
from jax import lax
from jax.sharding import PartitionSpec as P

NORM_EPS = 1e-6
CONV_WIDTH = 4
BORROW_ROWS = CONV_WIDTH - 1
IN_SPECS = (P(None, "cp", None), P(None, "cp", None), P(None, "cp"), P(), P(None, "tp"), P("tp"), P(None, "tp"), P("tp"), P(None, "tp"), P("tp"), P("tp", None, None), P("tp"), P("tp", None, None), P("tp"), P("tp"), P("tp", None), P())
OUT_SPECS = (P(None, "cp", None), P(None, "cp", None), P(), P(None, "tp"), P("tp"), P(None, "tp"), P("tp"), P(None, "tp"), P("tp"), P("tp", None, None), P("tp"), P("tp", None, None), P("tp"), P("tp"), P("tp", None), P())


def norm_apply(x_f, scale_f):
    mean_sq = jnp.mean(x_f * x_f, axis=-1, keepdims=True)
    return x_f * lax.rsqrt(mean_sq + NORM_EPS) * (1.0 + scale_f)


def gelu_tanh(pre_y):
    return jax.nn.gelu(pre_y, approximate=True)


def gate_math(pre_a, pre_i, conv_f, a_param, reset_mask):
    log_a = -8.0 * jax.nn.sigmoid(pre_a) * jax.nn.softplus(a_param)
    decays = jnp.where(reset_mask, 0.0, jnp.exp(log_a))
    multiplier = jnp.where(reset_mask, 1.0, jnp.sqrt(-jnp.expm1(2.0 * log_a)))
    return decays, multiplier * jax.nn.sigmoid(pre_i) * conv_f


def conv_apply(xb_ext, conv_w, conv_b, pos_t):
    n_rows = pos_t.shape[0]
    conv_wf = conv_w.astype(jnp.float32)
    conv_sum = conv_b.astype(jnp.float32)
    for tap_k in range(CONV_WIDTH):
        start_row = BORROW_ROWS - tap_k
        keep_mask = (pos_t >= tap_k)[:, :, None]
        conv_sum = conv_sum + jnp.where(keep_mask, xb_ext[start_row:start_row + n_rows], 0.0) * conv_wf[tap_k]
    return conv_sum


def conv_back(grad_conv, xb_ext, conv_w, pos_t):
    n_rows = pos_t.shape[0]
    conv_wf = conv_w.astype(jnp.float32)
    grad_ext = 0.0
    tap_grads = []
    for tap_k in range(CONV_WIDTH):
        start_row = BORROW_ROWS - tap_k
        masked = jnp.where((pos_t >= tap_k)[:, :, None], grad_conv, 0.0)
        tap_grads.append(jnp.sum(masked * xb_ext[start_row:start_row + n_rows], axis=(0, 1)))
        grad_ext = grad_ext + jnp.pad(masked * conv_wf[tap_k], ((start_row, tap_k), (0, 0), (0, 0)))
    return grad_ext, jnp.stack(tap_grads), jnp.sum(grad_conv, axis=(0, 1))


def local_scan(decays, drives):
    def scan_step(carry_in, inputs_t):
        state_h, prod_a = carry_in
        state_h = inputs_t[0] * state_h + inputs_t[1]
        prod_a = inputs_t[0] * prod_a
        return (state_h, prod_a), (state_h, prod_a)
    zeros_h = jnp.zeros(decays.shape[1:], jnp.float32)
    _, (states, run_prods) = lax.scan(scan_step, (zeros_h, jnp.ones_like(zeros_h)), (decays, drives))
    return states, run_prods


def local_scan_back(decays, grad_out):
    def scan_step(carry_in, inputs_t):
        next_grad, prod_a = carry_in
        grad_h = inputs_t[1] + next_grad
        return (inputs_t[0] * grad_h, inputs_t[0] * prod_a), (grad_h, prod_a)
    zeros_h = jnp.zeros(decays.shape[1:], jnp.float32)
    (head_grad, total_prod), (grad_loc, suffix_prods) = lax.scan(scan_step, (zeros_h, jnp.ones_like(zeros_h)), (decays, grad_out), reverse=True)
    return grad_loc, suffix_prods, head_grad, total_prod


def carry_in_forward(end_info, cp_index):
    def compose(carry_in, piece_info):
        return piece_info[0] * carry_in + piece_info[1], carry_in
    _, entering = lax.scan(compose, jnp.zeros_like(end_info[0, 0]), end_info)
    return lax.dynamic_index_in_dim(entering, cp_index, 0, keepdims=False)


def carry_in_backward(head_info, cp_index):
    def compose(carry_in, piece_info):
        return piece_info[0] * carry_in + piece_info[1], carry_in
    _, entering = lax.scan(compose, jnp.zeros_like(head_info[0, 0]), head_info, reverse=True)
    return lax.dynamic_index_in_dim(entering, cp_index, 0, keepdims=False)


def shard_body(x_in, grad_z, seg_pos, norm_scale, w_x, b_x, w_y, b_y, conv_w, conv_b, w_a, b_a, w_i, b_i, a_param, w_out, b_out, fwd_perm, back_perm):
    cp_index = lax.axis_index("cp")
    n_tok = x_in.shape[1]
    n_blocks, blk_width = w_a.shape[0], w_a.shape[1]
    x_f = x_in.astype(jnp.float32)
    normed_f, norm_pull = jax.vjp(norm_apply, x_f, norm_scale.astype(jnp.float32))
    normed = normed_f.astype(jnp.bfloat16)
    pre_y = jnp.einsum("btd,dl->tbl", normed, w_y, preferred_element_type=jnp.float32) + b_y
    y_act, gelu_pull = jax.vjp(gelu_tanh, pre_y)
    x_branch = (jnp.einsum("btd,dl->tbl", normed, w_x, preferred_element_type=jnp.float32) + b_x).astype(jnp.bfloat16).astype(jnp.float32)
    borrowed = lax.ppermute(x_branch[n_tok - BORROW_ROWS:], "cp", fwd_perm)
    xb_ext = jnp.concatenate([borrowed, x_branch], axis=0)
    pos_t = seg_pos.T
    conv_out = conv_apply(xb_ext, conv_w, conv_b, pos_t).astype(jnp.bfloat16)
    blocks = conv_out.reshape(conv_out.shape[0], conv_out.shape[1], n_blocks, blk_width)
    pre_a = jnp.einsum("tbhk,hkj->tbhj", blocks, w_a, preferred_element_type=jnp.float32).reshape(conv_out.shape) + b_a
    pre_i = jnp.einsum("tbhk,hkj->tbhj", blocks, w_i, preferred_element_type=jnp.float32).reshape(conv_out.shape) + b_i
    gate_fn = functools.partial(gate_math, reset_mask=(pos_t == 0)[:, :, None])
    (decays, drives), gate_pull = jax.vjp(gate_fn, pre_a, pre_i, conv_out.astype(jnp.float32), a_param)
    states, run_prods = local_scan(decays, drives)
    end_info = lax.all_gather(jnp.stack([run_prods[-1], states[-1]]), "cp")
    state_in = carry_in_forward(end_info, cp_index)
    hidden = states + run_prods * state_in
    prev_hidden = jnp.concatenate([state_in[None], hidden[:-1]], axis=0)
    mixed_v = (hidden * y_act).astype(jnp.bfloat16)
    out_part = jnp.einsum("tbl,ld->btd", mixed_v, w_out, preferred_element_type=jnp.float32)
    out_proj = lax.psum(out_part, "tp") + b_out
    z_out = (x_f + out_proj).astype(jnp.bfloat16)

    d_mixed = jnp.einsum("btd,ld->tbl", grad_z, w_out, preferred_element_type=jnp.float32)
    g_w_out = jnp.einsum("tbl,btd->ld", mixed_v, grad_z, preferred_element_type=jnp.float32)
    g_b_out = jnp.sum(grad_z, axis=(0, 1), dtype=jnp.float32)
    d_pre_y = gelu_pull(d_mixed * hidden)[0]
    grad_loc, suffix_prods, head_grad, total_prod = local_scan_back(decays, d_mixed * y_act)
    head_info = lax.all_gather(jnp.stack([total_prod, head_grad]), "cp")
    grad_in = carry_in_backward(head_info, cp_index)
    d_hidden = grad_loc + suffix_prods * grad_in
    d_pre_a, d_pre_i, d_conv_f, g_a_param = gate_pull((d_hidden * prev_hidden, d_hidden))
    d_pre_a16 = d_pre_a.astype(jnp.bfloat16).reshape(blocks.shape)
    d_pre_i16 = d_pre_i.astype(jnp.bfloat16).reshape(blocks.shape)
    g_w_a = jnp.einsum("tbhk,tbhj->hkj", blocks, d_pre_a16, preferred_element_type=jnp.float32)
    g_w_i = jnp.einsum("tbhk,tbhj->hkj", blocks, d_pre_i16, preferred_element_type=jnp.float32)
    d_gate_in = jnp.einsum("tbhj,hkj->tbhk", d_pre_a16, w_a, preferred_element_type=jnp.float32) + jnp.einsum("tbhj,hkj->tbhk", d_pre_i16, w_i, preferred_element_type=jnp.float32)
    d_conv = d_conv_f + d_gate_in.reshape(conv_out.shape)
    grad_ext, g_conv_w, g_conv_b = conv_back(d_conv, xb_ext, conv_w, pos_t)
    returned = lax.ppermute(grad_ext[:BORROW_ROWS], "cp", back_perm)
    d_branch = jnp.concatenate([grad_ext[BORROW_ROWS:n_tok], grad_ext[n_tok:] + returned], axis=0)
    d_branch16 = d_branch.astype(jnp.bfloat16)
    d_pre_y16 = d_pre_y.astype(jnp.bfloat16)
    g_w_x = jnp.einsum("btd,tbl->dl", normed, d_branch16, preferred_element_type=jnp.float32)
    g_w_y = jnp.einsum("btd,tbl->dl", normed, d_pre_y16, preferred_element_type=jnp.float32)
    d_norm_part = jnp.einsum("tbl,dl->btd", d_branch16, w_x, preferred_element_type=jnp.float32) + jnp.einsum("tbl,dl->btd", d_pre_y16, w_y, preferred_element_type=jnp.float32)
    d_normed = lax.psum(d_norm_part, "tp")
    d_x_norm, g_scale = norm_pull(d_normed)
    grad_x = (grad_z.astype(jnp.float32) + d_x_norm).astype(jnp.bfloat16)
    grad_sums = lax.psum((g_scale, g_w_x, jnp.sum(d_branch, axis=(0, 1)), g_w_y, jnp.sum(d_pre_y, axis=(0, 1)), g_conv_w, g_conv_b, g_w_a, jnp.sum(d_pre_a, axis=(0, 1)), g_w_i, jnp.sum(d_pre_i, axis=(0, 1)), g_a_param, g_w_out, g_b_out), "cp")
    return (z_out, grad_x) + tuple(grad_sums)


def solution(mesh):
    cp_size = mesh.shape["cp"]
    fwd_perm = [(dev_j, dev_j + 1) for dev_j in range(cp_size - 1)]
    back_perm = [(dev_j + 1, dev_j) for dev_j in range(cp_size - 1)]
    per_device = functools.partial(shard_body, fwd_perm=fwd_perm, back_perm=back_perm)
    return jax.shard_map(per_device, mesh=mesh, in_specs=IN_SPECS, out_specs=OUT_SPECS, check_vma=False)
```

profile of v0, /device:TPU:0, one launch (start us, length us, event | category | flops | bytes accessed | tf_op | source)
XLA Modules:
  0.0 4292.1 jit_solution(5954375390950168095)
XLA Ops:
  8.7 10.5 fusion.12
  19.9 23.5 convert_bitcast_fusion
  43.4 4.5 copy-done.3
  52.1 26.4 fusion.36
  78.5 33.1 bitcast_multiply_fusion.5
  111.8 29.0 add_convert_fusion
  140.8 8.8 copy.97
  149.7 9.1 fusion.65
  158.9 11.3 copy.104
  170.2 12.6 copy.105
  182.8 9.1 fusion.62
  191.9 11.3 copy.100
  203.2 12.6 copy.101
  215.8 11.9 exponential_select_fusion
  227.8 16.4 copy.108
  244.1 6.0 broadcast.107.clone.1
  250.1 6.0 broadcast.107
  256.2 1095.0 %while.70 = (s32[]{:T(128)}, f32[32,768]{1,0:T(8,128)S(1)}, f32[32,768]{1,0:T(8,128)S(1)}, f32[128,32,768]{2,0,1:T(8,128)}, f32[128,32,768]{2,0,1:T(8,128)}, /*i...) while((s32[]{:T(128)}, f32[32,768]{1,0:T(8,128)S(1)}, ...), condition=%wide.region_7.8_spmd.clone, body=%wide.region_6.7_spmd.clone.sunk | while | flops 122884 | bytes 1769619 | solution.py:71
  531.7 3.1 dynamic_update_slice.55
  1147.9 3.1 dynamic_update_slice.55
  1156.5 3.1 dynamic_update_slice.55
  1165.1 3.1 dynamic_update_slice.55
  1173.6 3.1 dynamic_update_slice.55
  1182.2 3.1 dynamic_update_slice.55
  1190.8 3.1 dynamic_update_slice.55
  1199.4 3.1 dynamic_update_slice.55
  1208.0 3.1 dynamic_update_slice.55
  1351.2 9.5 all-gather.1
  1361.1 34.8 fusion.89
  1395.9 364.9 %while.68 = (s32[]{:T(128)}, f32[32,768]{1,0:T(8,128)S(1)}, f32[32,768]{1,0:T(8,128)S(1)}, f32[128,32,768]{2,1,0:T(8,128)}, f32[128,32,768]{2,1,0:T(8,128)}, /*i...) while((s32[]{:T(128)}, f32[32,768]{1,0:T(8,128)S(1)}, ...), condition=%wide.region_2.3_spmd.clone, body=%wide.region_1.2_spmd.clone.sunk | while | flops 122883 | bytes 983159 | solution.py:61
  1762.6 8.9 all-gather
  1771.5 16.6 while.69
  1789.2 25.2 fusion.92
  1814.4 10.9 multiply_convert_fusion
  1825.3 28.3 multiply_reduce_fusion
  1853.6 10.2 fusion.77
  1863.8 8.7 copy.119
  1872.4 8.8 copy.121
  1881.2 4.6 fusion.40
  1885.8 9.6 add_bitcast_fusion.1
  1895.4 11.3 copy.123
  1906.8 12.7 copy.124
  1919.5 29.4 convolution_bitcast_fusion
  1949.0 27.8 fusion.57
  1976.9 41.2 multiply_reduce_fusion.3
  2018.1 16.4 select_multiply_fusion.3
  2034.5 4.9 pad_add_fusion.1
  2040.7 18.4 pad_add_fusion
  2059.0 9.3 slice.140
  2071.9 41.3 add_bitcast_fusion
  2113.5 7.3 convolution_bitcast_fusion.3
  2120.7 7.3 convolution_bitcast_fusion.2
  2128.1 25.3 convolution_bitcast_fusion.1
  2153.4 26.3 fusion.47
  2179.7 27.1 fusion.44
  2207.7 6.3 slice_reduce_fusion
  2213.9 1559.0 %all-reduce.12.cloned.1.call-done = (f32[32,128,3072]{2,1,0:T(8,128)}, f32[32,128,3072]{2,1,0:T(8,128)}) async-done(((f32[32,128,3072]{2,1,0:T(8,128)}, f32[32,128,3072]{2,1,0:T(8,128)}), (f32[32,128,3072]{2,1,0:T(8,128)}, f32[32,128,3072]{2,1,0:T(8,128)})) %all-reduce.12.cloned.1.call-update) | async-done | bytes 100663312 | tf_op jit(solution)/shard_map/psum | solution.py:115
  3772.9 24.4 fusion.10
  3797.4 65.3 %convert_reduce_fusion = (f32[3072]{0:T(1024)S(1)}, bf16[32,128,3072]{2,1,0:T(8,128)(2,1)}, bf16[32,128,3072]{2,1,0:T(8,128)(2,1)}) fusion(bf16[32,128,3072]{2,1,0:T(8,128)(2,1)} %param.26, f32[32,128]{1,0:T(8,128)S(1)} %multiply_multiply_fusion.2, bf16[32,128,3072]{2,1,0:T(8,128)(2,1)} %param.25, f32[32,128]{1,0:T(8,128)S(1)} %copy-done.16, ...), kind=kLoop, calls=%fused_computation.30 | loop fusion | flops 163574784 | bytes 201396224 | tf_op jit(solution)/shard_map/reduce_sum | solution.py:120
  3862.8 14.3 all-reduce.4
  3877.0 385.7 %all-reduce.10.cloned.1.call-done = (f32[3072,768]{1,0:T(8,128)}, f32[3072,768]{1,0:T(8,128)}, f32[6,128,128]{2,1,0:T(8,128)}, f32[6,128,128]{2,1,0:T(8,128)}, f32[768,3072]{1,0:T(8,128)}) async-done(((f32[3072,768]{1,0:T(8,128)}, f32[3072,768]{1,0:T(8,128)}, f32[6,128,128]{2,1,0:T(8,128)}, f32[6,128,128]{2,1,0:T(8,128)}, f32[768,3072]{1,0:T(8,128)}), (f32[3072,768]{1,0:T(8,128)}, f32[3072,768]{1,0:T(8,128)}, ...) | async-done | bytes 29098000 | tf_op jit(solution)/shard_map/psum | solution.py:144
  4262.8 9.3 copy.279
  4272.0 4.8 copy.280
  4281.2 3.7 copy.283
  (1241 shorter events, 1465.2 us)
Async XLA Ops:
  7.2 142.5 %copy-start = (bf16[6,128,128]{2,1,0:T(8,128)(2,1)S(1)}, bf16[6,128,128]{2,1,0:T(8,128)(2,1)}, u32[]{:S(2)}) copy-start(bf16[6,128,128]{2,1,0:T(8,128)(2,1)} %param.37) | copy-start | bytes 589828
  7.2 3765.7 %all-reduce.12.cloned.1.call-start = ((), (), s32[]{:S(2)}) async-start(), calls=%async_computation.1 | async-start | bytes 201326592 | tf_op jit(solution)/shard_map/psum | solution.py:115
  8.7 43.4 %copy-start.19 = (f32[3072]{0:T(1024)}, f32[3072]{0:T(1024)S(1)}, u32[]{:S(2)}) copy-start(f32[3072]{0:T(1024)S(1)} %convert_add_fusion.2) | copy-start | bytes 36868
  8.7 11.2 copy-start.58
  19.8 32.3 copy-start.15
  19.8 31.0 copy-start.54
  19.9 31.0 copy-start.55
  19.9 31.0 copy-start.56
  19.9 31.6 copy-start.57
  19.9 31.6 copy-start.49
  19.9 32.2 copy-start.52
  48.0 63.7 %collective-permute-start = (f32[3,32,768]{2,0,1:T(4,128)S(1)}, f32[3,32,768]{2,0,1:T(4,128)S(1)}, u32[]{:S(2)}, u32[]{:S(2)}) collective-permute-start(f32[3,32,768]{2,0,1:T(4,128)S(1)} %slice.96), channel_id=1, source_target_pairs={{0,1},{1,2},{2,3},{4,5},{5,6},{6,7},{8,9},{9,10},{10,11},{12,13},{... | collective-permute-start | bytes 884744 | tf_op jit(solution)/shard_map/ppermute | solution.py:99
  78.5 33.1 copy-start.51
  111.7 38.0 copy-start.31
  111.7 38.0 copy-start.33
  111.7 38.0 copy-start.35
  111.7 38.0 copy-start.37
  111.7 37.9 copy-start.22
  111.7 37.9 copy-start.24
  111.8 37.9 copy-start.26
  111.8 37.9 copy-start.28
  111.8 37.9 copy-start.12
  170.2 12.6 copy-start.14
  244.1 12.0 copy-start.7
  244.1 12.0 copy-start.8
  250.1 1110.5 %copy-start.4 = (f32[32,768]{1,0:T(8,128)S(1)}, f32[32,768]{1,0:T(8,128)}, u32[]{:S(2)}) copy-start(f32[32,768]{1,0:T(8,128)} %custom-call.5) | copy-start | bytes 294916
  250.1 1110.9 %copy-start.21 = (f32[768]{0:T(1024)S(1)}, f32[768]{0:T(1024)}, u32[]{:S(2)}) copy-start(f32[768]{0:T(1024)} %convert_element_type.89) | copy-start | bytes 9220
  1361.0 34.8 copy-start.9
  1361.0 34.8 copy-start.10
  1361.0 410.4 %copy-start.11 = (f32[32,768]{1,0:T(8,128)S(1)}, f32[32,768]{1,0:T(8,128)}, u32[]{:S(2)}) copy-start(f32[32,768]{1,0:T(8,128)} %custom-call.2) | copy-start | bytes 294916
  1771.5 53.8 %slice-start.3 = ((s8[6291456]{0:T(1024)(128)(4,1)}), s8[2097152]{0:T(1024)(128)(4,1)S(1)}, s32[]{:S(2)}) async-start(s8[6291456]{0:T(1024)(128)(4,1)} %bitcast.197), calls=%async_computation.5 | async-start | bytes 4194304
  1789.2 36.1 slice-start.4
  1814.4 10.9 copy-start.30
  1814.4 39.2 slice-start
  1825.3 28.3 slice-start.1
  1825.3 28.3 slice-start.2
  1906.8 42.1 slice-start.8
  1919.5 29.4 slice-start.9
  1948.9 27.9 copy-start.13
  1948.9 27.9 copy-start.23
  1948.9 27.9 copy-start.25
  1948.9 27.8 copy-start.27
  1949.0 27.8 copy-start.29
  1976.8 41.3 copy-start.32
  1976.8 41.3 copy-start.34
  1976.8 41.3 copy-start.36
  1976.8 41.3 copy-start.38
  2039.4 28.9 collective-permute-start.1
  2113.2 2149.5 %all-reduce.10.cloned.1.call-start = ((), (), s32[]{:S(2)}) async-start(), calls=%async_computation | async-start | bytes 58195968 | tf_op jit(solution)/shard_map/psum | solution.py:144
  2113.4 14.6 slice-start.14
  2120.7 32.6 slice-start.10
  2128.0 25.4 slice-start.11
  2128.0 25.4 copy-start.16
  2128.0 25.4 copy-start.20
  2128.1 51.6 %slice-start.12 = ((s8[6291456]{0:T(1024)(128)(4,1)}), s8[4194304]{0:T(1024)(128)(4,1)S(1)}, s32[]{:S(2)}) async-start(s8[6291456]{0:T(1024)(128)(4,1)} %bitcast.212), calls=%async_computation.14 | async-start | bytes 8388608
  2153.4 26.3 slice-start.13
  3772.9 24.4 copy-start.18
  3797.4 65.4 %copy-start.45 = (f32[768]{0:T(1024)S(1)}, f32[768]{0:T(1024)}, u32[]{:S(2)}) copy-start(f32[768]{0:T(1024)} %get-tuple-element.509) | copy-start | bytes 9220
  3797.4 65.4 %copy-start.46 = (f32[768]{0:T(1024)S(1)}, f32[768]{0:T(1024)}, u32[]{:S(2)}) copy-start(f32[768]{0:T(1024)} %get-tuple-element.514) | copy-start | bytes 9220
  3797.4 65.4 %copy-start.47 = (f32[768]{0:T(1024)S(1)}, f32[768]{0:T(1024)}, u32[]{:S(2)}) copy-start(f32[768]{0:T(1024)} %get-tuple-element.438) | copy-start | bytes 9220
  3797.4 65.4 %copy-start.48 = (f32[768]{0:T(1024)S(1)}, f32[768]{0:T(1024)}, u32[]{:S(2)}) copy-start(f32[768]{0:T(1024)} %get-tuple-element.440) | copy-start | bytes 9220
  4262.8 18.5 slice-start.5
  4262.8 18.5 slice-start.6
  4272.0 13.0 copy-start.1
  (15 other events, 52.2 us)
Sparse Core Ops, SparseCore 0:
  2113.3 1659.5 all-reduce.11
  3777.0 485.6 all-reduce.9
where the time goes:
time: 4330 us; the launch traced here: 4290 us
  waiting for transfers between devices  1940 us (45%)
  local copies, waits for them, and re-layouts  1300 us (30%)
  other arithmetic  681 us (16%)
  matrix products  307 us (7%)
    psum x1, waiting for transfers between devices, shard_body(): out_proj = lax.psum(out_part, 'tp') + b_out  1560 us
    dynamic_update_slice x512, local copies, waits for them, and re-layouts, local_scan(): lax.scan(scan_step, (zeros_h, jnp.ones_like(zeros_h)), (decays, drives))  815 us
    psum x1, waiting for transfers between devices, shard_body(): lax.psum((g_scale, g_w_x, jnp.sum(d_branch, axis=(0, 1)), g_w_y, jnp.sum(...  386 us
    dynamic_slice x256, local copies, waits for them, and re-layouts, local_scan(): lax.scan(scan_step, (zeros_h, jnp.ones_like(zeros_h)), (decays, drives))  308 us
    dynamic_update_slice x128, other arithmetic, local_scan(): lax.scan(scan_step, (zeros_h, jnp.ones_like(zeros_h)), (decays, drives))  210 us
    mul x128, other arithmetic, scan_step(): return ((inputs_t[0] * grad_h, inputs_t[0] * prod_a), (grad_h, prod_a))  123 us
  transfers between devices with their start and end apart: 4, of which 2 were waited for; matrix products, arithmetic and copies ran while one was open for 6% of the time, Pallas kernels for 0%

commit v1 on v0

v1 whole, which is shorter than its diff:
```python
import functools
import jax
import jax.numpy as jnp
from jax import lax
from jax.experimental import pallas as pl
from jax.experimental.pallas import tpu as pltpu
from jax.sharding import PartitionSpec as P

NORM_EPS = 1e-6
CONV_WIDTH = 4
HALO = CONV_WIDTH - 1
LANES = 128
CB = 256
TC = 16
TINY = 1.2e-38
GELU_A = 0.7978845608028654
GELU_B = 0.044715
VMEM_BYTES = 64 * 1024 * 1024 - 64 * 1024
F32 = jnp.float32
BF16 = jnp.bfloat16
IN_SPECS = (P(None, "cp", None), P(None, "cp", None), P(None, "cp"), P(), P(None, "tp"), P("tp"), P(None, "tp"), P("tp"), P(None, "tp"), P("tp"), P("tp", None, None), P("tp"), P("tp", None, None), P("tp"), P("tp"), P("tp", None), P())
OUT_SPECS = (P(None, "cp", None), P(None, "cp", None), P(), P(None, "tp"), P("tp"), P(None, "tp"), P("tp"), P(None, "tp"), P("tp"), P("tp", None, None), P("tp"), P("tp", None, None), P("tp"), P("tp"), P("tp", None), P())
R_BX, R_BY, R_CB, R_BA, R_BI, R_K, R_CW = 0, 1, 2, 3, 4, 5, 6
PAR_ROWS = 16


def dot_nn(lhs, rhs):
    return jnp.dot(lhs, rhs, preferred_element_type=F32)


def dot_nt(lhs, rhs):
    return lax.dot_general(lhs, rhs, (((1,), (1,)), ((), ())), preferred_element_type=F32)


def dot_tn(lhs, rhs):
    return lax.dot_general(lhs, rhs, (((0,), (0,)), ((), ())), preferred_element_type=F32)


def round16(val):
    return val.astype(BF16).astype(F32)


def sigmoid(val):
    return 1.0 / (1.0 + jnp.exp(-val))


def gates(pre_a, pre_i, slope, keep):
    gate_r = sigmoid(pre_a)
    gate_i = sigmoid(pre_i)
    log_a = gate_r * slope
    raw_a = jnp.exp(log_a)
    gap = jnp.tanh(-log_a) * (1.0 + raw_a * raw_a)
    inv_m = lax.rsqrt(jnp.maximum(gap, TINY))
    decay = jnp.where(keep, raw_a, 0.0)
    mult = jnp.where(keep, gap * inv_m, 1.0)
    return gate_r, gate_i, decay, mult, inv_m


def first_pass_kernel(ids_ref, n_ref, gz_ref, nh_ref, pos_ref, wx_ref, wy_ref, wo_ref, wg_ref, par_ref, *rest, n_blk, n_chunk, own, batch):
    if own:
        c_out, y_out, g_out, q_out, info_out, xb_out, xh, xs, ys, ds, pre, tail, state = rest
        wx_b, wy_b, wo_b = wx_ref, wy_ref, wo_ref
    else:
        c_out, y_out, g_out, q_out, info_out, wx_b, wy_b, wo_b, xs, ys, ds, pre, xh, tail, state = rest
        xb_out = None
    step = pl.program_id(0)
    n_steps = n_blk * n_chunk

    @pl.when((lax.rem(step, n_chunk) == 0) & (step < n_steps))
    def _():
        if not own:
            wx_b[...] = wx_ref[0].astype(BF16)
            wy_b[...] = wy_ref[0].astype(BF16)
            wo_b[...] = wo_ref[0].astype(BF16)
        xh[...] = dot_nn(nh_ref[...].astype(BF16), wx_b[...])

    def dots():
        rows = n_ref[...]
        xs[...] = dot_nn(rows, wx_b[...])
        ys[...] = dot_nn(rows, wy_b[...])
        ds[...] = dot_nt(gz_ref[...], wo_b[...])

    def elementwise():
        first = lax.rem(step + n_chunk - 1, n_chunk) == 0
        for half in range(CB // LANES):
            lane = slice(half * LANES, (half + 1) * LANES)
            row = lambda idx: par_ref[0, idx:idx + 1, lane]
            bias_x, conv_b = row(R_BX), row(R_CB)
            taps = [row(R_CW + k) for k in range(CONV_WIDTH)]
            past = []
            for j in range(HALO):
                sl = slice(j * batch, (j + 1) * batch)
                past.append(jnp.where(first, round16(xh[sl, lane] + bias_x), tail[sl, lane]))
            for t in range(TC):
                sl = slice(t * batch, (t + 1) * batch)
                cur = round16(xs[sl, lane] + bias_x)
                if own:
                    xb_out[0, t, :, lane] = cur.astype(BF16)
                pos = pos_ref[t]
                total = conv_b + cur * taps[0]
                for k in range(1, CONV_WIDTH):
                    total = total + jnp.where(pos >= k, past[HALO - k], 0.0) * taps[k]
                c_out[0, t, :, lane] = total.astype(BF16)
                past = past[1:] + [cur]
            for j in range(HALO):
                tail[j * batch:(j + 1) * batch, lane] = past[j]
            wg = wg_ref[0, half].astype(BF16)
            pre[half] = dot_nn(c_out[0, :, :, lane].reshape(TC * batch, LANES), wg)
            bias_y, bias_a, bias_i, slope = row(R_BY), row(R_BA), row(R_BI), row(R_K)
            hid = jnp.where(first, 0.0, state[0, :, lane])
            prod = jnp.where(first, 1.0, state[1, :, lane])
            head = jnp.where(first, 0.0, state[2, :, lane])
            for t in range(TC):
                sl = slice(t * batch, (t + 1) * batch)
                keep = pos_ref[t] >= 1
                conv = c_out[0, t, :, lane].astype(F32)
                _, gate_i, decay, mult, _ = gates(pre[half, sl, :LANES] + bias_a, pre[half, sl, LANES:] + bias_i, slope, keep)
                hid = decay * hid + mult * gate_i * conv
                prod = prod * decay
                pre_y = ys[sl, lane] + bias_y
                sq = pre_y * pre_y
                tan = jnp.tanh(pre_y * (GELU_A + GELU_A * GELU_B * sq))
                half_y = 0.5 * pre_y
                d_mixed = ds[sl, lane]
                y_act = half_y + half_y * tan
                slope_y = 0.5 + 0.5 * tan + half_y * (1.0 - tan * tan) * (GELU_A + 3.0 * GELU_A * GELU_B * sq)
                grad_h = d_mixed * y_act
                head = head + prod * grad_h
                y_out[0, t, :, lane] = y_act
                g_out[0, t, :, lane] = grad_h
                q_out[0, t, :, lane] = d_mixed * slope_y
            for idx, val in enumerate((hid, prod, head)):
                state[idx, :, lane] = val
                info_out[idx, :, lane] = val

    @pl.when(step == 0)
    def _():
        dots()

    @pl.when((step > 0) & (step < n_steps))
    def _():
        elementwise()
        dots()

    @pl.when(step == n_steps)
    def _():
        elementwise()


def first_pass(ids, normed, gz, n_halo, pos_b, wx, wy, wo, wg, par, own):
    n_blk = ids.shape[0]
    n_rows, width = normed.shape
    n_tok, batch = pos_b.shape[0], pos_b.shape[1]
    n_chunk = n_tok // TC
    n_steps = n_blk * n_chunk
    cols = n_blk * CB
    cur = lambda s: jnp.minimum(s, n_steps - 1)
    old = lambda s: jnp.maximum(s - 1, 0)
    row_spec = pl.BlockSpec((TC * batch, width), lambda s, ids: (lax.rem(cur(s), n_chunk), 0))
    if own:
        w_specs = [pl.BlockSpec((width, CB), lambda s, ids: (0, cur(s) // n_chunk))] * 2 + [pl.BlockSpec((CB, width), lambda s, ids: (cur(s) // n_chunk, 0))]
    else:
        w_specs = [pl.BlockSpec((1, width, CB), lambda s, ids: (ids[cur(s) // n_chunk], 0, 0))] * 2 + [pl.BlockSpec((1, CB, width), lambda s, ids: (ids[cur(s) // n_chunk], 0, 0))]
    in_specs = [row_spec, row_spec, pl.BlockSpec((HALO * batch, width), lambda s, ids: (0, 0)),
                pl.BlockSpec((TC, batch, LANES), lambda s, ids: (lax.rem(old(s), n_chunk), 0, 0)), *w_specs,
                pl.BlockSpec((1, CB // LANES, LANES, 2 * LANES), lambda s, ids: (ids[old(s) // n_chunk], 0, 0, 0)),
                pl.BlockSpec((1, PAR_ROWS, CB), lambda s, ids: (ids[old(s) // n_chunk], 0, 0))]
    tok_spec = pl.BlockSpec((1, TC, batch, CB), lambda s, ids: (old(s) // n_chunk, lax.rem(old(s), n_chunk), 0, 0))
    tok_shape = lambda dt: jax.ShapeDtypeStruct((n_blk, n_tok, batch, CB), dt)
    out_specs = [tok_spec] * 4 + [pl.BlockSpec((3, batch, CB), lambda s, ids: (0, 0, old(s) // n_chunk))]
    out_shape = [tok_shape(BF16), tok_shape(F32), tok_shape(F32), tok_shape(F32), jax.ShapeDtypeStruct((3, batch, cols), F32)]
    if own:
        out_specs += [tok_spec, pl.BlockSpec((HALO * batch, CB), lambda s, ids: (0, cur(s) // n_chunk))]
        out_shape += [tok_shape(BF16), jax.ShapeDtypeStruct((HALO * batch, cols), F32)]
    else:
        out_specs += [pl.BlockSpec((width, CB), lambda s, ids: (0, cur(s) // n_chunk))] * 2 + [pl.BlockSpec((CB, width), lambda s, ids: (cur(s) // n_chunk, 0))]
        out_shape += [jax.ShapeDtypeStruct((width, cols), BF16)] * 2 + [jax.ShapeDtypeStruct((cols, width), BF16)]
    rows = TC * batch
    scratch = [pltpu.VMEM((rows, CB), F32)] * 3 + [pltpu.VMEM((CB // LANES, rows, 2 * LANES), F32)] + [pltpu.VMEM((HALO * batch, CB), F32)] * (1 if own else 2) + [pltpu.VMEM((3, batch, CB), F32)]
    flops = 6 * n_rows * width * cols
    return pl.pallas_call(
        functools.partial(first_pass_kernel, n_blk=n_blk, n_chunk=n_chunk, own=own, batch=batch),
        grid_spec=pltpu.PrefetchScalarGridSpec(num_scalar_prefetch=1, grid=(n_steps + 1,), in_specs=in_specs, out_specs=out_specs, scratch_shapes=scratch),
        out_shape=out_shape,
        compiler_params=pltpu.CompilerParams(dimension_semantics=("arbitrary",), vmem_limit_bytes=VMEM_BYTES),
        cost_estimate=pl.CostEstimate(flops=flops, bytes_accessed=n_blk * n_rows * width * 4, transcendentals=0),
        name="first_pass_own" if own else "first_pass_far",
    )(ids, normed, gz, n_halo, pos_b, wx, wy, wo, wg, par)


N_ACC = 11


def second_pass_kernel(ids_ref, c_ref, y_ref, g_ref, q_ref, pos_ref, enter_ref, wg_ref, par_ref, *rest, n_chunk, own, batch):
    if own:
        xb_ref, xh_ref, mix_out, dpy_out, dbr_out, head_out, tail_out, acc_out, gw_out, s_a, s_A, s_i, s_m, pre, dpai, dgate, s_e = rest
    else:
        mix_out, dpy_out, dbr_out, head_out, tail_out, s_a, s_A, s_i, s_m, pre, dpai, dgate = rest
    row = lambda idx: par_ref[0, idx:idx + 1, :]
    wg = wg_ref[0, 0].astype(BF16)
    bias_a, bias_i, slope = row(R_BA), row(R_BI), row(R_K)
    taps = [row(R_CW + k) for k in range(CONV_WIDTH)]
    fold = lambda val: jnp.sum(val.reshape(batch // 8, 8, LANES), axis=0)
    if own:
        halo = [round16(xh_ref[k] + row(R_BX)) for k in range(HALO)]
        acc_out[...] = jnp.zeros_like(acc_out)
        gw_out[...] = jnp.zeros_like(gw_out)

    def forward(j, hid):
        base = j * TC
        pre[...] = dot_nn(c_ref[0, pl.ds(base, TC)].reshape(TC * batch, LANES), wg)
        acc_y = jnp.zeros((8, LANES), F32)
        for t in range(TC):
            sl = slice(t * batch, (t + 1) * batch)
            tok = base + t
            keep = pos_ref[tok] >= 1
            conv = c_ref[0, tok].astype(F32)
            gate_r, gate_i, decay, mult, inv_m = gates(pre[sl, :LANES] + bias_a, pre[sl, LANES:] + bias_i, slope, keep)
            in_conv = gate_i * conv
            before = hid
            hid = decay * before + mult * in_conv
            d_log = decay * (before - in_conv * decay * inv_m)
            r_log = d_log * gate_r
            s_a[tok] = decay
            s_A[tok] = r_log * (1.0 - gate_r) * slope
            s_i[tok] = mult * in_conv * (1.0 - gate_i)
            s_m[tok] = mult * gate_i
            mix_out[tok] = (hid * y_ref[0, tok]).astype(BF16)
            d_pre_y = hid * q_ref[0, tok]
            dpy_out[tok] = d_pre_y.astype(BF16)
            if own:
                s_e[tok] = r_log
                acc_y = acc_y + fold(d_pre_y)
        if own:
            acc_out[0, 8:16] = acc_out[0, 8:16] + acc_y
        return hid

    lax.fori_loop(0, n_chunk, forward, enter_ref[0])

    def recur(j, carry):
        base = j * TC
        acc_a = acc_i = acc_p = jnp.zeros((8, LANES), F32)
        for t in range(TC - 1, -1, -1):
            sl = slice(t * batch, (t + 1) * batch)
            tok = base + t
            grad_h = g_ref[0, tok] + carry
            carry = s_a[tok] * grad_h
            d_pre_a = grad_h * s_A[tok]
            d_pre_i = grad_h * s_i[tok]
            s_m[tok] = grad_h * s_m[tok]
            dpai[sl, :LANES] = d_pre_a.astype(BF16)
            dpai[sl, LANES:] = d_pre_i.astype(BF16)
            if own:
                acc_a = acc_a + fold(d_pre_a)
                acc_i = acc_i + fold(d_pre_i)
                acc_p = acc_p + fold(grad_h * s_e[tok])
        dgate[...] = dot_nt(dpai[...], wg)
        if own:
            acc_out[0, 16:24] = acc_out[0, 16:24] + acc_a
            acc_out[0, 24:32] = acc_out[0, 24:32] + acc_i
            acc_out[0, 32:40] = acc_out[0, 32:40] + acc_p
            gw_out[0] = gw_out[0] + dot_tn(c_ref[0, pl.ds(base, TC)].reshape(TC * batch, LANES), dpai[...])
        return carry

    def conv_back(j, later):
        base = j * TC
        later = list(later)
        acc_x = acc_b = jnp.zeros((8, LANES), F32)
        acc_w = [jnp.zeros((8, LANES), F32) for _ in range(CONV_WIDTH)]
        for t in range(TC - 1, -1, -1):
            sl = slice(t * batch, (t + 1) * batch)
            tok = base + t
            d_conv = s_m[tok] + dgate[sl]
            total = d_conv * taps[0] + later[0]
            pos = pos_ref[tok]
            masked = [jnp.where(pos >= k, d_conv, 0.0) for k in range(1, CONV_WIDTH)]
            later = [later[1] + masked[0] * taps[1], later[2] + masked[1] * taps[2], masked[2] * taps[3]]
            dbr_out[tok] = total.astype(BF16)
            if t >= TC - HALO:
                tail_out[t - (TC - HALO)] = jnp.where(j == n_chunk - 1, total, tail_out[t - (TC - HALO)])
            if own:
                acc_x = acc_x + fold(total)
                acc_b = acc_b + fold(d_conv)
                acc_w[0] = acc_w[0] + fold(d_conv * xb_ref[0, tok].astype(F32))
                for k in range(1, CONV_WIDTH):
                    past = xb_ref[0, jnp.maximum(tok - k, 0)].astype(F32)
                    if t < k:
                        past = jnp.where(j == 0, halo[HALO + t - k], past)
                    acc_w[k] = acc_w[k] + fold(masked[k - 1] * past)
        if own:
            acc_out[0, 0:8] = acc_out[0, 0:8] + acc_x
            acc_out[0, 40:48] = acc_out[0, 40:48] + acc_b
            for k in range(CONV_WIDTH):
                acc_out[0, 48 + 8 * k:56 + 8 * k] = acc_out[0, 48 + 8 * k:56 + 8 * k] + acc_w[k]
        return tuple(later)

    tail_out[...] = jnp.zeros_like(tail_out)
    zero = jnp.zeros((batch, LANES), F32)
    carry = recur(n_chunk - 1, enter_ref[1])

    def back(idx, vals):
        carry, later = vals[0], vals[1:]
        j = n_chunk - 2 - idx
        later = conv_back(j + 1, later)
        carry = recur(j, carry)
        return (carry, *later)

    vals = lax.fori_loop(0, n_chunk - 1, back, (carry, zero, zero, zero))
    later = conv_back(0, vals[1:])
    for k in range(HALO):
        head_out[HALO - 1 - k] = later[k]


def second_pass(ids, conv, y_act, grad_h, q_val, pos_b, enter, wg, par, xb=None, xb_halo=None):
    own = xb is not None
    n_blk, n_tok, batch, _ = conv.shape
    n_chunk = n_tok // TC
    per = CB // LANES
    cols = n_blk * CB
    tok_spec = pl.BlockSpec((1, n_tok, batch, LANES), lambda s, ids: (s // per, 0, 0, lax.rem(s, per)))
    lane_spec = lambda n: pl.BlockSpec((n, batch, LANES), lambda s, ids: (0, 0, s))
    in_specs = [tok_spec] * 4 + [pl.BlockSpec((n_tok, batch, LANES), lambda s, ids: (0, 0, 0)), lane_spec(2),
                pl.BlockSpec((1, 1, LANES, 2 * LANES), lambda s, ids: (ids[s // per], lax.rem(s, per), 0, 0)),
                pl.BlockSpec((1, PAR_ROWS, LANES), lambda s, ids: (ids[s // per], 0, lax.rem(s, per)))]
    out_specs = [lane_spec(n_tok)] * 3 + [lane_spec(HALO)] * 2
    out_shape = [jax.ShapeDtypeStruct((n_tok, batch, cols), BF16)] * 3 + [jax.ShapeDtypeStruct((HALO, batch, cols), F32)] * 2
    scratch = [pltpu.VMEM((n_tok, batch, LANES), F32)] * 4 + [pltpu.VMEM((TC * batch, 2 * LANES), F32), pltpu.VMEM((TC * batch, 2 * LANES), BF16), pltpu.VMEM((TC * batch, LANES), F32)]
    args = [ids, conv, y_act, grad_h, q_val, pos_b, enter, wg, par]
    if own:
        in_specs += [tok_spec, lane_spec(HALO)]
        out_specs += [pl.BlockSpec((1, 8 * N_ACC - 8, LANES), lambda s, ids: (s, 0, 0)), pl.BlockSpec((1, LANES, 2 * LANES), lambda s, ids: (s, 0, 0))]
        out_shape += [jax.ShapeDtypeStruct((n_blk * per, 8 * N_ACC - 8, LANES), F32), jax.ShapeDtypeStruct((n_blk * per, LANES, 2 * LANES), F32)]
        scratch.append(pltpu.VMEM((n_tok, batch, LANES), F32))
        args += [xb, xb_halo]
    n_elem = n_tok * batch * cols
    return pl.pallas_call(
        functools.partial(second_pass_kernel, n_chunk=n_chunk, own=own, batch=batch),
        grid_spec=pltpu.PrefetchScalarGridSpec(num_scalar_prefetch=1, grid=(n_blk * per,), in_specs=in_specs, out_specs=out_specs, scratch_shapes=scratch),
        out_shape=out_shape,
        compiler_params=pltpu.CompilerParams(dimension_semantics=("arbitrary",), vmem_limit_bytes=VMEM_BYTES),
        cost_estimate=pl.CostEstimate(flops=n_elem * 12000, bytes_accessed=n_elem * 20, transcendentals=n_elem * 6),
        name="second_pass_own" if own else "second_pass_far",
    )(*args)


def out_kernel(mo_ref, mf_ref, wo_ref, wf_ref, x_ref, b_ref, z_ref):
    n_t, n_b, _ = mo_ref.shape
    proj = dot_nn(mo_ref[...].reshape(n_t * n_b, -1), wo_ref[...]) + dot_nn(mf_ref[...].reshape(n_t * n_b, -1), wf_ref[...])
    proj = jnp.swapaxes(proj.reshape(n_t, n_b, -1), 0, 1)
    z_ref[...] = (x_ref[...].astype(F32) + (proj + b_ref[...].reshape(1, 1, -1))).astype(BF16)


def out_pass(mix_own, mix_far, w_own, w_far, x_in, b_out):
    n_tok, batch, c_own = mix_own.shape
    c_far = mix_far.shape[2]
    width = x_in.shape[2]
    b_blk = 16
    act = lambda c: pl.BlockSpec((TC, b_blk, c), lambda i, j: (i, j, 0))
    full = lambda shape: pl.BlockSpec(shape, lambda i, j: (0,) * len(shape), pipeline_mode=pl.Buffered(1))
    native = pl.BlockSpec((b_blk, TC, width), lambda i, j: (j, i, 0))
    return pl.pallas_call(
        out_kernel, grid=(n_tok // TC, batch // b_blk),
        in_specs=[act(c_own), act(c_far), full(w_own.shape), full(w_far.shape), native, full((1, width))],
        out_specs=native, out_shape=jax.ShapeDtypeStruct(x_in.shape, BF16),
        compiler_params=pltpu.CompilerParams(dimension_semantics=("arbitrary", "arbitrary"), vmem_limit_bytes=VMEM_BYTES),
        cost_estimate=pl.CostEstimate(flops=2 * n_tok * batch * (c_own + c_far) * width, bytes_accessed=n_tok * batch * width * 8, transcendentals=0),
        name="out_pass",
    )(mix_own, mix_far, w_own, w_far, x_in, b_out)


def norm_back_kernel(do_ref, df_ref, po_ref, pf_ref, xo_ref, xf_ref, yo_ref, yf_ref, x_ref, gz_ref, s_ref, gx_ref, gs_ref):
    n_t, n_b, _ = do_ref.shape
    flat = lambda ref: ref[...].reshape(n_t * n_b, -1)
    d_n = dot_nt(flat(do_ref), xo_ref[...]) + dot_nt(flat(df_ref), xf_ref[...]) + dot_nt(flat(po_ref), yo_ref[...]) + dot_nt(flat(pf_ref), yf_ref[...])
    d_n = jnp.swapaxes(d_n.reshape(n_t, n_b, -1), 0, 1)
    x_f = x_ref[...].astype(F32)
    inv = lax.rsqrt(jnp.mean(x_f * x_f, axis=-1, keepdims=True) + NORM_EPS)
    x_hat = x_f * inv
    gain = 1.0 + s_ref[...].reshape(1, 1, -1)
    scaled = d_n * gain
    proj = jnp.mean(scaled * x_hat, axis=-1, keepdims=True)
    gx_ref[...] = (gz_ref[...].astype(F32) + inv * (scaled - x_hat * proj)).astype(BF16)
    part = jnp.sum((d_n * x_hat).reshape(n_t * n_b // 8, 8, -1), axis=0)

    @pl.when((pl.program_id(0) == 0) & (pl.program_id(1) == 0))
    def _():
        gs_ref[...] = jnp.zeros_like(gs_ref)
    gs_ref[...] += part


def norm_back_pass(dbr_own, dbr_far, dpy_own, dpy_far, wx_own, wx_far, wy_own, wy_far, x_in, grad_z, scale):
    n_tok, batch, c_own = dbr_own.shape
    c_far = dbr_far.shape[2]
    width = x_in.shape[2]
    b_blk = 16
    act = lambda c: pl.BlockSpec((TC, b_blk, c), lambda i, j: (i, j, 0))
    full = lambda shape: pl.BlockSpec(shape, lambda i, j: (0,) * len(shape), pipeline_mode=pl.Buffered(1))
    native = pl.BlockSpec((b_blk, TC, width), lambda i, j: (j, i, 0))
    return pl.pallas_call(
        norm_back_kernel, grid=(n_tok // TC, batch // b_blk),
        in_specs=[act(c_own), act(c_far), act(c_own), act(c_far), full(wx_own.shape), full(wx_far.shape), full(wy_own.shape), full(wy_far.shape), native, native, full((1, width))],
        out_specs=[native, full((8, width))],
        out_shape=[jax.ShapeDtypeStruct(x_in.shape, BF16), jax.ShapeDtypeStruct((8, width), F32)],
        compiler_params=pltpu.CompilerParams(dimension_semantics=("arbitrary", "arbitrary"), vmem_limit_bytes=VMEM_BYTES),
        cost_estimate=pl.CostEstimate(flops=4 * n_tok * batch * (c_own + c_far) * width, bytes_accessed=n_tok * batch * width * 10, transcendentals=0),
        name="norm_back_pass",
    )(dbr_own, dbr_far, dpy_own, dpy_far, wx_own, wx_far, wy_own, wy_far, x_in, grad_z, scale)


def entering(info, cp_index, swap_core, swap_x):
    end, prod, head = info[0], info[1], info[2]
    other = lax.ppermute(info, "cp", swap_core)
    o_end, o_prod, o_head = other[0], other[1], other[2]
    upper_core = cp_index % 2 == 1
    upper_chip = cp_index >= 2
    chip_end = jnp.where(upper_core, prod * o_end + end, o_prod * end + o_end)
    chip_head = jnp.where(upper_core, o_head + o_prod * head, head + prod * o_head)
    got = lax.ppermute(jnp.where(upper_chip, chip_head, chip_end), "cp", swap_x)
    from_low = jnp.where(upper_chip, got, 0.0)
    from_high = jnp.where(upper_chip, 0.0, got)
    state_in = jnp.where(upper_core, o_prod * from_low + o_end, from_low)
    grad_in = jnp.where(upper_core, from_high, o_head + o_prod * from_high)
    return jnp.stack([state_in, grad_in])


def shard_body(x_in, grad_z, seg_pos, norm_scale, w_x, b_x, w_y, b_y, conv_w, conv_b, w_a, b_a, w_i, b_i, a_param, w_out, b_out, fwd_perm, back_perm, cp_size, tp_size):
    cp_index = lax.axis_index("cp")
    tp_index = lax.axis_index("tp")
    batch, n_tok, width = x_in.shape
    c_own = w_x.shape[1]
    n_own = c_own // CB
    swap_core = [(j, j ^ 1) for j in range(cp_size)]
    swap_x = [(j, j ^ 2) for j in range(cp_size)]

    def spread(arr):
        n = arr.shape[0] // cp_size
        part = lax.dynamic_slice_in_dim(arr, cp_index * n, n, 0).astype(F32)
        return lax.all_gather(part, ("tp", "cp")).reshape(tp_size, *arr.shape)

    slope = -8.0 * jax.nn.softplus(a_param)
    rows = [b_x, b_y, conv_b, b_a, b_i, slope, *[conv_w[k] for k in range(CONV_WIDTH)]]
    par = jnp.stack([r.astype(F32) for r in rows] + [jnp.zeros_like(slope)] * (PAR_ROWS - len(rows)))
    par = par.reshape(PAR_ROWS, n_own, CB).transpose(1, 0, 2)
    wg = jnp.concatenate([w_a, w_i], axis=-1)
    par_all = lax.all_gather(par, "tp")
    wg_all = spread(wg.reshape(-1, 2 * LANES)).reshape(tp_size, n_own, CB // LANES, LANES, 2 * LANES)
    wg = wg.reshape(n_own, CB // LANES, LANES, 2 * LANES)
    parts = []
    for p in range(n_own):
        parts.append((spread(w_x[:, p * CB:(p + 1) * CB]), spread(w_y[:, p * CB:(p + 1) * CB]), spread(w_out[p * CB:(p + 1) * CB])))

    x_f = x_in.astype(F32)
    inv = lax.rsqrt(jnp.mean(x_f * x_f, axis=-1, keepdims=True) + NORM_EPS)
    normed = (x_f * inv * (1.0 + norm_scale.astype(F32))).astype(BF16).transpose(1, 0, 2)
    gz_t = grad_z.transpose(1, 0, 2)
    n_halo = lax.ppermute(normed[n_tok - HALO:].astype(F32), "cp", fwd_perm).reshape(HALO * batch, width)
    normed = normed.reshape(n_tok * batch, width)
    gz_t = gz_t.reshape(n_tok * batch, width)
    pos_b = jnp.broadcast_to(seg_pos.T[:, :, None], (n_tok, batch, LANES))

    own_ids = jnp.arange(n_own, dtype=jnp.int32)
    c_o, y_o, g_o, q_o, info_o, xb_o, xh_o = first_pass(own_ids, normed, gz_t, n_halo, pos_b, w_x, w_y, w_out, wg, par, True)
    enter_o = entering(info_o, cp_index, swap_core, swap_x)
    mix_o, dpy_o, dbr_o, head_o, tail_o, acc, g_gate = second_pass(own_ids, c_o, y_o, g_o, q_o, pos_b, enter_o, wg, par, xb_o, xh_o.reshape(HALO, batch, c_own))
    back_o = lax.ppermute(head_o, "cp", back_perm)
    dbr_o = dbr_o.at[n_tok - HALO:].set((tail_o + back_o).astype(BF16))

    far = jnp.stack([tp_index ^ k for k in range(1, tp_size)]).astype(jnp.int32)
    mixes, dpys, dbrs, wxs, wys, wos = [], [], [], [], [], []
    for p, (wx_p, wy_p, wo_p) in enumerate(parts):
        wg_p, par_p = wg_all[:, p], par_all[:, p]
        c_f, y_f, g_f, q_f, info_f, wx16, wy16, wo16 = first_pass(far, normed, gz_t, n_halo, pos_b, wx_p, wy_p, wo_p, wg_p, par_p, False)
        enter_f = entering(info_f, cp_index, swap_core, swap_x)
        mix_f, dpy_f, dbr_f, head_f, tail_f = second_pass(far, c_f, y_f, g_f, q_f, pos_b, enter_f, wg_p, par_p)
        back_f = lax.ppermute(head_f, "cp", back_perm)
        dbr_f = dbr_f.at[n_tok - HALO:].set((tail_f + back_f).astype(BF16))
        for lst, val in zip((mixes, dpys, dbrs, wxs, wys, wos), (mix_f, dpy_f, dbr_f, wx16, wy16, wo16)):
            lst.append(val)
    mix_f, dpy_f, dbr_f = [jnp.concatenate(v, axis=2) for v in (mixes, dpys, dbrs)]
    wx_f, wy_f, wo_f = jnp.concatenate(wxs, axis=1), jnp.concatenate(wys, axis=1), jnp.concatenate(wos, axis=0)
    z_out = out_pass(mix_o, mix_f, w_out, wo_f, x_in, b_out.astype(F32).reshape(1, width))
    grad_x, gs_part = norm_back_pass(dbr_o, dbr_f, dpy_o, dpy_f, w_x, wx_f, w_y, wy_f, x_in, grad_z, norm_scale.astype(F32).reshape(1, width))

    flat = lambda arr: arr.reshape(n_tok * batch, -1)
    g_w_x = dot_tn(normed, flat(dbr_o))
    g_w_y = dot_tn(normed, flat(dpy_o))
    g_w_out = dot_tn(flat(mix_o), gz_t)
    acc = acc.reshape(c_own // LANES, N_ACC - 1, 8, LANES).sum(axis=2).transpose(1, 0, 2).reshape(N_ACC - 1, c_own)
    g_b_x = acc[0] + jnp.sum(back_o, axis=(0, 1))
    g_a_param = -8.0 * jax.nn.sigmoid(a_param) * acc[4]
    g_b_out = jnp.sum(gz_t, axis=0, dtype=F32)
    g_scale = jnp.sum(gs_part, axis=0)
    sums = lax.psum((g_scale, g_w_x, g_b_x, g_w_y, acc[1], acc[6:10], acc[5], g_gate[:, :, :LANES], acc[2], g_gate[:, :, LANES:], acc[3], g_a_param, g_w_out, g_b_out), "cp")
    return (z_out, grad_x) + tuple(sums)


def solution(mesh):
    cp_size = mesh.shape["cp"]
    fwd_perm = [(j, j + 1) for j in range(cp_size - 1)]
    back_perm = [(j + 1, j) for j in range(cp_size - 1)]
    per_device = functools.partial(shard_body, fwd_perm=fwd_perm, back_perm=back_perm, cp_size=cp_size, tp_size=mesh.shape["tp"])
    return jax.shard_map(per_device, mesh=mesh, in_specs=IN_SPECS, out_specs=OUT_SPECS, check_vma=False)
```

time: 4330 us -> 1440 us (0.33)
  waiting for transfers between devices: 1940 us -> 95.8 us
  local copies, waits for them, and re-layouts: 1300 us -> 74.3 us
  Pallas kernels: 0 us -> 900 us
  other arithmetic: 681 us -> 216 us
  matrix products: 307 us -> 91.1 us
    psum x2 -> x1, waiting for transfers between devices: 1940 us -> 0.01 us  [shard_body(): lax.psum((g_scale, g_w_x, g_b_x, g_w_y, acc[1], acc[6:10], acc[5], g_gate...]
    pallas_call x0 -> x10, Pallas kernels: none -> 900 us  [the longest x4 401 us: first_pass(): pl.pallas_call(functools.partial(first_pass_kernel, n_blk=n_blk, n_chunk=...]
    dynamic_update_slice x520 -> x0, local copies, waits for them, and re-layouts: 827 us -> none  [the longest x512 815 us: local_scan(): lax.scan(scan_step, (zeros_h, jnp.ones_like(zeros_h)), (decays, drives))]
    dynamic_slice x257 -> x0, local copies, waits for them, and re-layouts: 309 us -> none  [the longest x256 308 us: local_scan(): lax.scan(scan_step, (zeros_h, jnp.ones_like(zeros_h)), (decays, drives))]
    dot_general x15 -> x3, matrix products: 307 us -> 91.1 us  [dot_tn(): lax.dot_general(lhs, rhs, (((0,), (0,)), ((), ())), preferred_element_typ...]
    dynamic_update_slice x132 -> x0, other arithmetic: 210 us -> none  [the longest x128 210 us: local_scan(): lax.scan(scan_step, (zeros_h, jnp.ones_like(zeros_h)), (decays, drives))]
    reduce_sum x10 -> x5, other arithmetic: 239 us -> 53.8 us  [the longest x1 41.6 us: shard_body(): inv = lax.rsqrt(jnp.mean(x_f * x_f, axis=-1, keepdims=True) + NORM_EPS)]
    mul x130 -> x2, other arithmetic: 140 us -> 0.62 us  [the longest x1 0.61 us: shard_body(): g_a_param = -8.0 * jax.nn.sigmoid(a_param) * acc[4]]
  transfers between devices with their start and end apart: 4 -> 24, of which waited for: 2 -> 3; matrix products, arithmetic and copies ran while one was open for 6% -> 25% of each run, Pallas kernels for 0% -> 63%
where the time goes in v1:
time: 1440 us
  Pallas kernels  900 us (62%)
  other arithmetic  216 us (15%)
  waiting for transfers between devices  95.8 us (7%)
  matrix products  91.1 us (6%)
  local copies, waits for them, and re-layouts  74.3 us (5%)
  blocking collectives  27.1 us (2%)
  between operations  16.5 us (1%)
  starting transfers between devices  15.2 us (1%)
    pallas_call x4, Pallas kernels, first_pass(): pl.pallas_call(functools.partial(first_pass_kernel, n_blk=n_blk, n_chunk=...  401 us
    pallas_call x4, Pallas kernels, second_pass(): pl.pallas_call(functools.partial(second_pass_kernel, n_chunk=n_chunk, own...  200 us
    pallas_call x1, Pallas kernels, norm_back_pass(): pl.pallas_call(norm_back_kernel, grid=(n_tok // TC, batch // b_blk), in_s...  197 us
    pallas_call x1, Pallas kernels, out_pass(): pl.pallas_call(out_kernel, grid=(n_tok // TC, batch // b_blk), in_specs=[...  101 us
    dot_general x3, matrix products, dot_tn(): lax.dot_general(lhs, rhs, (((0,), (0,)), ((), ())), preferred_element_typ...  91.1 us
    all_gather x10, waiting for transfers between devices, spread(): return lax.all_gather(part, ('tp', 'cp')).reshape(tp_size, *arr.shape)  86.6 us
    concatenate x3, other arithmetic, shard_body(): jnp.concatenate(v, axis=2)  46.5 us
    reduce_sum x1, other arithmetic, shard_body(): inv = lax.rsqrt(jnp.mean(x_f * x_f, axis=-1, keepdims=True) + NORM_EPS)  41.6 us
  transfers between devices with their start and end apart: 24, of which 3 were waited for; matrix products, arithmetic and copies ran while one was open for 25% of the time, Pallas kernels for 63%

profile of v1, /device:TPU:0, one launch (start us, length us, event | category | flops | bytes accessed | tf_op | source)
XLA Modules:
  0.0 1435.9 jit_solution(9289265962502745175)
XLA Ops:
  8.1 1.0 constant_dynamic-update-slice_fusion.1
  9.0 1.0 constant_dynamic-update-slice_fusion
  10.8 3.8 fusion.37
  14.7 1.0 dynamic-slice_convert_fusion.2
  15.7 3.8 fusion.36
  20.6 4.3 fusion.35
  25.9 2.0 dynamic-slice_convert_fusion.5
  28.0 2.0 dynamic-slice_convert_fusion.4
  30.0 1.9 dynamic-slice_convert_fusion.3
  32.0 1.0 dynamic-slice_convert_fusion.8
  33.1 1.0 dynamic-slice_convert_fusion.7
  34.2 41.6 %fusion = f32[32,128]{0,1:T(8,128)S(1)} fusion(bf16[32,128,3072]{2,1,0:T(8,128)(2,1)} %x_ref.3), kind=kLoop, calls=%fused_computation.2 | loop fusion | flops 37744640 | bytes 25182208 | tf_op jit(solution)/shard_map/reduce_sum | solution.py:453
  75.8 24.1 %fusion.43 = bf16[128,32,3072]{2,1,0:T(8,128)(2,1)S(1)} fusion(f32[3072]{0:T(1024)S(1)} %broadcast_add_fusion, f32[32,128]{0,1:T(8,128)S(1)} %add_rsqrt_fusion, bf16[32,128,3072]{2,1,0:T(8,128)(2,1)} %x_ref.3), kind=kLoop, calls=%fused_computation.133 | loop fusion | flops 50331648 | bytes 50360320 | tf_op jit(solution)/shard_map/transpose | solution.py:454
  100.0 2.7 collective-permute-start
  102.7 2.0 dynamic-slice_convert_fusion.6
  105.3 28.2 %fusion.2 = bf16[32,128,3072]{2,0,1:T(8,128)(2,1)} fusion(f32[3072]{0:T(1024)S(1)} %broadcast_add_fusion, f32[32,128]{0,1:T(8,128)S(1)} %add_rsqrt_fusion, bf16[32,128,3072]{2,1,0:T(8,128)(2,1)} %x_ref.3), kind=kLoop, calls=%fused_computation.4 | loop fusion | flops 50331648 | bytes 50360320 | tf_op jit(solution)/shard_map/convert_element_type | solution.py:454
  133.8 27.0 %copy.58 = bf16[128,32,3072]{2,1,0:T(8,128)(2,1)} copy(bf16[128,32,3072]{2,0,1:T(8,128)(2,1)} %bitcast.299) | data formatting | bytes 50331648 | tf_op jit(solution)/shard_map/transpose | solution.py:455
  160.8 1.3 stack.126
  162.7 2.3 broadcast_in_dim.20.pos_ref
  165.0 94.6 %first_pass_own.1 = (bf16[3,128,32,256]{3,2,1,0:T(8,128)(2,1)}, f32[3,128,32,256]{3,2,1,0:T(8,128)}, f32[3,128,32,256]{3,2,1,0:T(8,128)}, f32[3,128,32,256]{3,2,...) custom-call(s32[3]{0:T(128)} %iota.6.ids_ref, ...), custom_call_target="tpu_custom_call" | custom-call | flops 57982058496 | bytes 150994944 | tf_op jit(solution)/shard_map/first_pass_own/pallas_call | solution.py:181
  259.7 2.6 collective-permute-start.1
  262.2 11.2 convert_reduce_fusion
  274.6 10.6 all-gather.4
  286.6 6.5 collective-permute-done.2
  294.3 56.8 %second_pass_own.1 = (bf16[128,32,768]{2,1,0:T(8,128)(2,1)}, bf16[128,32,768]{2,1,0:T(8,128)(2,1)}, bf16[128,32,768]{2,1,0:T(8,128)(2,1)}, f32[3,32,768]{2,1,0:T...) custom-call(s32[3]{0:T(128)} %iota.5.ids_ref, ...), custom_call_target="tpu_custom_call" | custom-call | flops 37748736000 | bytes 62914560 | tf_op jit(solution)/shard_map/second_pass_own/pallas_call | solution.py:336
  351.1 1.3 collective-permute-start.9
  352.4 26.8 %convolution_bitcast_fusion = f32[3072,768]{1,0:T(8,128)} fusion(bf16[128,32,768]{2,1,0:T(8,128)(2,1)} %get-tuple-element.160.po_ref, bf16[32,128,3072]{2,0,1:T(8,128)(2,1)} %fusion.2), kind=kOutput, calls=%fused_computation.12 | convolution fusion | flops 19327352832 | bytes 40894464 | tf_op jit(solution)/shard_map/dot_general | solution.py:36
  380.5 37.3 %convolution_bitcast_fusion.2 = f32[768,3072]{1,0:T(8,128)} fusion(bf16[128,32,768]{2,1,0:T(8,128)(2,1)S(1)} %copy-done.29, bf16[128,32,3072]{2,0,1:T(8,128)(2,1)} %bitcast.300), kind=kOutput, calls=%fused_computation.14 | convolution fusion | flops 19327352832 | bytes 40894464 | tf_op jit(solution)/shard_map/dot_general | solution.py:36
  418.3 1.0 fusion.38
  420.6 27.1 %convolution_bitcast_fusion.1 = f32[3072,768]{1,0:T(8,128)} fusion(bf16[128,32,768]{2,1,0:T(8,128)(2,1)} %fusion.3.do_ref, bf16[32,128,3072]{2,0,1:T(8,128)(2,1)} %fusion.2), kind=kOutput, calls=%fused_computation.13 | convolution fusion | flops 19327352832 | bytes 40894464 | tf_op jit(solution)/shard_map/dot_general | solution.py:36
  447.8 3.6 slice_bitcast_fusion.2
  451.3 102.1 %first_pass_far.5 = (bf16[3,128,32,256]{3,2,1,0:T(8,128)(2,1)}, f32[3,128,32,256]{3,2,1,0:T(8,128)}, f32[3,128,32,256]{3,2,1,0:T(8,128)}, f32[3,128,32,256]{3,2,...) custom-call(s32[3]{0:T(128)} %pad_add_fusion.ids_ref, ...), custom_call_target="tpu_custom_call" | custom-call | flops 57982058496 | bytes 150994944 | tf_op jit(solution)/shard_map/first_pass_far/pallas_call | solution.py:181
  553.5 1.2 collective-permute-start.7
  554.7 102.4 %first_pass_far.4 = (bf16[3,128,32,256]{3,2,1,0:T(8,128)(2,1)}, f32[3,128,32,256]{3,2,1,0:T(8,128)}, f32[3,128,32,256]{3,2,1,0:T(8,128)}, f32[3,128,32,256]{3,2,...) custom-call(s32[3]{0:T(128)} %pad_add_fusion.ids_ref, ...), custom_call_target="tpu_custom_call" | custom-call | flops 57982058496 | bytes 150994944 | tf_op jit(solution)/shard_map/first_pass_far/pallas_call | solution.py:181
  657.2 86.6 %all-gather.26.cloned.1.call-done = f32[1024,3072]{1,0:T(8,128)} async-done(((f32[64,3072]{1,0:T(8,128)}), f32[1024,3072]{1,0:T(8,128)}) %all-gather.26.cloned.1.call-update) | async-done | bytes 12582928 | tf_op jit(solution)/shard_map/all_gather | solution.py:438
  743.8 102.2 %first_pass_far.3 = (bf16[3,128,32,256]{3,2,1,0:T(8,128)(2,1)}, f32[3,128,32,256]{3,2,1,0:T(8,128)}, f32[3,128,32,256]{3,2,1,0:T(8,128)}, f32[3,128,32,256]{3,2,...) custom-call(s32[3]{0:T(128)} %pad_add_fusion.ids_ref, ...), custom_call_target="tpu_custom_call" | custom-call | flops 57982058496 | bytes 150994944 | tf_op jit(solution)/shard_map/first_pass_far/pallas_call | solution.py:181
  846.4 19.6 %pad_maximum_fusion.4 = (bf16[3072,2304]{1,0:T(8,128)(2,1)}, bf16[3072,2304]{1,0:T(8,128)(2,1)}) fusion(bf16[3072,768]{1,0:T(8,128)(2,1)} %get-tuple-element.166, bf16[3072,768]{1,0:T(8,128)(2,1)} %get-tuple-element.165, bf16[3072,768]{1,0:T(8,128)(2,1)} %get-tuple-element.164, bf16[3072,768]{1,0:T(8,128)(2,1)} %get-tuple-element.169, ...), kind=kLoop, calls=%fused_computation.10 | loop fusion | flops 84934656 | bytes 56623104 | tf_op jit(solution)/shard_map/concatenate | solution.py:480
  866.0 12.4 pad_maximum_fusion.3.wf_ref
  878.5 1.0 fusion.8
  879.7 1.7 fusion.14
  881.4 1.9 collective-permute-start.6
  884.8 2.5 collective-permute-done.8
  887.3 1.0 select_bitcast_fusion.1
  889.1 47.8 %second_pass_far.5 = (bf16[128,32,768]{2,1,0:T(8,128)(2,1)}, bf16[128,32,768]{2,1,0:T(8,128)(2,1)}, bf16[128,32,768]{2,1,0:T(8,128)(2,1)}, f32[3,32,768]{2,1,0:T(8,128)}, f32[3,32,768]{2,1,0:T(8,128)}) custom-call(s32[3]{0:T(128)} %pad_add_fusion.ids_ref, bf16[3,128,32,256]{3,2,1,0:T(8,128)(2,1)} %get-tuple-element.139.c_ref, ...), custom_call_target="tpu_custom_call" | custom-call | flops 37748736000 | bytes 62914560 | tf_op jit(solution)/shard_map/second_pass_far/pallas_call | solution.py:336
  936.8 1.3 collective-permute-start.12
  938.2 1.1 select_bitcast_fusion.3
  939.9 47.9 %second_pass_far.4 = (bf16[128,32,768]{2,1,0:T(8,128)(2,1)}, bf16[128,32,768]{2,1,0:T(8,128)(2,1)}, bf16[128,32,768]{2,1,0:T(8,128)(2,1)}, f32[3,32,768]{2,1,0:T(8,128)}, f32[3,32,768]{2,1,0:T(8,128)}) custom-call(s32[3]{0:T(128)} %pad_add_fusion.ids_ref, bf16[3,128,32,256]{3,2,1,0:T(8,128)(2,1)} %get-tuple-element.133.c_ref, ...), custom_call_target="tpu_custom_call" | custom-call | flops 37748736000 | bytes 62914560 | tf_op jit(solution)/shard_map/second_pass_far/pallas_call | solution.py:336
  987.8 1.3 collective-permute-start.11
  989.1 1.1 select_bitcast_fusion.5
  990.9 48.0 %second_pass_far.3 = (bf16[128,32,768]{2,1,0:T(8,128)(2,1)}, bf16[128,32,768]{2,1,0:T(8,128)(2,1)}, bf16[128,32,768]{2,1,0:T(8,128)(2,1)}, f32[3,32,768]{2,1,0:T(8,128)}, f32[3,32,768]{2,1,0:T(8,128)}) custom-call(s32[3]{0:T(128)} %pad_add_fusion.ids_ref, bf16[3,128,32,256]{3,2,1,0:T(8,128)(2,1)} %get-tuple-element.127.c_ref, ...), custom_call_target="tpu_custom_call" | custom-call | flops 37748736000 | bytes 62914560 | tf_op jit(solution)/shard_map/second_pass_far/pallas_call | solution.py:336
  1038.9 1.3 collective-permute-start.10
  1040.2 16.2 %pad_maximum_fusion.mf_ref = bf16[128,32,2304]{2,1,0:T(8,128)(2,1)} fusion(bf16[128,32,768]{2,1,0:T(8,128)(2,1)} %get-tuple-element.144, bf16[128,32,768]{2,1,0:T(8,128)(2,1)} %get-tuple-element.138, bf16[128,32,768]{2,1,0:T(8,128)(2,1)} %get-tuple-element.132), kind=kLoop, calls=%fused_computation.6 | loop fusion | flops 56623104 | bytes 37748736 | tf_op jit(solution)/shard_map/concatenate | solution.py:479
  1056.4 101.1 %out_pass.1 = bf16[32,128,3072]{2,1,0:T(8,128)(2,1)} custom-call(bf16[128,32,768]{2,1,0:T(8,128)(2,1)} %get-tuple-element.126.mo_ref, bf16[128,32,2304]{2,1,0:T(8,128)(2,1)} %pad_maximum_fusion.mf_ref, bf16[768,3072]{1,0:T(8,128)(2,1)} %wo_ref.3, bf16[2304,3072]{1,0:T(8,128)(2,1)} %pad_maximum_fusion.3.wf_ref, bf16[32,128,3072]{2,1,0:T(8,128)(2,1)} %x_ref.3, ...), custom_call_target="tpu_custom_call" | custom-call | flops 77309411328 | bytes 100663296 | tf_op jit(solution)/shard_map/out_pass/pallas_call | solution.py:361
  1157.5 16.9 %pad_maximum_fusion.2.pf_ref = bf16[128,32,2304]{2,1,0:T(8,128)(2,1)} fusion(bf16[128,32,768]{2,1,0:T(8,128)(2,1)} %get-tuple-element.163, bf16[128,32,768]{2,1,0:T(8,128)(2,1)} %get-tuple-element.162, bf16[128,32,768]{2,1,0:T(8,128)(2,1)} %get-tuple-element.161), kind=kLoop, calls=%fused_computation.8 | loop fusion | flops 56623104 | bytes 37748736 | tf_op jit(solution)/shard_map/concatenate | solution.py:479
  1174.5 1.7 fusion.6
  1176.1 1.7 fusion.5
  1177.8 1.0 fusion.4
  1178.8 13.4 pad_maximum_fusion.1.df_ref
  1192.2 197.2 %norm_back_pass.1 = (bf16[32,128,3072]{2,1,0:T(8,128)(2,1)}, f32[8,3072]{1,0:T(8,128)}) custom-call(bf16[128,32,768]{2,1,0:T(8,128)(2,1)} %fusion.3.do_ref, bf16[128,32,2304]{2,1,0:T(8,128)(2,1)} %pad_maximum_fusion.1.df_ref, bf16[128,32,768]{2,1,0:T(8,128)(2,1)} %get-tuple-element.160.po_ref, bf16[128,32,2304]{2,1,0:T(8,128)(2,1)} %pad_maximum_fusion.2.pf_ref, ...), custom_call_target="tpu_custom_call" | custom-call | flops 154618822656 | bytes 125829120 | tf_op jit(solution)/shard_map/norm_back_pass/pallas_call | solution.py:399
  1390.3 16.5 %all-reduce = (f32[3072]{0:T(1024)}, f32[768]{0:T(1024)}, f32[768]{0:T(1024)}, f32[4,768]{1,0:T(4,128)}, f32[768]{0:T(1024)}, /*index=5*/f32[768]{0:T(1024)}, f32[768]{0:T(1024)}, f32[768]{0:T(1024)}, f32[3072]{0:T(1024)}) all-reduce(f32[3072]{0:T(1024)S(1)} %reduce_sum.46, ...), channel_id=1, replica_groups=mesh['tp'=4,'cp'=4] {'cp'}, use_global_device_ids=true, to_apply=%region_2.3 | all-reduce | flops 13824 | bytes 110592 | tf_op jit(solution)/shard_map/psum | solution.py:493
  1406.8 9.3 copy.97
  1416.1 4.8 copy.98
  1420.9 2.7 copy.99
  1424.3 3.7 copy.101
  (154 shorter events, 17.8 us)
Async XLA Ops:
  8.0 439.8 %all-gather.28.cloned.1.call-start = ((), (), s32[]{:S(2)}) async-start(), calls=%async_computation.3 | async-start | bytes 3342336 | tf_op jit(solution)/shard_map/all_gather | solution.py:438
  10.0 14.9 %copy-start.14 = (bf16[6,128,256]{2,1,0:T(8,128)(2,1)}, bf16[6,128,256]{2,1,0:T(8,128)(2,1)S(1)}, u32[]{:S(2)}) copy-start(bf16[6,128,256]{2,1,0:T(8,128)(2,1)S(1)} %constant_dynamic-update-slice_fusion) | copy-start | bytes 1179652
  10.8 440.5 %all-gather.36.cloned.1.call-start = ((), (), s32[]{:S(2)}) async-start(), calls=%async_computation.7 | async-start | bytes 13369344 | tf_op jit(solution)/shard_map/all_gather | solution.py:438
  15.7 435.7 %all-gather.38.cloned.1.call-start = ((), (), s32[]{:S(2)}) async-start(), calls=%async_computation.8 | async-start | bytes 13369344 | tf_op jit(solution)/shard_map/all_gather | solution.py:438
  19.6 14.6 %copy-start.17 = (bf16[3072]{0:T(1024)(128)(2,1)S(1)}, bf16[3072]{0:T(1024)(128)(2,1)}, u32[]{:S(2)}) copy-start(bf16[3072]{0:T(1024)(128)(2,1)} %param.28) | copy-start | bytes 18436
  20.5 430.8 %all-gather.40.cloned.1.call-start = ((), (), s32[]{:S(2)}) async-start(), calls=%async_computation.9 | async-start | bytes 13369344 | tf_op jit(solution)/shard_map/all_gather | solution.py:438
  25.9 528.8 %all-gather.30.cloned.1.call-start = ((), (), s32[]{:S(2)}) async-start(), calls=%async_computation.4 | async-start | bytes 13369344 | tf_op jit(solution)/shard_map/all_gather | solution.py:438
  27.9 526.7 %all-gather.32.cloned.1.call-start = ((), (), s32[]{:S(2)}) async-start(), calls=%async_computation.5 | async-start | bytes 13369344 | tf_op jit(solution)/shard_map/all_gather | solution.py:438
  30.0 524.7 %all-gather.34.cloned.1.call-start = ((), (), s32[]{:S(2)}) async-start(), calls=%async_computation.6 | async-start | bytes 13369344 | tf_op jit(solution)/shard_map/all_gather | solution.py:438
  32.0 625.3 %all-gather.22.cloned.1.call-start = ((), (), s32[]{:S(2)}) async-start(), calls=%async_computation | async-start | bytes 13369344 | tf_op jit(solution)/shard_map/all_gather | solution.py:438
  33.0 624.2 %all-gather.24.cloned.1.call-start = ((), (), s32[]{:S(2)}) async-start(), calls=%async_computation.1 | async-start | bytes 13369344 | tf_op jit(solution)/shard_map/all_gather | solution.py:438
  34.1 709.7 %all-gather.26.cloned.1.call-start = ((), (), s32[]{:S(2)}) async-start(), calls=%async_computation.2 | async-start | bytes 13369344 | tf_op jit(solution)/shard_map/all_gather | solution.py:438
  100.0 62.1 %collective-permute-start = (f32[3,32,3072]{2,1,0:T(8,128)S(1)}, f32[3,32,3072]{2,1,0:T(8,128)S(1)}, u32[]{:S(2)}, u32[]{:S(2)}) collective-permute-start(f32[3,32,3072]{2,1,0:T(8,128)S(1)} %slice_convert_fusion), channel_id=1, source_target_pairs={{0,1},{1,2},{2,3},{4,5},{5,6},{6,7},{8,9},{9,10},{10,11},{12,13},{... | collective-permute-start | bytes 3538952 | tf_op jit(solution)/shard_map/ppermute | solution.py:456
  104.7 28.8 %copy-start.23 = (bf16[768]{0:T(1024)(128)(2,1)S(1)}, bf16[768]{0:T(1024)(128)(2,1)}, u32[]{:S(2)}) copy-start(bf16[768]{0:T(1024)(128)(2,1)} %param.30) | copy-start | bytes 4612
  104.7 28.8 %copy-start.24 = (bf16[768]{0:T(1024)(128)(2,1)S(1)}, bf16[768]{0:T(1024)(128)(2,1)}, u32[]{:S(2)}) copy-start(bf16[768]{0:T(1024)(128)(2,1)} %param.32) | copy-start | bytes 4612
  104.7 28.9 %copy-start.25 = (bf16[768]{0:T(1024)(128)(2,1)S(1)}, bf16[768]{0:T(1024)(128)(2,1)}, u32[]{:S(2)}) copy-start(bf16[768]{0:T(1024)(128)(2,1)} %param.34) | copy-start | bytes 4612
  104.7 28.9 %copy-start.26 = (bf16[768]{0:T(1024)(128)(2,1)S(1)}, bf16[768]{0:T(1024)(128)(2,1)}, u32[]{:S(2)}) copy-start(bf16[768]{0:T(1024)(128)(2,1)} %param.36) | copy-start | bytes 4612
  104.7 28.9 %copy-start.27 = (bf16[768]{0:T(1024)(128)(2,1)S(1)}, bf16[768]{0:T(1024)(128)(2,1)}, u32[]{:S(2)}) copy-start(bf16[768]{0:T(1024)(128)(2,1)} %param.38) | copy-start | bytes 4612
  104.8 28.9 %copy-start.20 = (f32[768]{0:T(1024)S(1)}, f32[768]{0:T(1024)}, u32[]{:S(2)}) copy-start(f32[768]{0:T(1024)} %param.39) | copy-start | bytes 9220
  104.8 28.9 %copy-start.19 = (s32[32,128]{1,0:T(8,128)S(1)}, s32[32,128]{1,0:T(8,128)}, u32[]{:S(2)}) copy-start(s32[32,128]{1,0:T(8,128)} %param.27) | copy-start | bytes 49156
  104.8 1302.1 %all-reduce.4.cloned.1.call-start = ((), (), s32[]{:S(2)}) async-start(), calls=%async_computation.10 | async-start | bytes 58195968 | tf_op jit(solution)/shard_map/psum | solution.py:493
  133.8 27.0 %copy-start.16 = (bf16[4,768]{1,0:T(4,128)(2,1)S(1)}, bf16[4,768]{1,0:T(4,128)(2,1)}, u32[]{:S(2)}) copy-start(bf16[4,768]{1,0:T(4,128)(2,1)} %param.33) | copy-start | bytes 18436
  162.1 2.8 copy-start.28
  259.6 13.8 copy-start.18
  259.6 14.4 %copy-start.22 = (bf16[3072]{0:T(1024)(128)(2,1)S(1)}, bf16[3072]{0:T(1024)(128)(2,1)}, u32[]{:S(2)}) copy-start(bf16[3072]{0:T(1024)(128)(2,1)} %param.41) | copy-start | bytes 18436
  259.6 15.0 %copy-start.15 = (f32[16,3,256]{2,0,1:T(8,128)S(1)}, f32[16,3,256]{2,0,1:T(8,128)}, u32[]{:S(2)}) copy-start(f32[16,3,256]{2,0,1:T(8,128)} %stack.126) | copy-start | bytes 147460
  259.6 26.3 %copy-start.7 = (f32[3,32,768]{2,1,0:T(8,128)S(1)}, f32[3,32,768]{2,1,0:T(8,128)}, u32[]{:S(2)}) copy-start(f32[3,32,768]{2,1,0:T(8,128)} %get-tuple-element.123) | copy-start | bytes 884740
  259.7 26.3 %collective-permute-start.1 = (f32[3,32,768]{2,1,0:T(8,128)}, f32[3,32,768]{2,1,0:T(8,128)S(1)}, u32[]{:S(2)}, u32[]{:S(2)}) collective-permute-start(f32[3,32,768]{2,1,0:T(8,128)} %get-tuple-element.123), channel_id=1, source_target_pairs={{0,1},{1,0},{2,3},{3,2},{4,5},{5,4},{6,7},{7,6},{8,9},{9,8},{10,11... | collective-permute-start | bytes 884744 | tf_op jit(solution)/shard_map/ppermute | solution.py:412
  286.0 7.1 collective-permute-start.2
  351.1 68.2 %collective-permute-start.9 = (f32[3,32,768]{2,1,0:T(8,128)}, f32[3,32,768]{2,1,0:T(8,128)S(1)}, u32[]{:S(2)}, u32[]{:S(2)}) collective-permute-start(f32[3,32,768]{2,1,0:T(8,128)} %get-tuple-element.150), channel_id=1, source_target_pairs={{1,0},{2,1},{3,2},{5,4},{6,5},{7,6},{9,8},{10,9},{11,10},{13,12},{... | collective-permute-start | bytes 884744 | tf_op jit(solution)/shard_map/ppermute | solution.py:465
  352.4 26.8 %copy-start.13 = (f32[6,80,128]{2,1,0:T(8,128)S(1)}, f32[6,80,128]{2,1,0:T(8,128)}, u32[]{:S(2)}) copy-start(f32[6,80,128]{2,1,0:T(8,128)} %get-tuple-element.172) | copy-start | bytes 737284
  352.4 28.1 %copy-start.29 = (bf16[128,32,768]{2,1,0:T(8,128)(2,1)S(1)}, bf16[128,32,768]{2,1,0:T(8,128)(2,1)}, u32[]{:S(2)}) copy-start(bf16[128,32,768]{2,1,0:T(8,128)(2,1)} %get-tuple-element.126.mo_ref) | copy-start | bytes 18874372
  380.5 37.3 %copy-start.21 = (f32[768]{0:T(1024)S(1)}, f32[768]{0:T(1024)}, u32[]{:S(2)}) copy-start(f32[768]{0:T(1024)} %param.39) | copy-start | bytes 9220
  380.5 37.9 %copy-start.3 = (f32[6,128,256]{2,1,0:T(8,128)S(1)}, f32[6,128,256]{2,1,0:T(8,128)}, u32[]{:S(2)}) copy-start(f32[6,128,256]{2,1,0:T(8,128)} %get-tuple-element.173) | copy-start | bytes 2359300
  380.5 39.5 %copy-start.12 = (f32[3,32,768]{2,1,0:T(8,128)S(1)}, f32[3,32,768]{2,1,0:T(8,128)}, u32[]{:S(2)}) copy-start(f32[3,32,768]{2,1,0:T(8,128)} %get-tuple-element.149) | copy-start | bytes 884740
  553.5 325.0 %collective-permute-start.7 = (f32[3,32,768]{2,1,0:T(8,128)}, f32[3,32,768]{2,1,0:T(8,128)}, u32[]{:S(2)}, u32[]{:S(2)}) collective-permute-start(f32[3,32,768]{2,1,0:T(8,128)} %get-tuple-element.143), channel_id=1, source_target_pairs={{0,1},{1,0},{2,3},{3,2},{4,5},{5,4},{6,7},{7,6},{8,9},{9,8},{10,11... | collective-permute-start | bytes 884744 | tf_op jit(solution)/shard_map/ppermute | solution.py:412
  657.1 222.6 %collective-permute-start.5 = (f32[3,32,768]{2,1,0:T(8,128)}, f32[3,32,768]{2,1,0:T(8,128)}, u32[]{:S(2)}, u32[]{:S(2)}) collective-permute-start(f32[3,32,768]{2,1,0:T(8,128)} %get-tuple-element.137), channel_id=1, source_target_pairs={{0,1},{1,0},{2,3},{3,2},{4,5},{5,4},{6,7},{7,6},{8,9},{9,8},{10,11... | collective-permute-start | bytes 884744 | tf_op jit(solution)/shard_map/ppermute | solution.py:412
  846.1 37.2 %collective-permute-start.3 = (f32[3,32,768]{2,1,0:T(8,128)}, f32[3,32,768]{2,1,0:T(8,128)S(1)}, u32[]{:S(2)}, u32[]{:S(2)}) collective-permute-start(f32[3,32,768]{2,1,0:T(8,128)} %get-tuple-element.131), channel_id=1, source_target_pairs={{0,1},{1,0},{2,3},{3,2},{4,5},{5,4},{6,7},{7,6},{8,9},{9,8},{10,11... | collective-permute-start | bytes 884744 | tf_op jit(solution)/shard_map/ppermute | solution.py:412
  866.0 12.5 copy-start.5
  866.0 13.7 copy-start.6
  866.0 18.0 %copy-start.8 = (f32[3,32,768]{2,1,0:T(8,128)S(1)}, f32[3,32,768]{2,1,0:T(8,128)}, u32[]{:S(2)}) copy-start(f32[3,32,768]{2,1,0:T(8,128)} %get-tuple-element.131) | copy-start | bytes 884740
  879.5 7.8 collective-permute-start.8
  881.4 56.7 %collective-permute-start.6 = (f32[32,768]{1,0:T(8,128)}, f32[32,768]{1,0:T(8,128)}, u32[]{:S(2)}, u32[]{:S(2)}) collective-permute-start(f32[32,768]{1,0:T(8,128)} %fusion.14), channel_id=1, source_target_pairs={{0,2},{1,3},{2,0},{3,1},{4,6},{5,7},{6,4},{7,5},{8,10},{9,11},{10,... | collective-permute-start | bytes 294920 | tf_op jit(solution)/shard_map/ppermute | solution.py:418
  883.3 0.7 copy-start.2
  884.7 104.4 %collective-permute-start.4 = (f32[32,768]{1,0:T(8,128)}, f32[32,768]{1,0:T(8,128)}, u32[]{:S(2)}, u32[]{:S(2)}) collective-permute-start(f32[32,768]{1,0:T(8,128)} %fusion.20), channel_id=1, source_target_pairs={{0,2},{1,3},{2,0},{3,1},{4,6},{5,7},{6,4},{7,5},{8,10},{9,11},{10,... | collective-permute-start | bytes 294920 | tf_op jit(solution)/shard_map/ppermute | solution.py:418
  936.8 237.6 %collective-permute-start.12 = (f32[3,32,768]{2,1,0:T(8,128)}, f32[3,32,768]{2,1,0:T(8,128)}, u32[]{:S(2)}, u32[]{:S(2)}) collective-permute-start(f32[3,32,768]{2,1,0:T(8,128)} %get-tuple-element.159), channel_id=1, source_target_pairs={{1,0},{2,1},{3,2},{5,4},{6,5},{7,6},{9,8},{10,9},{11,10},{13,12},{... | collective-permute-start | bytes 884744 | tf_op jit(solution)/shard_map/ppermute | solution.py:475
  987.8 188.3 %collective-permute-start.11 = (f32[3,32,768]{2,1,0:T(8,128)}, f32[3,32,768]{2,1,0:T(8,128)}, u32[]{:S(2)}, u32[]{:S(2)}) collective-permute-start(f32[3,32,768]{2,1,0:T(8,128)} %get-tuple-element.156), channel_id=1, source_target_pairs={{1,0},{2,1},{3,2},{5,4},{6,5},{7,6},{9,8},{10,9},{11,10},{13,12},{... | collective-permute-start | bytes 884744 | tf_op jit(solution)/shard_map/ppermute | solution.py:475
  1038.9 138.9 %collective-permute-start.10 = (f32[3,32,768]{2,1,0:T(8,128)}, f32[3,32,768]{2,1,0:T(8,128)}, u32[]{:S(2)}, u32[]{:S(2)}) collective-permute-start(f32[3,32,768]{2,1,0:T(8,128)} %get-tuple-element.153), channel_id=1, source_target_pairs={{1,0},{2,1},{3,2},{5,4},{6,5},{7,6},{9,8},{10,9},{11,10},{13,12},{... | collective-permute-start | bytes 884744 | tf_op jit(solution)/shard_map/ppermute | solution.py:475
  1157.5 16.9 %copy-start.9 = (f32[3,32,768]{2,1,0:T(8,128)S(1)}, f32[3,32,768]{2,1,0:T(8,128)}, u32[]{:S(2)}) copy-start(f32[3,32,768]{2,1,0:T(8,128)} %get-tuple-element.158) | copy-start | bytes 884740
  1157.5 18.6 %copy-start.10 = (f32[3,32,768]{2,1,0:T(8,128)S(1)}, f32[3,32,768]{2,1,0:T(8,128)}, u32[]{:S(2)}) copy-start(f32[3,32,768]{2,1,0:T(8,128)} %get-tuple-element.155) | copy-start | bytes 884740
  1157.5 20.3 %copy-start.1 = (bf16[128,32,768]{2,1,0:T(8,128)(2,1)S(1)}, bf16[128,32,768]{2,1,0:T(8,128)(2,1)}, u32[]{:S(2)}) copy-start(bf16[128,32,768]{2,1,0:T(8,128)(2,1)} %get-tuple-element.151) | copy-start | bytes 18874372
  1157.5 20.3 %copy-start.11 = (f32[3,32,768]{2,1,0:T(8,128)S(1)}, f32[3,32,768]{2,1,0:T(8,128)}, u32[]{:S(2)}) copy-start(f32[3,32,768]{2,1,0:T(8,128)} %get-tuple-element.152) | copy-start | bytes 884740
  1406.8 9.3 copy-start
  1406.8 17.5 %slice-start = ((s8[9437184]{0:T(1024)(128)(4,1)}), s8[4194304]{0:T(1024)(128)(4,1)S(1)}, s32[]{:S(2)}) async-start(s8[9437184]{0:T(1024)(128)(4,1)} %bitcast.309), calls=%async_computation.11 | async-start | bytes 8388608
  1406.8 17.5 %slice-start.1 = ((s8[9437184]{0:T(1024)(128)(4,1)}), s8[4194304]{0:T(1024)(128)(4,1)S(1)}, s32[]{:S(2)}) async-start(s8[9437184]{0:T(1024)(128)(4,1)} %bitcast.309), calls=%async_computation.12 | async-start | bytes 8388608
  1416.1 7.5 copy-start.4
  1416.1 8.2 slice-start.2
Sparse Core Ops, SparseCore 0:
  11.0 34.3 all-gather.27
  47.7 62.2 all-gather.35
  112.2 62.3 all-gather.37
  176.7 62.3 all-gather.39
  241.1 64.0 all-gather.29
  307.3 65.0 all-gather.31
  374.7 62.2 all-gather.33
  439.2 89.4 all-gather.21
  531.0 105.2 all-gather.23
  638.4 105.4 all-gather.25
Sparse Core Ops, SparseCore 1:
  447.8 610.7 all-reduce.3

commit v2 on v1

v2 whole, which is shorter than its diff:
```python
import functools
import jax
import jax.numpy as jnp
from jax import lax
from jax.experimental import pallas as pl
from jax.experimental.pallas import tpu as pltpu
from jax.sharding import PartitionSpec as P

NORM_EPS = 1e-6
CONV_WIDTH = 4
HALO = CONV_WIDTH - 1
LANES = 128
CB = 256
TC = 16
TINY = 1.2e-38
GELU_A = 0.7978845608028654
GELU_B = 0.044715
VMEM_BYTES = 67043328
F32 = jnp.float32
BF16 = jnp.bfloat16
TOKENS, COLS, CHANNEL = P(None, "cp"), P(None, "tp"), P("tp")
PARAM_SPECS = (P(), COLS, CHANNEL, COLS, CHANNEL, COLS, CHANNEL, CHANNEL, CHANNEL, CHANNEL, CHANNEL, CHANNEL, CHANNEL, P())
IN_SPECS = (TOKENS, TOKENS, TOKENS, *PARAM_SPECS)
OUT_SPECS = (TOKENS, TOKENS, *PARAM_SPECS)
R_BX, R_BY, R_CB, R_BA, R_BI, R_K, R_CW = range(7)
PAR_ROWS = 16
EXT_ROWS = 48
EXT_PAR = 256
N_TILE = 512
SUB = 8
B_BLK = 16


def dot_nn(lhs, rhs):
    return jnp.dot(lhs, rhs, preferred_element_type=F32)


def dot_nt(lhs, rhs):
    return lax.dot_general(lhs, rhs, (((1,), (1,)), ((), ())), preferred_element_type=F32)


def dot_tn(lhs, rhs):
    return lax.dot_general(lhs, rhs, (((0,), (0,)), ((), ())), preferred_element_type=F32)


def round16(val):
    return val.astype(BF16).astype(F32)


def sigmoid(val):
    return 1.0 / (1.0 + jnp.exp(-val))


def gates(pre_a, pre_i, slope, keep):
    gate_r = sigmoid(pre_a)
    gate_i = sigmoid(pre_i)
    log_a = gate_r * slope
    raw_a = jnp.exp(log_a)
    gap = jnp.tanh(-log_a) * (1.0 + raw_a * raw_a)
    inv_m = lax.rsqrt(jnp.maximum(gap, TINY))
    decay = jnp.where(keep, raw_a, 0.0)
    mult = jnp.where(keep, gap * inv_m, 1.0)
    return gate_r, gate_i, decay, mult, inv_m


def first_pass_kernel(n_ref, gz_ref, nh_ref, pos_ref, *rest, n_blk, n_chunk, own, batch):
    if own:
        ext, rest = rest[0], rest[1:]
        w_hbm, rest = rest[:3], rest[3:]
        c_out, y_out, g_out, q_out, info_out, xb_out, xh, w16, wo16, w_sem, xs, ys, ds, pre, tail, state = rest
    else:
        w_hbm, rest = rest[:4 * n_blk], rest[4 * n_blk:]
        c_out, y_out, g_out, q_out, info_out, ext, w_out, w16, stage, w_sem, o_sem, xs, ys, ds, pre, xh, tail, state = rest
        xb_out = None
    step = pl.program_id(0)
    width = n_ref.shape[1]
    quarter = width // 4

    def own_loads(blk):
        cols = pl.ds(blk * CB, CB)
        pair = [pltpu.make_async_copy(w_hbm[k].at[:, cols], w16.at[blk, k], w_sem.at[blk, k]) for k in range(2)]
        return pair + [pltpu.make_async_copy(w_hbm[2].at[cols, :], wo16.at[blk], w_sem.at[blk, 2])]

    def far_load(idx):
        return pltpu.make_async_copy(w_hbm[idx], stage.at[idx % 4], w_sem.at[idx])

    def stores(blk):
        return [pltpu.make_async_copy(w16.at[blk, k], w_out.at[k, :, pl.ds(blk * CB, CB)], o_sem.at[blk, k]) for k in range(3)]

    def dots(blk):
        rows = n_ref[:]
        xs[blk] = dot_nn(rows, w16[blk, 0])
        ys[blk] = dot_nn(rows, w16[blk, 1])
        ds[blk] = dot_nt(gz_ref[:], wo16[blk]) if own else dot_nn(gz_ref[:], w16[blk, 2])

    def fetch(blk):
        if own:
            for copy in own_loads(blk):
                copy.wait()
        else:
            core = lax.rem(lax.axis_index("cp"), 2)
            for i in range(4):
                far_load(4 * blk + i).wait()
                side = core if i < 2 else 1 - core
                start = pl.multiple_of((2 * side + i % 2) * quarter, quarter)
                for k in range(3):
                    w16[blk, k, pl.ds(start, quarter), :] = stage[i, k, :quarter].astype(BF16)
                    if i < 2:
                        ext[blk, (3 * i + k) * EXT_ROWS:(3 * i + k + 1) * EXT_ROWS] = stage[i, k, quarter:]
                if blk + 1 < n_blk:
                    far_load(4 * blk + 4 + i).start()
            for copy in stores(blk):
                copy.start()
        xh[blk] = dot_nn(nh_ref[:].astype(BF16), w16[blk, 0])

    def elementwise(blk):
        first = step == 1
        for half in range(CB // LANES):
            lane = slice(half * LANES, (half + 1) * LANES)
            row = lambda idx: ext[blk, EXT_PAR + idx:EXT_PAR + idx + 1, lane]
            bias_x, conv_b = row(R_BX), row(R_CB)
            taps = [row(R_CW + k) for k in range(CONV_WIDTH)]
            past = []
            for j in range(HALO):
                sl = slice(j * batch, (j + 1) * batch)
                past.append(jnp.where(first, round16(xh[blk, sl, lane] + bias_x), tail[blk, sl, lane]))
            for t in range(TC):
                sl = slice(t * batch, (t + 1) * batch)
                cur = round16(xs[blk, sl, lane] + bias_x)
                if own:
                    xb_out[blk, t, :, lane] = cur.astype(BF16)
                pos = pos_ref[t]
                total = conv_b + cur * taps[0]
                for k in range(1, CONV_WIDTH):
                    total = total + jnp.where(pos >= k, past[HALO - k], 0.0) * taps[k]
                c_out[blk, t, :, lane] = total.astype(BF16)
                past = past[1:] + [cur]
            for j in range(HALO):
                tail[blk, j * batch:(j + 1) * batch, lane] = past[j]
            wg = ext[blk, half * LANES:(half + 1) * LANES].astype(BF16)
            pre[half] = dot_nn(c_out[blk, :, :, lane].reshape(TC * batch, LANES), wg)
            bias_y, bias_a, bias_i, slope = row(R_BY), row(R_BA), row(R_BI), row(R_K)
            hid = jnp.where(first, 0.0, state[blk, 0, :, lane])
            prod = jnp.where(first, 1.0, state[blk, 1, :, lane])
            head = jnp.where(first, 0.0, state[blk, 2, :, lane])
            for t in range(TC):
                sl = slice(t * batch, (t + 1) * batch)
                keep = pos_ref[t] >= 1
                conv = c_out[blk, t, :, lane].astype(F32)
                _, gate_i, decay, mult, _ = gates(pre[half, sl, :LANES] + bias_a, pre[half, sl, LANES:] + bias_i, slope, keep)
                hid = decay * hid + mult * gate_i * conv
                prod = prod * decay
                pre_y = ys[blk, sl, lane] + bias_y
                sq = pre_y * pre_y
                tan = jnp.tanh(pre_y * (GELU_A + GELU_A * GELU_B * sq))
                half_y = 0.5 * pre_y
                d_mixed = ds[blk, sl, lane]
                y_act = half_y + half_y * tan
                slope_y = 0.5 + 0.5 * tan + half_y * (1.0 - tan * tan) * (GELU_A + 3.0 * GELU_A * GELU_B * sq)
                grad_h = d_mixed * y_act
                head = head + prod * grad_h
                y_out[blk, t, :, lane] = y_act
                g_out[blk, t, :, lane] = grad_h
                q_out[blk, t, :, lane] = d_mixed * slope_y
            for idx, val in enumerate((hid, prod, head)):
                state[blk, idx, :, lane] = val
                info_out[blk, idx, :, lane] = val

    @pl.when(step == 0)
    def _():
        if own:
            for blk in range(n_blk):
                for copy in own_loads(blk):
                    copy.start()
        else:
            for i in range(4):
                far_load(i).start()
        for blk in range(n_blk):
            fetch(blk)
            dots(blk)

    @pl.when((step > 0) & (step < n_chunk))
    def _():
        for blk in range(n_blk):
            elementwise(blk)
            dots(blk)

    @pl.when(step == n_chunk)
    def _():
        def last(blk, _):
            elementwise(blk)
            return 0

        lax.fori_loop(0, n_blk, last, 0)
        if not own:
            for blk in range(n_blk):
                for copy in stores(blk):
                    copy.wait()


def first_pass(n_blk, normed, gz, n_halo, pos_b, weights, ext=None):
    own = ext is not None
    n_rows, width = normed.shape
    n_tok, batch = pos_b.shape[0], pos_b.shape[1]
    n_chunk = n_tok // TC
    cols = n_blk * CB
    rows = TC * batch
    cur = lambda s: jnp.minimum(s, n_chunk - 1)
    old = lambda s: jnp.maximum(s - 1, 0)
    const = lambda shape: pl.BlockSpec(shape, lambda s: (0,) * len(shape))
    row_spec = pl.BlockSpec((rows, width), lambda s: (cur(s), 0))
    any_spec = pl.BlockSpec(memory_space=pl.ANY)
    in_specs = [row_spec, row_spec, const((HALO * batch, width)), pl.BlockSpec((TC, batch, LANES), lambda s: (old(s), 0, 0))]
    tok_spec = pl.BlockSpec((n_blk, TC, batch, CB), lambda s: (0, old(s), 0, 0))
    tok_shape = lambda dt: jax.ShapeDtypeStruct((n_blk, n_tok, batch, CB), dt)
    ext_shape = (n_blk, 6 * EXT_ROWS, CB)
    out_specs = [tok_spec] * 4 + [const((n_blk, 3, batch, CB))]
    out_shape = [tok_shape(BF16), tok_shape(F32), tok_shape(F32), tok_shape(F32), jax.ShapeDtypeStruct((n_blk, 3, batch, CB), F32)]
    work = [pltpu.VMEM((n_blk, rows, CB), F32)] * 3 + [pltpu.VMEM((CB // LANES, rows, 2 * LANES), F32)]
    halo = pltpu.VMEM((n_blk, HALO * batch, CB), F32)
    state = pltpu.VMEM((n_blk, 3, batch, CB), F32)
    args = [normed, gz, n_halo, pos_b]
    if own:
        in_specs.append(const(ext_shape))
        args.append(ext)
        out_specs += [tok_spec, const((n_blk, HALO * batch, CB))]
        out_shape += [tok_shape(BF16), jax.ShapeDtypeStruct((n_blk, HALO * batch, CB), F32)]
        scratch = [pltpu.VMEM((n_blk, 2, width, CB), BF16), pltpu.VMEM((n_blk, CB, width), BF16), pltpu.SemaphoreType.DMA((n_blk, 3)), *work, halo, state]
    else:
        out_specs += [const(ext_shape), any_spec]
        out_shape += [jax.ShapeDtypeStruct(ext_shape, F32), jax.ShapeDtypeStruct((3, width, cols), BF16)]
        scratch = [pltpu.VMEM((n_blk, 3, width, CB), BF16), pltpu.VMEM((4, *weights[0].shape), F32), pltpu.SemaphoreType.DMA((4 * n_blk,)), pltpu.SemaphoreType.DMA((n_blk, 3)), *work, halo, halo, state]
    in_specs += [any_spec] * len(weights)
    flops = 6 * n_rows * width * cols
    return pl.pallas_call(
        functools.partial(first_pass_kernel, n_blk=n_blk, n_chunk=n_chunk, own=own, batch=batch),
        grid=(n_chunk + 1,), in_specs=in_specs, out_specs=out_specs, scratch_shapes=scratch, out_shape=out_shape,
        compiler_params=pltpu.CompilerParams(dimension_semantics=("arbitrary",), vmem_limit_bytes=VMEM_BYTES),
        cost_estimate=pl.CostEstimate(flops=flops, bytes_accessed=n_rows * width * 4, transcendentals=0),
        name="first_pass_own" if own else "first_pass_far",
    )(*args, *weights)


def turned(val):
    return jnp.swapaxes(val, 0, 1)


def lane_tiles(width):
    return [slice(k, k + LANES) for k in range(0, width, LANES)]


def pre_kernel(x_ref, gz_ref, s_ref, n_out, gz_out, inv_out, gb_out):
    width = x_ref.shape[2]
    total = 0.0
    for lane in lane_tiles(width):
        x_f = x_ref[:, :, lane].astype(F32)
        total = total + x_f * x_f
    inv_out[:] = jnp.broadcast_to(lax.rsqrt(jnp.sum(total, axis=-1, keepdims=True) * (1.0 / width) + NORM_EPS), inv_out.shape)

    @pl.when(pl.program_id(0) == 0)
    def _():
        gb_out[:] = jnp.zeros_like(gb_out)

    for lane in lane_tiles(width):
        normed = x_ref[:, :, lane].astype(F32) * inv_out[:] * (1.0 + s_ref[:, lane])
        n_out[:, :, lane] = turned(normed).astype(BF16)
        gz_f = gz_ref[:, :, lane].astype(F32)
        gz_out[:, :, lane] = turned(gz_f).astype(BF16)
        gb_out[:, lane] += jnp.sum(gz_f.reshape(-1, SUB, LANES), axis=0)


def row_specs(batch, n_tok):
    per = batch // B_BLK
    n_steps = (n_tok // TC) * per
    cur = lambda s: jnp.minimum(s, n_steps - 1)
    old = lambda s: jnp.maximum(s - 1, 0)
    act = lambda lanes: pl.BlockSpec((TC, B_BLK, lanes), lambda s: (cur(s) // per, lax.rem(cur(s), per), 0))
    native = lambda lag, lanes: pl.BlockSpec((B_BLK, TC, lanes), lambda s: (lax.rem(lag(s), per), lag(s) // per, 0))
    return n_steps, cur, old, act, native


def pre_pass(x_in, grad_z, scale):
    batch, n_tok, width = x_in.shape
    n_steps, cur, _, act, native = row_specs(batch, n_tok)
    const = lambda shape: pl.BlockSpec(shape, lambda s: (0,) * len(shape))
    return pl.pallas_call(
        pre_kernel, grid=(n_steps,),
        in_specs=[native(cur, width), native(cur, width), const((1, width))], out_specs=[act(width), act(width), native(cur, LANES), const((SUB, width))],
        out_shape=[jax.ShapeDtypeStruct((n_tok, batch, width), BF16)] * 2 + [jax.ShapeDtypeStruct((batch, n_tok, LANES), F32), jax.ShapeDtypeStruct((SUB, width), F32)],
        compiler_params=pltpu.CompilerParams(dimension_semantics=("arbitrary",), vmem_limit_bytes=VMEM_BYTES),
        cost_estimate=pl.CostEstimate(flops=n_tok * batch * width * 200, bytes_accessed=n_tok * batch * width * 8, transcendentals=0),
        name="pre_pass",
    )(x_in, grad_z, scale)


def send_kernel(core_ref, wx_ref, wy_ref, wo_ref, ext_ref, *outs):
    quarter = wx_ref.shape[0]
    for idx, out in enumerate(outs):
        @pl.when(pl.program_id(0) == idx)
        def _():
            values = wx_ref[:].astype(F32), wy_ref[:].astype(F32), wo_ref[:].astype(F32).T
            for k, val in enumerate(values):
                out[k, :quarter] = val
                out[k, quarter:] = ext_ref[0, k * EXT_ROWS:(k + 1) * EXT_ROWS]


def send_pass(core, w_x, w_y, w_out, ext):
    (width, _), n_own = w_x.shape, len(ext)
    quarter = width // 4
    tall = pl.BlockSpec((quarter, CB), lambda i, core: (2 * core[0] + lax.rem(i, 2), i // 2))
    wide = pl.BlockSpec((CB, quarter), lambda i, core: (i // 2, 2 * core[0] + lax.rem(i, 2)))
    shape = (3, quarter + EXT_ROWS, CB)
    return pl.pallas_call(
        send_kernel,
        grid_spec=pltpu.PrefetchScalarGridSpec(num_scalar_prefetch=1, grid=(2 * n_own,), in_specs=[tall, tall, wide, pl.BlockSpec((1, 3 * EXT_ROWS, CB), lambda i, core: (i // 2, lax.rem(i, 2), 0))],
                                               out_specs=[pl.BlockSpec(shape, lambda i, core: (0, 0, 0))] * (2 * n_own)),
        out_shape=[jax.ShapeDtypeStruct(shape, F32)] * (2 * n_own),
        compiler_params=pltpu.CompilerParams(dimension_semantics=("arbitrary",), vmem_limit_bytes=VMEM_BYTES),
        cost_estimate=pl.CostEstimate(flops=10 ** 9, bytes_accessed=2 * 10 ** 7, transcendentals=0),
        name="send_pass",
    )(core, w_x, w_y, w_out, ext)


N_ACC = 10
ACC_ROWS = 8 * N_ACC


def second_pass_kernel(c_ref, y_ref, g_ref, q_ref, pos_ref, enter_ref, wg_ref, par_ref, *rest, n_chunk, own, batch):
    if own:
        xb_ref, xh_ref, mix_out, dpy_out, dbr_out, head_out, tail_out, acc_out, gw_out, s_a, s_A, s_i, s_m, pre, dpai, dgate, s_e = rest
    else:
        mix_out, dpy_out, dbr_out, head_out, tail_out, s_a, s_A, s_i, s_m, pre, dpai, dgate = rest
    row = lambda idx: par_ref[0, idx:idx + 1, :]
    wg = wg_ref[0].astype(BF16)
    enter = (enter_ref[0, 0], enter_ref[0, 1])
    bias_a, bias_i, slope = row(R_BA), row(R_BI), row(R_K)
    taps = [row(R_CW + k) for k in range(CONV_WIDTH)]

    def add(idx, val):
        acc_out[0, pl.ds(8 * idx, 8)] = acc_out[0, pl.ds(8 * idx, 8)] + val

    fold = lambda val: jnp.sum(val.reshape(batch // 8, 8, LANES), axis=0)
    if own:
        halo = [round16(xh_ref[0, k * batch:(k + 1) * batch] + row(R_BX)) for k in range(HALO)]
        acc_out[:] = jnp.zeros_like(acc_out)
        gw_out[:] = jnp.zeros_like(gw_out)

    def chunk_of(j):
        return c_ref[0, pl.ds(j * TC, TC)].reshape(TC * batch, LANES)

    def pre_gates(j):
        pre[:] = dot_nn(chunk_of(j), wg)

    def forward(j, hid):
        base = j * TC
        acc_y = jnp.zeros((8, LANES), F32)
        for t in range(TC):
            sl = slice(t * batch, (t + 1) * batch)
            tok = base + t
            keep = pos_ref[tok] >= 1
            conv = c_ref[0, tok].astype(F32)
            gate_r, gate_i, decay, mult, inv_m = gates(pre[sl, :LANES] + bias_a, pre[sl, LANES:] + bias_i, slope, keep)
            in_conv = gate_i * conv
            before = hid
            hid = decay * before + mult * in_conv
            d_log = decay * (before - in_conv * decay * inv_m)
            r_log = d_log * gate_r
            s_a[tok] = decay
            s_A[tok] = r_log * (1.0 - gate_r) * slope
            s_i[tok] = mult * in_conv * (1.0 - gate_i)
            s_m[tok] = mult * gate_i
            mix_out[tok] = (hid * y_ref[0, tok]).astype(BF16)
            d_pre_y = hid * q_ref[0, tok]
            dpy_out[tok] = d_pre_y.astype(BF16)
            if own:
                s_e[tok] = r_log
                acc_y = acc_y + fold(d_pre_y)
        if own:
            add(1, acc_y)
        pre_gates(jnp.minimum(j + 1, n_chunk - 1))
        return hid

    pre_gates(0)
    lax.fori_loop(0, n_chunk, forward, enter[0])

    def recur(j, carry):
        base = j * TC
        acc_a = acc_i = acc_p = jnp.zeros((8, LANES), F32)
        for t in range(TC - 1, -1, -1):
            sl = slice(t * batch, (t + 1) * batch)
            tok = base + t
            grad_h = g_ref[0, tok] + carry
            carry = s_a[tok] * grad_h
            d_pre_a = grad_h * s_A[tok]
            d_pre_i = grad_h * s_i[tok]
            s_m[tok] = grad_h * s_m[tok]
            dpai[sl, :LANES] = d_pre_a.astype(BF16)
            dpai[sl, LANES:] = d_pre_i.astype(BF16)
            if own:
                acc_a = acc_a + fold(d_pre_a)
                acc_i = acc_i + fold(d_pre_i)
                acc_p = acc_p + fold(grad_h * s_e[tok])
        if own:
            add(2, acc_a)
            add(3, acc_i)
            add(4, acc_p)
            gw_out[0] = gw_out[0] + dot_tn(chunk_of(j), dpai[:])
        return carry

    def conv_back(j, later):
        base = j * TC
        later = list(later)
        acc_x = acc_b = jnp.zeros((8, LANES), F32)
        acc_w = [jnp.zeros((8, LANES), F32) for _ in range(CONV_WIDTH)]
        for t in range(TC - 1, -1, -1):
            sl = slice(t * batch, (t + 1) * batch)
            tok = base + t
            d_conv = s_m[tok] + dgate[sl]
            total = d_conv * taps[0] + later[0]
            pos = pos_ref[tok]
            masked = [jnp.where(pos >= k, d_conv, 0.0) for k in range(1, CONV_WIDTH)]
            later = [later[1] + masked[0] * taps[1], later[2] + masked[1] * taps[2], masked[2] * taps[3]]
            dbr_out[tok] = total.astype(BF16)
            if t >= TC - HALO:
                tail_out[t - (TC - HALO)] = jnp.where(j == n_chunk - 1, total, tail_out[t - (TC - HALO)])
            if own:
                acc_x = acc_x + fold(total)
                acc_b = acc_b + fold(d_conv)
                acc_w[0] = acc_w[0] + fold(d_conv * xb_ref[0, tok].astype(F32))
                for k in range(1, CONV_WIDTH):
                    past = xb_ref[0, jnp.maximum(tok - k, 0)].astype(F32)
                    if t < k:
                        past = jnp.where(j == 0, halo[HALO + t - k], past)
                    acc_w[k] = acc_w[k] + fold(masked[k - 1] * past)
        if own:
            add(0, acc_x)
            add(5, acc_b)
            for k in range(CONV_WIDTH):
                add(6 + k, acc_w[k])
        return tuple(later)

    tail_out[:] = jnp.zeros_like(tail_out)
    zero = jnp.zeros((batch, LANES), F32)
    carry = recur(n_chunk - 1, enter[1])
    dgate[:] = dot_nt(dpai[:], wg)

    def back(idx, vals):
        carry, later = vals[0], vals[1:]
        j = n_chunk - 2 - idx
        carry = recur(j, carry)
        later = conv_back(j + 1, later)
        dgate[:] = dot_nt(dpai[:], wg)
        return (carry, *later)

    vals = lax.fori_loop(0, n_chunk - 1, back, (carry, zero, zero, zero))
    later = conv_back(0, vals[1:])
    for k in range(HALO):
        head_out[HALO - 1 - k] = later[k]


def second_pass(conv, y_act, grad_h, q_val, pos_b, enter, ext, xb=None, xb_halo=None):
    own = xb is not None
    n_blk, n_tok, batch, _ = conv.shape
    n_chunk = n_tok // TC
    per = CB // LANES
    cols = n_blk * CB
    tok_spec = pl.BlockSpec((1, n_tok, batch, LANES), lambda s: (s // per, 0, 0, lax.rem(s, per)))
    lane_spec = lambda n: pl.BlockSpec((n, batch, LANES), lambda s: (0, 0, s))
    in_specs = [tok_spec] * 4 + [pl.BlockSpec((n_tok, batch, LANES), lambda s: (0, 0, 0)),
                pl.BlockSpec((1, 2, batch, LANES), lambda s: (s // per, 0, 0, lax.rem(s, per))),
                pl.BlockSpec((1, LANES, CB), lambda s: (s // per, lax.rem(s, per), 0)),
                pl.BlockSpec((1, PAR_ROWS, LANES), lambda s: (s // per, EXT_PAR // PAR_ROWS, lax.rem(s, per)))]
    out_specs = [lane_spec(n_tok)] * 3 + [lane_spec(HALO)] * 2
    out_shape = [jax.ShapeDtypeStruct((n_tok, batch, cols), BF16)] * 3 + [jax.ShapeDtypeStruct((HALO, batch, cols), F32)] * 2
    scratch = [pltpu.VMEM((n_tok, batch, LANES), F32)] * 4 + [pltpu.VMEM((TC * batch, 2 * LANES), F32), pltpu.VMEM((TC * batch, 2 * LANES), BF16), pltpu.VMEM((TC * batch, LANES), F32)]
    args = [conv, y_act, grad_h, q_val, pos_b, enter, ext, ext]
    if own:
        in_specs += [tok_spec, pl.BlockSpec((1, HALO * batch, LANES), lambda s: (s // per, 0, lax.rem(s, per)))]
        out_specs += [pl.BlockSpec((1, ACC_ROWS, LANES), lambda s: (s, 0, 0)), pl.BlockSpec((1, LANES, 2 * LANES), lambda s: (s, 0, 0))]
        out_shape += [jax.ShapeDtypeStruct((n_blk * per, ACC_ROWS, LANES), F32), jax.ShapeDtypeStruct((n_blk * per, LANES, 2 * LANES), F32)]
        scratch.append(pltpu.VMEM((n_tok, batch, LANES), F32))
        args += [xb, xb_halo]
    n_elem = n_tok * batch * cols
    return pl.pallas_call(
        functools.partial(second_pass_kernel, n_chunk=n_chunk, own=own, batch=batch),
        grid=(n_blk * per,), in_specs=in_specs, out_specs=out_specs, scratch_shapes=scratch, out_shape=out_shape,
        compiler_params=pltpu.CompilerParams(dimension_semantics=("arbitrary",), vmem_limit_bytes=VMEM_BYTES),
        cost_estimate=pl.CostEstimate(flops=n_elem * 12000, bytes_accessed=n_elem * 20, transcendentals=n_elem * 6),
        name="second_pass_own" if own else "second_pass_far",
    )(*args)


def tile_of(j):
    return pl.ds(pl.multiple_of(j * N_TILE, N_TILE), N_TILE)


def out_kernel(*refs, n_part, n_steps, n_pass):
    mixes, refs = refs[:n_part], refs[n_part:]
    w_hbm, refs = refs[:n_part], refs[n_part:]
    pass_in, refs = refs[:n_pass], refs[n_pass:]
    x_ref, b_ref, z_ref, refs = refs[0], refs[1], refs[2], refs[3:]
    pass_out, refs = refs[:n_pass], refs[n_pass:]
    w_v, acc, sem = refs[:n_part], refs[n_part], refs[n_part + 1]
    rows = TC * B_BLK
    n_tiles = z_ref.shape[2] // N_TILE
    step = pl.program_id(0)

    def copies(j):
        tile = tile_of(j)
        first = pltpu.make_async_copy(w_hbm[0].at[:, tile], w_v[0].at[:, tile], sem.at[j, 0])
        return [first] + [pltpu.make_async_copy(w_hbm[i].at[2, tile, :], w_v[i].at[tile, :], sem.at[j, i]) for i in range(1, n_part)]

    def product(tile):
        proj = dot_nn(mixes[0][:].reshape(rows, -1), w_v[0][:, tile])
        for i in range(1, n_part):
            proj = proj + dot_nt(mixes[i][:].reshape(rows, -1), w_v[i][tile, :])
        acc[:, tile] = proj

    def finish():
        for lane in lane_tiles(z_ref.shape[2]):
            proj = turned(acc[:, lane].reshape(TC, B_BLK, LANES))
            z_ref[:, :, lane] = (x_ref[:, :, lane].astype(F32) + (proj + b_ref[:, lane])).astype(BF16)
        for src, dst in zip(pass_in, pass_out):
            dst[:] = src[:]

    @pl.when(step == 0)
    def _():
        for j in range(n_tiles):
            for copy in copies(j):
                copy.start()

        def first(j, _):
            for copy in copies(j):
                copy.wait()
            product(tile_of(j))
            return 0

        lax.fori_loop(0, n_tiles, first, 0)

    @pl.when((step > 0) & (step < n_steps))
    def _():
        finish()
        product(slice(None))

    @pl.when(step == n_steps)
    def _():
        finish()


def out_pass(mixes, w_own, w_far, x_in, b_out, sums):
    n_tok, batch, _ = mixes[0].shape
    width = x_in.shape[2]
    n_steps, _, old, act, native = row_specs(batch, n_tok)
    n_part = len(mixes)
    any_spec = pl.BlockSpec(memory_space=pl.ANY)
    strips = [pl.BlockSpec((g.shape[0] // n_steps, g.shape[1]), lambda s: (old(s), 0)) for g in sums]
    return pl.pallas_call(
        functools.partial(out_kernel, n_part=n_part, n_steps=n_steps, n_pass=len(sums)), grid=(n_steps + 1,),
        in_specs=[act(m.shape[2]) for m in mixes] + [any_spec] * n_part + strips + [native(old, width), pl.BlockSpec((1, width), lambda s: (0, 0))],
        out_specs=[native(old, width)] + strips, out_shape=[jax.ShapeDtypeStruct(a.shape, a.dtype) for a in (x_in, *sums)],
        scratch_shapes=[pltpu.VMEM(w_own.shape, BF16)] + [pltpu.VMEM(w.shape[1:], BF16) for w in w_far] + [pltpu.VMEM((TC * B_BLK, width), F32), pltpu.SemaphoreType.DMA((width // N_TILE, n_part))],
        compiler_params=pltpu.CompilerParams(dimension_semantics=("arbitrary",), vmem_limit_bytes=VMEM_BYTES),
        cost_estimate=pl.CostEstimate(flops=2 * n_tok * batch * width * width, bytes_accessed=n_tok * batch * width * 8, transcendentals=0),
        name="out_pass",
    )(*mixes, w_own, *w_far, *sums, x_in, b_out)


def norm_back_kernel(*refs, n_part, n_steps):
    n_all = 2 * n_part
    lhs, refs = refs[:n_all], refs[n_all:]
    w_hbm, refs = refs[:n_part + 1], refs[n_part + 1:]
    x_ref, inv_ref, gz_ref, s_ref, gx_ref, gs_ref, *refs = refs
    w_v, (acc, d_n, x_old, sums, scale, shift, sem) = refs[:n_all], refs[n_all:]
    rows = TC * B_BLK
    width = gx_ref.shape[2]
    n_tiles = width // N_TILE
    wide = width // 2
    step = pl.program_id(0)

    def copies(j):
        tile = tile_of(j)
        lst = []
        for k in range(2):
            for i in range(n_part):
                src = w_hbm[k].at[tile, :] if i == 0 else w_hbm[i + 1].at[k, tile, :]
                idx = k * n_part + i
                lst.append(pltpu.make_async_copy(src, w_v[idx].at[tile, :], sem.at[j, idx]))
        return lst

    def product(tile):
        val = dot_nt(lhs[0][:].reshape(rows, -1), w_v[0][tile, :])
        for arr, weight in zip(lhs[1:], w_v[1:]):
            val = val + dot_nt(arr[:].reshape(rows, -1), weight[tile, :])
        acc[:, tile] = val

    def turn(tiles):
        for lane in tiles:
            val = turned(acc[:, lane].reshape(TC, B_BLK, LANES))
            d_n[:, :, lane] = val
            x_t = x_ref[:, :, lane]
            x_old[:, :, lane] = x_t
            sums[:] += val * (1.0 + s_ref[:, lane]) * x_t.astype(F32)

    def close():
        inv = inv_ref[:]
        scale[:] = inv
        shift[:] = inv * inv * inv * (jnp.sum(sums[:], axis=-1, keepdims=True) * (1.0 / width))
        sums[:] = jnp.zeros_like(sums)

    def finish():
        for lane in lane_tiles(width):
            val, inv = d_n[:, :, lane], scale[:]
            x_f = x_old[:, :, lane].astype(F32)
            gx_ref[:, :, lane] = (gz_ref[:, :, lane].astype(F32) + (inv * (val * (1.0 + s_ref[:, lane])) - x_f * shift[:])).astype(BF16)
            gs_ref[:, lane] += jnp.sum((val * x_f * inv).reshape(-1, SUB, LANES), axis=0)

    low, high = lane_tiles(width)[:wide // LANES], lane_tiles(width)[wide // LANES:]

    @pl.when(step == 0)
    def _():
        gs_ref[:] = jnp.zeros_like(gs_ref)
        sums[:] = jnp.zeros_like(sums)
        for j in range(n_tiles):
            for copy in copies(j):
                copy.start()

        def first(j, _):
            for copy in copies(j):
                copy.wait()
            product(tile_of(j))
            return 0

        lax.fori_loop(0, n_tiles, first, 0)
        turn(low + high)
        close()

    @pl.when((step > 0) & (step < n_steps))
    def _():
        finish()
        product(slice(wide))
        turn(low)
        product(slice(wide, None))
        turn(high)
        close()

    @pl.when(step == n_steps)
    def _():
        finish()


def norm_back_pass(dbrs, dpys, wx_own, wy_own, w_far, x_in, inv_b, grad_z, scale):
    n_tok, batch, _ = dbrs[0].shape
    width = x_in.shape[2]
    n_steps, cur, old, act, native = row_specs(batch, n_tok)
    n_part = len(dbrs)
    const = lambda shape: pl.BlockSpec(shape, lambda s: (0,) * len(shape))
    planes = [pltpu.VMEM(wx_own.shape, BF16)] + [pltpu.VMEM(w.shape[1:], BF16) for w in w_far]
    block = lambda dt, lanes: pltpu.VMEM((B_BLK, TC, lanes), dt)
    return pl.pallas_call(
        functools.partial(norm_back_kernel, n_part=n_part, n_steps=n_steps), grid=(n_steps + 1,),
        in_specs=[act(m.shape[2]) for m in (*dbrs, *dpys)] + [pl.BlockSpec(memory_space=pl.ANY)] * (n_part + 1) + [native(cur, width), native(cur, LANES), native(old, width), const((1, width))],
        out_specs=[native(old, width), const((SUB, width))],
        out_shape=[jax.ShapeDtypeStruct(x_in.shape, BF16), jax.ShapeDtypeStruct((SUB, width), F32)],
        scratch_shapes=[*planes, *planes, pltpu.VMEM((TC * B_BLK, width), F32), block(F32, width), block(BF16, width), *[block(F32, LANES)] * 3, pltpu.SemaphoreType.DMA((width // N_TILE, 2 * n_part))],
        compiler_params=pltpu.CompilerParams(dimension_semantics=("arbitrary",), vmem_limit_bytes=VMEM_BYTES),
        cost_estimate=pl.CostEstimate(flops=4 * n_tok * batch * width * width, bytes_accessed=n_tok * batch * width * 10, transcendentals=0),
        name="norm_back_pass",
    )(*dbrs, *dpys, wx_own, wy_own, *w_far, x_in, inv_b, grad_z, scale)


def after(val, *deps):
    return lax.optimization_barrier((val, *deps))[0]


def entering(info, cp_index, swap_core, swap_x):
    end, prod, head = [info[:, k] for k in range(3)]
    other = lax.ppermute(info, "cp", swap_core)
    o_end, o_prod, o_head = [other[:, k] for k in range(3)]
    upper_core = cp_index % 2 == 1
    upper_chip = cp_index >= 2
    chip_end = jnp.where(upper_core, prod * o_end + end, o_prod * end + o_end)
    chip_head = jnp.where(upper_core, o_head + o_prod * head, head + prod * o_head)
    got = lax.ppermute(jnp.where(upper_chip, chip_head, chip_end), "cp", swap_x)
    from_low = jnp.where(upper_chip, got, 0.0)
    from_high = jnp.where(upper_chip, 0.0, got)
    state_in = jnp.where(upper_core, o_prod * from_low + o_end, from_low)
    grad_in = jnp.where(upper_core, from_high, o_head + o_prod * from_high)
    return jnp.stack([state_in, grad_in], axis=1)


def shard_body(x_in, grad_z, seg_pos, norm_scale, w_x, b_x, w_y, b_y, conv_w, conv_b, w_a, b_a, w_i, b_i, a_param, w_out, b_out, fwd_perm, back_perm, cp_size, tp_size):
    cp_index = lax.axis_index("cp")
    batch, n_tok, width = x_in.shape
    c_own = w_x.shape[1]
    n_own = c_own // CB
    swap_core = [(j, j ^ 1) for j in range(cp_size)]
    swap_x = [(j, j ^ 2) for j in range(cp_size)]

    slope = -8.0 * jax.nn.softplus(a_param)
    rows = [b_x, b_y, conv_b, b_a, b_i, slope, *[conv_w[k] for k in range(CONV_WIDTH)]]
    par = jnp.stack([r.astype(F32) for r in rows] + [jnp.zeros_like(slope)] * (PAR_ROWS - len(rows)))
    par = par.reshape(PAR_ROWS, n_own, CB).transpose(1, 0, 2)
    wg = jnp.concatenate([w_a, w_i], axis=-1).astype(F32).reshape(n_own, EXT_PAR, CB)
    ext = jnp.concatenate([wg, par, jnp.zeros((n_own, 6 * EXT_ROWS - EXT_PAR - PAR_ROWS, CB), F32)], axis=1)

    core = jnp.full((1,), cp_index % 2, jnp.int32)
    mine = send_pass(core, w_x, w_y, w_out, ext)
    to_y, to_z = [[(k, k ^ m) for k in range(tp_size)] for m in (1, 2)]
    got = {}
    for p in range(n_own):
        for u in range(2):
            got["y", p, u] = lax.ppermute(mine[2 * p + u], "tp", to_y)
            got["z", p, u] = lax.ppermute(mine[2 * p + u], "tp", to_z)
    for p in range(n_own):
        got["d", p, 0] = lax.ppermute(got["y", p, 0], "tp", to_z)
        got["d", p, 1] = lax.ppermute(got["z", p, 1], "tp", to_y)

    def blocks(keys):
        lst = []
        for way, p in keys:
            pair = [got[way, p, u] for u in range(2)]
            lst += pair
            for arr in pair:
                lst.append(lax.ppermute(arr, "cp", swap_core))
        return lst

    normed, gz_t, inv_b, gb_part = pre_pass(after(x_in, *mine), grad_z, norm_scale.astype(F32).reshape(1, width))
    n_halo = lax.ppermute(normed[n_tok - HALO:].astype(F32), "cp", fwd_perm).reshape(HALO * batch, width)
    normed = normed.reshape(n_tok * batch, width)
    gz_t = gz_t.reshape(n_tok * batch, width)
    pos_b = jnp.broadcast_to(seg_pos.T[:, :, None], (n_tok, batch, LANES))
    flat = lambda arr: arr.reshape(n_tok * batch, -1)

    c_o, y_o, g_o, q_o, info_o, xb_o, xh_o = first_pass(n_own, normed, gz_t, n_halo, pos_b, [w_x, w_y, w_out], ext)
    enter_o = entering(info_o, cp_index, swap_core, swap_x)
    mix_o, dpy_o, dbr_o, head_o, tail_o, acc, g_gate = second_pass(c_o, y_o, g_o, q_o, pos_b, enter_o, ext, xb_o, xh_o)
    back_o = lax.ppermute(head_o, "cp", back_perm)
    dbr_o = dbr_o.at[n_tok - HALO:].set((tail_o + back_o).astype(BF16))
    g_w_out = dot_tn(flat(mix_o), gz_t)
    g_w_y = dot_tn(normed, flat(dpy_o))
    g_w_x = dot_tn(after(normed, g_w_y, g_w_out), flat(dbr_o))

    calls = [[("y", 0), ("z", 0), ("y", 1)], [("z", 1), ("y", 2), ("z", 2)], [("d", 0), ("d", 1), ("d", 2)]]
    mixes, dpys, dbrs, w_far = [mix_o], [dpy_o], [dbr_o], []
    firsts = {}
    last = g_w_x
    for kind, idx in (("first", 0), ("second", 0), ("first", 1), ("first", 2), ("second", 1), ("second", 2)):
        if kind == "first":
            rows_n = after(normed, last)
            arrays = blocks(calls[idx])
            *acts, last, ext_f, w16 = first_pass(len(calls[idx]), rows_n, gz_t, n_halo, pos_b, arrays)
            firsts[idx] = acts, entering(last, cp_index, swap_core, swap_x), ext_f
            w_far.append(w16)
            continue
        (conv, *acts), enter_f, ext_f = firsts[idx]
        conv = after(conv, last)
        last, dpy_f, dbr_f, head_f, tail_f = second_pass(conv, *acts, pos_b, enter_f, ext_f)
        back_f = lax.ppermute(head_f, "cp", back_perm)
        dbr_f = dbr_f.at[n_tok - HALO:].set((tail_f + back_f).astype(BF16))
        for lst, val in zip((mixes, dpys, dbrs), (last, dpy_f, dbr_f)):
            lst.append(val)
    grad_x, gs_part = norm_back_pass(dbrs, dpys, w_x, w_y, w_far, x_in, inv_b, grad_z, norm_scale.astype(F32).reshape(1, width))
    acc = acc.reshape(c_own // LANES, N_ACC, 8, LANES).sum(axis=2).transpose(1, 0, 2).reshape(N_ACC, c_own)
    g_b_x = acc[:1] + jnp.sum(back_o, axis=(0, 1))
    g_a_param = -8.0 * jax.nn.sigmoid(a_param) * acc[4:5]
    g_b_out = jnp.sum(gb_part, axis=0).reshape(-1, c_own)
    smalls = jnp.concatenate([g_b_x, acc[1:4], g_a_param, acc[5:], g_b_out])
    n_small = smalls.shape[0]
    packed = jnp.concatenate([g_gate.reshape(-1, CB), jnp.pad(smalls, ((0, PAR_ROWS - n_small), (0, 0))).reshape(-1, CB)])
    g_w_x, g_w_y, g_w_out, packed = lax.psum((g_w_x, g_w_y, g_w_out, packed), "cp")
    g_gate = packed[:c_own].reshape(g_gate.shape)
    g_w_a, g_w_i = g_gate[:, :, :LANES], g_gate[:, :, LANES:]
    smalls = packed[c_own:].reshape(PAR_ROWS, c_own)
    g_b_x, g_b_y, g_b_a, g_b_i, g_a_param, g_conv_b = [smalls[k] for k in range(6)]
    g_conv_w, g_b_out = smalls[6:6 + CONV_WIDTH], smalls[6 + CONV_WIDTH:n_small].reshape(-1)
    g_scale = jnp.sum(gs_part, axis=0)
    g_scale = g_scale + sum(lax.ppermute(g_scale, "cp", [(j, j ^ m) for j in range(cp_size)]) for m in range(1, cp_size))
    mixes[0] = after(mixes[0], gs_part)
    z_out, g_w_x, g_w_y, g_w_out = out_pass(mixes, w_out, w_far, x_in, b_out.astype(F32).reshape(1, width), (g_w_x, g_w_y, g_w_out))
    return (z_out, grad_x, g_scale, g_w_x, g_b_x, g_w_y, g_b_y, g_conv_w, g_conv_b, g_w_a, g_b_a, g_w_i, g_b_i, g_a_param, g_w_out, g_b_out)


def solution(mesh):
    cp_size = mesh.shape["cp"]
    fwd_perm = [(j, j + 1) for j in range(cp_size - 1)]
    back_perm = [(j + 1, j) for j in range(cp_size - 1)]

    def per_device(*args):
        return shard_body(*args, fwd_perm=fwd_perm, back_perm=back_perm, cp_size=cp_size, tp_size=mesh.shape["tp"])

    return jax.shard_map(per_device, mesh=mesh, in_specs=IN_SPECS, out_specs=OUT_SPECS, check_vma=False)
```

time: 1440 us -> 1490 us (1.035)
  waiting for transfers between devices: 95.8 us -> 341 us
  other arithmetic: 216 us -> 27.1 us
  local copies, waits for them, and re-layouts: 74.3 us -> 24.3 us
  starting transfers between devices: 15.2 us -> 64.1 us
  Pallas kernels: 900 us -> 936 us
  blocking collectives: 27.1 us -> 0 us
    ppermute x0 -> x39, waiting for transfers between devices: none -> 277 us  [the longest x6 113 us: shard_body(): got['z', p, u] = lax.ppermute(mine[2 * p + u], 'tp', to_z)]
    all_gather x10 -> x0, waiting for transfers between devices: 86.6 us -> none  [spread(): return lax.all_gather(part, ('tp', 'cp')).reshape(tp_size, *arr.shape)]
    concatenate x5 -> x2, other arithmetic: 78.6 us -> 3.15 us  [the longest x1 2.11 us: shard_body(): jnp.concatenate([g_gate.reshape(-1, CB), jnp.pad(smalls, ((0, PAR_ROWS -...]
    psum x1, waiting for transfers between devices: 0.01 us -> 59.6 us  [shard_body(): lax.psum((g_w_x, g_w_y, g_w_out, packed), 'cp')]
    pallas_call x2 -> x4, Pallas kernels: 298 us -> 353 us  [the longest x1 200 us: norm_back_pass(): pl.pallas_call(functools.partial(norm_back_kernel, n_part=n_part, n_steps...]
    reduce_sum x4 -> x3, other arithmetic: 52.9 us -> 2.92 us  [the longest x1 1.01 us: shard_body(): acc.reshape(c_own // LANES, N_ACC, 8, LANES).sum(axis=2).transpose(1, 0, 2)]
    ppermute x0 -> x39, starting transfers between devices: none -> 36.2 us  [the longest x3 13.3 us: shard_body(): lax.ppermute(g_scale, 'cp', [(j, j ^ m) for j in range(cp_size)])]
    convert_element_type x2 -> x1, other arithmetic: 28.8 us -> 1.07 us  [shard_body(): jnp.concatenate([w_a, w_i], axis=-1).astype(F32).reshape(n_own, EXT_PAR, CB)]
  transfers between devices with their start and end apart: 24 -> 53, of which waited for: 3 -> 16; matrix products, arithmetic and copies ran while one was open for 25% -> 7% of each run, Pallas kernels for 63% -> 46%
where the time goes in v2:
time: 1490 us
  Pallas kernels  936 us (63%)
  waiting for transfers between devices  341 us (23%)
  matrix products  81.4 us (5%)
  starting transfers between devices  64.1 us (4%)
  other arithmetic  27.1 us (2%)
  local copies, waits for them, and re-layouts  24.3 us (2%)
    pallas_call x4, Pallas kernels, first_pass(): pl.pallas_call(functools.partial(first_pass_kernel, n_blk=n_blk, n_chunk=...  396 us
    pallas_call x1, Pallas kernels, norm_back_pass(): pl.pallas_call(functools.partial(norm_back_kernel, n_part=n_part, n_steps...  200 us
    pallas_call x4, Pallas kernels, second_pass(): pl.pallas_call(functools.partial(second_pass_kernel, n_chunk=n_chunk, own...  186 us
    ppermute x6, waiting for transfers between devices, shard_body(): got['z', p, u] = lax.ppermute(mine[2 * p + u], 'tp', to_z)  113 us
    ppermute x6, waiting for transfers between devices, shard_body(): got['y', p, u] = lax.ppermute(mine[2 * p + u], 'tp', to_y)  103 us
    pallas_call x1, Pallas kernels, out_pass(): pl.pallas_call(functools.partial(out_kernel, n_part=n_part, n_steps=n_ste...  96.9 us
    dot_general x3, matrix products, dot_tn(): lax.dot_general(lhs, rhs, (((0,), (0,)), ((), ())), preferred_element_typ...  81.4 us
    psum x1, waiting for transfers between devices, shard_body(): lax.psum((g_w_x, g_w_y, g_w_out, packed), 'cp')  59.6 us
  transfers between devices with their start and end apart: 53, of which 16 were waited for; matrix products, arithmetic and copies ran while one was open for 7% of the time, Pallas kernels for 46%

profile of v2, /device:TPU:0, one launch (start us, length us, event | category | flops | bytes accessed | tf_op | source)
XLA Modules:
  0.0 1488.1 jit_solution(3966849441130225952)
XLA Ops:
  11.4 1.3 reshape.284
  13.7 1.1 maximum_convert_fusion
  14.9 1.0 maximum_maximum_fusion.ext_ref.rest_0_.wg_ref.par_ref
  15.9 10.7 send_pass.1
  26.6 45.7 %pre_pass.1 = (bf16[128,32,3072]{2,1,0:T(8,128)(2,1)}, bf16[128,32,3072]{2,1,0:T(8,128)(2,1)}, f32[32,128,128]{2,1,0:T(8,128)}, f32[8,3072]{1,0:T(8,128)}) custom-call(bf16[32,128,3072]{2,1,0:T(8,128)(2,1)} %refs_11_.1, bf16[32,128,3072]{2,1,0:T(8,128)(2,1)} %refs_15_.1, f32[1,3072]{1,0:T(1,128)} %bitcast.199), custom_call_target="tpu_custom_call" | custom-call | flops 2516582400 | bytes 100663296 | tf_op jit(solution)/shard_map/pre_pass/pallas_call | solution.py:286
  72.3 1.2 slice_convert_fusion
  73.5 2.7 collective-permute-start
  77.0 1.6 collective-permute-done
  78.6 2.4 broadcast_in_dim.28.pos_ref
  80.9 94.8 %first_pass_own.1 = (bf16[3,128,32,256]{3,2,1,0:T(8,128)(2,1)}, f32[3,128,32,256]{3,2,1,0:T(8,128)}, f32[3,128,32,256]{3,2,1,0:T(8,128)}, f32[3,128,32,256]{3,2,...) custom-call(bf16[4096,3072]{1,0:T(8,128)(2,1)} %bitcast.202, ...), custom_call_target="tpu_custom_call" | custom-call | flops 57982058496 | bytes 50331648 | tf_op jit(solution)/shard_map/first_pass_own/pallas_call | solution.py:235
  176.7 13.3 collective-permute-start.1
  190.0 1.2 collective-permute-done.1
  191.2 1.0 select_select_fusion.3
  192.3 2.8 collective-permute-start.2
  195.1 1.6 collective-permute-start.8
  196.6 1.5 collective-permute-start.4
  199.9 52.8 %second_pass_own.1 = (bf16[128,32,768]{2,1,0:T(8,128)(2,1)}, bf16[128,32,768]{2,1,0:T(8,128)(2,1)}, bf16[128,32,768]{2,1,0:T(8,128)(2,1)}, f32[3,32,768]{2,1,0:T...) custom-call(bf16[3,128,32,256]{3,2,1,0:T(8,128)(2,1)} %get-tuple-element.148.c_ref, ...), custom_call_target="tpu_custom_call" | custom-call | flops 37748736000 | bytes 62914560 | tf_op jit(solution)/shard_map/second_pass_own/pallas_call | solution.py:484
  252.7 1.3 collective-permute-start.3
  254.1 26.7 %convolution_bitcast_fusion = f32[3072,768]{1,0:T(8,128)} fusion(bf16[128,32,3072]{2,1,0:T(8,128)(2,1)} %get-tuple-element.146, bf16[128,32,768]{2,1,0:T(8,128)(2,1)} %get-tuple-element.159.refs_4_), kind=kOutput, calls=%fused_computation | convolution fusion | flops 19327352832 | bytes 40894464 | tf_op jit(solution)/shard_map/dot_general | solution.py:43
  280.8 1.5 collective-permute-start.12
  283.4 26.8 %convolution_bitcast_fusion.1 = f32[768,3072]{1,0:T(8,128)} fusion(bf16[128,32,768]{2,1,0:T(8,128)(2,1)} %get-tuple-element.204.refs_0_, bf16[128,32,3072]{2,1,0:T(8,128)(2,1)} %get-tuple-element.147), kind=kOutput, calls=%fused_computation.1 | convolution fusion | flops 19327352832 | bytes 40894464 | tf_op jit(solution)/shard_map/dot_general | solution.py:43
  311.4 50.1 %collective-permute-done.12.rest_8_ = f32[3,816,256]{2,1,0:T(8,128)S(1)} collective-permute-done((f32[3,816,256]{2,1,0:T(8,128)}, f32[3,816,256]{2,1,0:T(8,128)S(1)}, u32[]{:S(2)}, u32[]{:S(2)}) %collective-permute-start.12) | collective-permute-done | bytes 2506784 | tf_op jit(solution)/shard_map/ppermute | solution.py:712
  361.6 52.4 %collective-permute-done.13.rest_9_ = f32[3,816,256]{2,1,0:T(8,128)} collective-permute-done((f32[3,816,256]{2,1,0:T(8,128)}, f32[3,816,256]{2,1,0:T(8,128)}, u32[]{:S(2)}, u32[]{:S(2)}) %collective-permute-start.13) | collective-permute-done | bytes 2506784 | tf_op jit(solution)/shard_map/ppermute | solution.py:712
  414.5 27.9 %fusion.10 = f32[3072,768]{1,0:T(8,128)} fusion(bf16[4096,3072]{1,0:T(8,128)(2,1)S(1)} %bitcast.208, bf16[4096,768]{1,0:T(8,128)(2,1)} %bitcast.218), kind=kOutput, calls=%fused_computation.68 | convolution fusion | flops 19327352832 | bytes 40894464 | tf_op jit(solution)/shard_map/dot_general | solution.py:43
  443.0 1.6 collective-permute-start.20
  445.0 1.5 collective-permute-start.23
  446.5 92.1 %first_pass_far.3 = (bf16[3,128,32,256]{3,2,1,0:T(8,128)(2,1)}, f32[3,128,32,256]{3,2,1,0:T(8,128)}, f32[3,128,32,256]{3,2,1,0:T(8,128)}, f32[3,128,32,256]{3,2,...) custom-call(bf16[4096,3072]{1,0:T(8,128)(2,1)} %bitcast.203, ...), custom_call_target="tpu_custom_call" | custom-call | flops 57982058496 | bytes 50331648 | tf_op jit(solution)/shard_map/first_pass_far/pallas_call | solution.py:235
  539.7 1.6 collective-permute-done.16
  541.2 1.0 select_select_fusion.2
  542.6 1.6 collective-permute-start.28
  544.2 9.6 collective-permute-done.20.rest_1_
  553.8 1.5 collective-permute-start.24
  555.3 52.2 %collective-permute-done.27.rest_8_ = f32[3,816,256]{2,1,0:T(8,128)} collective-permute-done((f32[3,816,256]{2,1,0:T(8,128)}, f32[3,816,256]{2,1,0:T(8,128)}, u32[]{:S(2)}, u32[]{:S(2)}) %collective-permute-start.27) | collective-permute-done | bytes 2506784 | tf_op jit(solution)/shard_map/ppermute | solution.py:713
  608.0 1.5 collective-permute-start.32
  610.3 51.0 %collective-permute-done.28.rest_9_ = f32[3,816,256]{2,1,0:T(8,128)} collective-permute-done((f32[3,816,256]{2,1,0:T(8,128)}, f32[3,816,256]{2,1,0:T(8,128)}, u32[]{:S(2)}, u32[]{:S(2)}) %collective-permute-start.28) | collective-permute-done | bytes 2506784 | tf_op jit(solution)/shard_map/ppermute | solution.py:713
  661.8 52.3 %collective-permute-done.31.rest_0_ = f32[3,816,256]{2,1,0:T(8,128)} collective-permute-done((f32[3,816,256]{2,1,0:T(8,128)}, f32[3,816,256]{2,1,0:T(8,128)}, u32[]{:S(2)}, u32[]{:S(2)}) %collective-permute-start.31) | collective-permute-done | bytes 2506784 | tf_op jit(solution)/shard_map/ppermute | solution.py:715
  714.6 44.4 %second_pass_far.3 = (bf16[128,32,768]{2,1,0:T(8,128)(2,1)}, bf16[128,32,768]{2,1,0:T(8,128)(2,1)}, bf16[128,32,768]{2,1,0:T(8,128)(2,1)}, f32[3,32,768]{2,1,0:T(8,128)}, f32[3,32,768]{2,1,0:T(8,128)}) custom-call(bf16[3,128,32,256]{3,2,1,0:T(8,128)(2,1)} %get-tuple-element.164.c_ref, f32[3,128,32,256]{3,2,1,0:T(8,128)} %get-tuple-element.165.y_ref, ...), custom_call_target="tpu_custom_call" | custom-call | flops 37748736000 | bytes 62914560 | tf_op jit(solution)/shard_map/second_pass_far/pallas_call | solution.py:484
  759.5 1.5 collective-permute-start.36
  761.0 1.6 collective-permute-start.39
  763.1 104.8 %first_pass_far.4 = (bf16[3,128,32,256]{3,2,1,0:T(8,128)(2,1)}, f32[3,128,32,256]{3,2,1,0:T(8,128)}, f32[3,128,32,256]{3,2,1,0:T(8,128)}, f32[3,128,32,256]{3,2,...) custom-call(bf16[4096,3072]{1,0:T(8,128)(2,1)} %bitcast.204, ...), custom_call_target="tpu_custom_call" | custom-call | flops 57982058496 | bytes 50331648 | tf_op jit(solution)/shard_map/first_pass_far/pallas_call | solution.py:235
  875.0 2.1 pad_maximum_fusion
  878.8 1.3 collective-permute-start.18
  880.1 2.7 collective-permute-start.44
  882.7 3.8 collective-permute-done.41.rest_10_
  886.5 3.6 collective-permute-done.42.rest_11_
  890.1 104.6 %first_pass_far.5 = (bf16[3,128,32,256]{3,2,1,0:T(8,128)(2,1)}, f32[3,128,32,256]{3,2,1,0:T(8,128)}, f32[3,128,32,256]{3,2,1,0:T(8,128)}, f32[3,128,32,256]{3,2,...) custom-call(bf16[4096,3072]{1,0:T(8,128)(2,1)} %bitcast.205, ...), custom_call_target="tpu_custom_call" | custom-call | flops 57982058496 | bytes 50331648 | tf_op jit(solution)/shard_map/first_pass_far/pallas_call | solution.py:235
  996.1 1.1 select_bitcast_fusion.3
  998.6 1.7 select_select_fusion
  1000.4 44.8 %second_pass_far.4 = (bf16[128,32,768]{2,1,0:T(8,128)(2,1)}, bf16[128,32,768]{2,1,0:T(8,128)(2,1)}, bf16[128,32,768]{2,1,0:T(8,128)(2,1)}, f32[3,32,768]{2,1,0:T(8,128)}, f32[3,32,768]{2,1,0:T(8,128)}) custom-call(bf16[3,128,32,256]{3,2,1,0:T(8,128)(2,1)} %get-tuple-element.178.c_ref, f32[3,128,32,256]{3,2,1,0:T(8,128)} %get-tuple-element.179.y_ref, ...), custom_call_target="tpu_custom_call" | custom-call | flops 37748736000 | bytes 62914560 | tf_op jit(solution)/shard_map/second_pass_far/pallas_call | solution.py:484
  1045.2 1.3 collective-permute-start.45
  1046.5 1.1 select_bitcast_fusion.1
  1048.3 44.4 %second_pass_far.5 = (bf16[128,32,768]{2,1,0:T(8,128)(2,1)}, bf16[128,32,768]{2,1,0:T(8,128)(2,1)}, bf16[128,32,768]{2,1,0:T(8,128)(2,1)}, f32[3,32,768]{2,1,0:T(8,128)}, f32[3,32,768]{2,1,0:T(8,128)}) custom-call(bf16[3,128,32,256]{3,2,1,0:T(8,128)(2,1)} %get-tuple-element.188.c_ref, f32[3,128,32,256]{3,2,1,0:T(8,128)} %get-tuple-element.189.y_ref, ...), custom_call_target="tpu_custom_call" | custom-call | flops 37748736000 | bytes 62914560 | tf_op jit(solution)/shard_map/second_pass_far/pallas_call | solution.py:484
  1092.7 1.3 collective-permute-start.48
  1094.0 1.7 fusion.1.refs_1_
  1095.7 1.8 fusion.2.refs_2_
  1097.5 1.7 fusion.3.refs_3_
  1099.2 199.5 %norm_back_pass.1 = (bf16[32,128,3072]{2,1,0:T(8,128)(2,1)}, f32[8,3072]{1,0:T(8,128)}) custom-call(bf16[128,32,768]{2,1,0:T(8,128)(2,1)} %fusion.refs_0_, bf16[128,32,768]{2,1,0:T(8,128)(2,1)} %fusion.1.refs_1_, bf16[128,32,768]{2,1,0:T(8,128)(2,1)} %fusion.2.refs_2_, bf16[128,32,768]{2,1,0:T(8,128)(2,1)} %fusion.3.refs_3_, ...), custom_call_target="tpu_custom_call" | custom-call | flops 154618822656 | bytes 125829120 | tf_op jit(solution)/shard_map/norm_back_pass/pallas_call | solution.py:659
  1299.6 3.8 collective-permute-start.51
  1303.4 9.5 collective-permute-start.50
  1312.9 1.3 reshape.286
  1314.2 1.1 collective-permute-done.50
  1316.0 59.6 %all-reduce.4.cloned.1.call-done = (f32[3072,768]{1,0:T(8,128)}, f32[3072,768]{1,0:T(8,128)}, f32[768,3072]{1,0:T(8,128)}, f32[816,256]{1,0:T(8,128)}) async-done(((f32[3072,768]{1,0:T(8,128)}, f32[3072,768]{1,0:T(8,128)}, f32[768,3072]{1,0:T(8,128)}, f32[816,256]{1,0:T(8,128)}), (f32[3072,768]{1,0:T(8,128)}, f32[3072,768]{1,0:T(8,128)}, f32[768,3072]{1,0:T(8,128)}, ...) | async-done | bytes 29147152 | tf_op jit(solution)/shard_map/psum | solution.py:770
  1377.2 1.2 slice.332
  1384.2 96.9 %out_pass.1 = (bf16[32,128,3072]{2,1,0:T(8,128)(2,1)}, f32[3072,768]{1,0:T(8,128)}, f32[3072,768]{1,0:T(8,128)}, f32[768,3072]{1,0:T(8,128)}) custom-call(bf16[128,32,768]{2,1,0:T(8,128)(2,1)} %get-tuple-element.204.refs_0_, bf16[128,32,768]{2,1,0:T(8,128)(2,1)} %get-tuple-element.172.refs_1_, bf16[128,32,768]{2,1,0:T(8,128)(2,1)} %get-tuple-element.187.refs_2_, ...), custom_call_target="tpu_custom_call" | custom-call | flops 77309411328 | bytes 100663296 | tf_op jit(solution)/shard_map/out_pass/pallas_call | solution.py:557
  (156 shorter events, 38.4 us)
Async XLA Ops:
  7.2 1368.3 %all-reduce.4.cloned.1.call-start = ((), (), s32[]{:S(2)}) async-start(), calls=%async_computation | async-start | bytes 58294272 | tf_op jit(solution)/shard_map/psum | solution.py:770
  73.5 5.1 collective-permute-start
  78.6 2.4 copy-start.6
  176.7 14.5 collective-permute-start.1
  192.3 6.8 collective-permute-start.2
  195.1 87.3 %collective-permute-start.8 = (f32[3,816,256]{2,1,0:T(8,128)}, f32[3,816,256]{2,1,0:T(8,128)}, u32[]{:S(2)}, u32[]{:S(2)}) collective-permute-start(f32[3,816,256]{2,1,0:T(8,128)} %get-tuple-element.139), channel_id=1, source_target_pairs={{0,8},{4,12},{8,0},{12,4},{1,9},{5,13},{9,1},{13,5},{2,10},{6,14},... | collective-permute-start | bytes 7520264 | tf_op jit(solution)/shard_map/ppermute | solution.py:713
  196.6 86.2 %collective-permute-start.4 = (f32[3,816,256]{2,1,0:T(8,128)}, f32[3,816,256]{2,1,0:T(8,128)}, u32[]{:S(2)}, u32[]{:S(2)}) collective-permute-start(f32[3,816,256]{2,1,0:T(8,128)} %get-tuple-element.139), channel_id=1, source_target_pairs={{0,4},{4,0},{8,12},{12,8},{1,5},{5,1},{9,13},{13,9},{2,6},{6,2},{1... | collective-permute-start | bytes 7520264 | tf_op jit(solution)/shard_map/ppermute | solution.py:712
  198.1 112.7 %collective-permute-start.9 = (f32[3,816,256]{2,1,0:T(8,128)}, f32[3,816,256]{2,1,0:T(8,128)}, u32[]{:S(2)}, u32[]{:S(2)}) collective-permute-start(f32[3,816,256]{2,1,0:T(8,128)} %get-tuple-element.140), channel_id=1, source_target_pairs={{0,8},{4,12},{8,0},{12,4},{1,9},{5,13},{9,1},{13,5},{2,10},{6,14},... | collective-permute-start | bytes 7520264 | tf_op jit(solution)/shard_map/ppermute | solution.py:713
  198.6 112.3 %collective-permute-start.5 = (f32[3,816,256]{2,1,0:T(8,128)}, f32[3,816,256]{2,1,0:T(8,128)}, u32[]{:S(2)}, u32[]{:S(2)}) collective-permute-start(f32[3,816,256]{2,1,0:T(8,128)} %get-tuple-element.140), channel_id=1, source_target_pairs={{0,4},{4,0},{8,12},{12,8},{1,5},{5,1},{9,13},{13,9},{2,6},{6,2},{1... | collective-permute-start | bytes 7520264 | tf_op jit(solution)/shard_map/ppermute | solution.py:712
  252.7 28.1 %collective-permute-start.3 = (f32[3,32,768]{2,1,0:T(8,128)}, f32[3,32,768]{2,1,0:T(8,128)S(1)}, u32[]{:S(2)}, u32[]{:S(2)}) collective-permute-start(f32[3,32,768]{2,1,0:T(8,128)} %get-tuple-element.158), channel_id=1, source_target_pairs={{1,0},{2,1},{3,2},{5,4},{6,5},{7,6},{9,8},{10,9},{11,10},{13,12},{... | collective-permute-start | bytes 884744 | tf_op jit(solution)/shard_map/ppermute | solution.py:737
  254.0 160.5 %slice-start = ((s8[25165824]{0:T(1024)(128)(4,1)}), s8[4194304]{0:T(1024)(128)(4,1)S(1)}, s32[]{:S(2)}) async-start(s8[25165824]{0:T(1024)(128)(4,1)} %bitcast.206), calls=%async_computation.1 | async-start | bytes 8388608
  254.0 160.5 %slice-start.1 = ((s8[25165824]{0:T(1024)(128)(4,1)}), s8[4194304]{0:T(1024)(128)(4,1)S(1)}, s32[]{:S(2)}) async-start(s8[25165824]{0:T(1024)(128)(4,1)} %bitcast.206), calls=%async_computation.2 | async-start | bytes 8388608
  254.1 160.4 %slice-start.2 = ((s8[25165824]{0:T(1024)(128)(4,1)}), s8[4194304]{0:T(1024)(128)(4,1)S(1)}, s32[]{:S(2)}) async-start(s8[25165824]{0:T(1024)(128)(4,1)} %bitcast.206), calls=%async_computation.3 | async-start | bytes 8388608
  280.8 29.4 %copy-start.3 = (f32[3,32,768]{2,1,0:T(8,128)}, f32[3,32,768]{2,1,0:T(8,128)S(1)}, u32[]{:S(2)}) copy-start(f32[3,32,768]{2,1,0:T(8,128)S(1)} %collective-permute-done.3) | copy-start | bytes 884740
  280.8 80.7 %collective-permute-start.12 = (f32[3,816,256]{2,1,0:T(8,128)}, f32[3,816,256]{2,1,0:T(8,128)S(1)}, u32[]{:S(2)}, u32[]{:S(2)}) collective-permute-start(f32[3,816,256]{2,1,0:T(8,128)} %get-tuple-element.141), channel_id=1, source_target_pairs={{0,4},{4,0},{8,12},{12,8},{1,5},{5,1},{9,13},{13,9},{2,6},{6,2},{1... | collective-permute-start | bytes 7520264 | tf_op jit(solution)/shard_map/ppermute | solution.py:712
  282.3 131.6 %collective-permute-start.13 = (f32[3,816,256]{2,1,0:T(8,128)}, f32[3,816,256]{2,1,0:T(8,128)}, u32[]{:S(2)}, u32[]{:S(2)}) collective-permute-start(f32[3,816,256]{2,1,0:T(8,128)} %get-tuple-element.142), channel_id=1, source_target_pairs={{0,4},{4,0},{8,12},{12,8},{1,5},{5,1},{9,13},{13,9},{2,6},{6,2},{1... | collective-permute-start | bytes 7520264 | tf_op jit(solution)/shard_map/ppermute | solution.py:712
  282.9 131.1 %collective-permute-start.10 = (f32[3,816,256]{2,1,0:T(8,128)}, f32[3,816,256]{2,1,0:T(8,128)}, u32[]{:S(2)}, u32[]{:S(2)}) collective-permute-start(f32[3,816,256]{2,1,0:T(8,128)} %collective-permute-done.8.rest_4_), channel_id=1, source_target_pairs={{0,1},{1,0},{2,3},{3,2},{4,5},{5,4},{6,7},{7,6},{8,9},{9,8},{10,11... | collective-permute-start | bytes 7520264 | tf_op jit(solution)/shard_map/ppermute | solution.py:724
  283.4 26.8 %copy-start.4 = (f32[3,32,768]{2,1,0:T(8,128)S(1)}, f32[3,32,768]{2,1,0:T(8,128)}, u32[]{:S(2)}) copy-start(f32[3,32,768]{2,1,0:T(8,128)} %get-tuple-element.157) | copy-start | bytes 884740
  283.4 131.1 %slice-start.3 = ((s8[25165824]{0:T(1024)(128)(4,1)}), s8[4194304]{0:T(1024)(128)(4,1)S(1)}, s32[]{:S(2)}) async-start(s8[25165824]{0:T(1024)(128)(4,1)} %bitcast.206), calls=%async_computation.4 | async-start | bytes 8388608
  283.4 131.1 %slice-start.4 = ((s8[25165824]{0:T(1024)(128)(4,1)}), s8[4194304]{0:T(1024)(128)(4,1)S(1)}, s32[]{:S(2)}) async-start(s8[25165824]{0:T(1024)(128)(4,1)} %bitcast.206), calls=%async_computation.5 | async-start | bytes 8388608
  283.4 131.1 %slice-start.5 = ((s8[25165824]{0:T(1024)(128)(4,1)}), s8[4194304]{0:T(1024)(128)(4,1)S(1)}, s32[]{:S(2)}) async-start(s8[25165824]{0:T(1024)(128)(4,1)} %bitcast.206), calls=%async_computation.6 | async-start | bytes 8388608
  310.9 131.6 %collective-permute-start.6 = (f32[3,816,256]{2,1,0:T(8,128)}, f32[3,816,256]{2,1,0:T(8,128)}, u32[]{:S(2)}, u32[]{:S(2)}) collective-permute-start(f32[3,816,256]{2,1,0:T(8,128)} %collective-permute-done.4.rest_0_), channel_id=1, source_target_pairs={{0,1},{1,0},{2,3},{3,2},{4,5},{5,4},{6,7},{7,6},{8,9},{9,8},{10,11... | collective-permute-start | bytes 7520264 | tf_op jit(solution)/shard_map/ppermute | solution.py:724
  310.9 132.0 %collective-permute-start.11 = (f32[3,816,256]{2,1,0:T(8,128)}, f32[3,816,256]{2,1,0:T(8,128)}, u32[]{:S(2)}, u32[]{:S(2)}) collective-permute-start(f32[3,816,256]{2,1,0:T(8,128)} %collective-permute-done.9.rest_5_), channel_id=1, source_target_pairs={{0,1},{1,0},{2,3},{3,2},{4,5},{5,4},{6,7},{7,6},{8,9},{9,8},{10,11... | collective-permute-start | bytes 7520264 | tf_op jit(solution)/shard_map/ppermute | solution.py:724
  361.6 80.9 %copy-start.5 = (f32[3,816,256]{2,1,0:T(8,128)}, f32[3,816,256]{2,1,0:T(8,128)S(1)}, u32[]{:S(2)}) copy-start(f32[3,816,256]{2,1,0:T(8,128)S(1)} %collective-permute-done.12.rest_8_) | copy-start | bytes 7520260
  361.6 83.0 %collective-permute-start.7 = (f32[3,816,256]{2,1,0:T(8,128)}, f32[3,816,256]{2,1,0:T(8,128)}, u32[]{:S(2)}, u32[]{:S(2)}) collective-permute-start(f32[3,816,256]{2,1,0:T(8,128)} %collective-permute-done.5.rest_1_), channel_id=1, source_target_pairs={{0,1},{1,0},{2,3},{3,2},{4,5},{5,4},{6,7},{7,6},{8,9},{9,8},{10,11... | collective-permute-start | bytes 7520264 | tf_op jit(solution)/shard_map/ppermute | solution.py:724
  414.0 31.0 %collective-permute-start.14 = (f32[3,816,256]{2,1,0:T(8,128)S(1)}, f32[3,816,256]{2,1,0:T(8,128)}, u32[]{:S(2)}, u32[]{:S(2)}) collective-permute-start(f32[3,816,256]{2,1,0:T(8,128)S(1)} %collective-permute-done.12.rest_8_), channel_id=1, source_target_pairs={{0,1},{1,0},{2,3},{3,2},{4,5},{5,4},{6,7},{7,6},{8,9},{9,8},{10,11... | collective-permute-start | bytes 7520264 | tf_op jit(solution)/shard_map/ppermute | solution.py:724
  414.0 32.5 %collective-permute-start.15 = (f32[3,816,256]{2,1,0:T(8,128)}, f32[3,816,256]{2,1,0:T(8,128)}, u32[]{:S(2)}, u32[]{:S(2)}) collective-permute-start(f32[3,816,256]{2,1,0:T(8,128)} %collective-permute-done.13.rest_9_), channel_id=1, source_target_pairs={{0,1},{1,0},{2,3},{3,2},{4,5},{5,4},{6,7},{7,6},{8,9},{9,8},{10,11... | collective-permute-start | bytes 7520264 | tf_op jit(solution)/shard_map/ppermute | solution.py:724
  442.5 100.1 %collective-permute-start.19 = (f32[3,816,256]{2,1,0:T(8,128)}, f32[3,816,256]{2,1,0:T(8,128)}, u32[]{:S(2)}, u32[]{:S(2)}) collective-permute-start(f32[3,816,256]{2,1,0:T(8,128)} %get-tuple-element.141), channel_id=1, source_target_pairs={{0,8},{4,12},{8,0},{12,4},{1,9},{5,13},{9,1},{13,5},{2,10},{6,14},... | collective-permute-start | bytes 7520264 | tf_op jit(solution)/shard_map/ppermute | solution.py:713
  443.0 110.9 %collective-permute-start.20 = (f32[3,816,256]{2,1,0:T(8,128)}, f32[3,816,256]{2,1,0:T(8,128)}, u32[]{:S(2)}, u32[]{:S(2)}) collective-permute-start(f32[3,816,256]{2,1,0:T(8,128)} %get-tuple-element.142), channel_id=1, source_target_pairs={{0,8},{4,12},{8,0},{12,4},{1,9},{5,13},{9,1},{13,5},{2,10},{6,14},... | collective-permute-start | bytes 7520264 | tf_op jit(solution)/shard_map/ppermute | solution.py:713
  444.5 163.0 %collective-permute-start.27 = (f32[3,816,256]{2,1,0:T(8,128)}, f32[3,816,256]{2,1,0:T(8,128)}, u32[]{:S(2)}, u32[]{:S(2)}) collective-permute-start(f32[3,816,256]{2,1,0:T(8,128)} %get-tuple-element.143), channel_id=1, source_target_pairs={{0,8},{4,12},{8,0},{12,4},{1,9},{5,13},{9,1},{13,5},{2,10},{6,14},... | collective-permute-start | bytes 7520264 | tf_op jit(solution)/shard_map/ppermute | solution.py:713
  445.0 163.0 %collective-permute-start.23 = (f32[3,816,256]{2,1,0:T(8,128)}, f32[3,816,256]{2,1,0:T(8,128)}, u32[]{:S(2)}, u32[]{:S(2)}) collective-permute-start(f32[3,816,256]{2,1,0:T(8,128)} %get-tuple-element.143), channel_id=1, source_target_pairs={{0,4},{4,0},{8,12},{12,8},{1,5},{5,1},{9,13},{13,9},{2,6},{6,2},{1... | collective-permute-start | bytes 7520264 | tf_op jit(solution)/shard_map/ppermute | solution.py:712
  539.6 1.6 collective-permute-start.16
  542.3 67.2 %collective-permute-start.17 = (f32[3,32,256]{2,1,0:T(8,128)S(1)}, f32[3,32,256]{2,1,0:T(8,128)S(1)}, u32[]{:S(2)}, u32[]{:S(2)}) collective-permute-start(f32[3,32,256]{2,1,0:T(8,128)S(1)} %select_select_fusion.2), channel_id=1, source_target_pairs={{0,2},{1,3},{2,0},{3,1},{4,6},{5,7},{6,4},{7,5},{8,10},{9,11},{10,... | collective-permute-start | bytes 294920 | tf_op jit(solution)/shard_map/ppermute | solution.py:683
  542.6 118.6 %collective-permute-start.28 = (f32[3,816,256]{2,1,0:T(8,128)}, f32[3,816,256]{2,1,0:T(8,128)}, u32[]{:S(2)}, u32[]{:S(2)}) collective-permute-start(f32[3,816,256]{2,1,0:T(8,128)} %get-tuple-element.144), channel_id=1, source_target_pairs={{0,8},{4,12},{8,0},{12,4},{1,9},{5,13},{9,1},{13,5},{2,10},{6,14},... | collective-permute-start | bytes 7520264 | tf_op jit(solution)/shard_map/ppermute | solution.py:713
  553.8 107.4 %collective-permute-start.24 = (f32[3,816,256]{2,1,0:T(8,128)}, f32[3,816,256]{2,1,0:T(8,128)}, u32[]{:S(2)}, u32[]{:S(2)}) collective-permute-start(f32[3,816,256]{2,1,0:T(8,128)} %get-tuple-element.144), channel_id=1, source_target_pairs={{0,4},{4,0},{8,12},{12,8},{1,5},{5,1},{9,13},{13,9},{2,6},{6,2},{1... | collective-permute-start | bytes 7520264 | tf_op jit(solution)/shard_map/ppermute | solution.py:712
  607.5 106.5 %collective-permute-start.31 = (f32[3,816,256]{2,1,0:T(8,128)}, f32[3,816,256]{2,1,0:T(8,128)}, u32[]{:S(2)}, u32[]{:S(2)}) collective-permute-start(f32[3,816,256]{2,1,0:T(8,128)} %collective-permute-done.4.rest_0_), channel_id=1, source_target_pairs={{0,8},{4,12},{8,0},{12,4},{1,9},{5,13},{9,1},{13,5},{2,10},{6,14},... | collective-permute-start | bytes 7520264 | tf_op jit(solution)/shard_map/ppermute | solution.py:715
  608.0 106.0 %collective-permute-start.32 = (f32[3,816,256]{2,1,0:T(8,128)}, f32[3,816,256]{2,1,0:T(8,128)}, u32[]{:S(2)}, u32[]{:S(2)}) collective-permute-start(f32[3,816,256]{2,1,0:T(8,128)} %collective-permute-done.9.rest_5_), channel_id=1, source_target_pairs={{0,4},{4,0},{8,12},{12,8},{1,5},{5,1},{9,13},{13,9},{2,6},{6,2},{1... | collective-permute-start | bytes 7520264 | tf_op jit(solution)/shard_map/ppermute | solution.py:716
  609.5 105.0 %collective-permute-start.21 = (f32[3,816,256]{2,1,0:T(8,128)}, f32[3,816,256]{2,1,0:T(8,128)}, u32[]{:S(2)}, u32[]{:S(2)}) collective-permute-start(f32[3,816,256]{2,1,0:T(8,128)} %collective-permute-done.19.rest_0_), channel_id=1, source_target_pairs={{0,1},{1,0},{2,3},{3,2},{4,5},{5,4},{6,7},{7,6},{8,9},{9,8},{10,11... | collective-permute-start | bytes 7520264 | tf_op jit(solution)/shard_map/ppermute | solution.py:724
  661.2 97.7 %collective-permute-start.22 = (f32[3,816,256]{2,1,0:T(8,128)}, f32[3,816,256]{2,1,0:T(8,128)}, u32[]{:S(2)}, u32[]{:S(2)}) collective-permute-start(f32[3,816,256]{2,1,0:T(8,128)} %collective-permute-done.20.rest_1_), channel_id=1, source_target_pairs={{0,1},{1,0},{2,3},{3,2},{4,5},{5,4},{6,7},{7,6},{8,9},{9,8},{10,11... | collective-permute-start | bytes 7520264 | tf_op jit(solution)/shard_map/ppermute | solution.py:724
  661.3 98.2 %collective-permute-start.29 = (f32[3,816,256]{2,1,0:T(8,128)}, f32[3,816,256]{2,1,0:T(8,128)}, u32[]{:S(2)}, u32[]{:S(2)}) collective-permute-start(f32[3,816,256]{2,1,0:T(8,128)} %collective-permute-done.27.rest_8_), channel_id=1, source_target_pairs={{0,1},{1,0},{2,3},{3,2},{4,5},{5,4},{6,7},{7,6},{8,9},{9,8},{10,11... | collective-permute-start | bytes 7520264 | tf_op jit(solution)/shard_map/ppermute | solution.py:724
  714.0 47.0 %collective-permute-start.25 = (f32[3,816,256]{2,1,0:T(8,128)}, f32[3,816,256]{2,1,0:T(8,128)}, u32[]{:S(2)}, u32[]{:S(2)}) collective-permute-start(f32[3,816,256]{2,1,0:T(8,128)} %collective-permute-done.23.rest_4_), channel_id=1, source_target_pairs={{0,1},{1,0},{2,3},{3,2},{4,5},{5,4},{6,7},{7,6},{8,9},{9,8},{10,11... | collective-permute-start | bytes 7520264 | tf_op jit(solution)/shard_map/ppermute | solution.py:724
  714.0 48.6 %collective-permute-start.30 = (f32[3,816,256]{2,1,0:T(8,128)}, f32[3,816,256]{2,1,0:T(8,128)}, u32[]{:S(2)}, u32[]{:S(2)}) collective-permute-start(f32[3,816,256]{2,1,0:T(8,128)} %collective-permute-done.28.rest_9_), channel_id=1, source_target_pairs={{0,1},{1,0},{2,3},{3,2},{4,5},{5,4},{6,7},{7,6},{8,9},{9,8},{10,11... | collective-permute-start | bytes 7520264 | tf_op jit(solution)/shard_map/ppermute | solution.py:724
  714.5 48.6 %collective-permute-start.26 = (f32[3,816,256]{2,1,0:T(8,128)}, f32[3,816,256]{2,1,0:T(8,128)}, u32[]{:S(2)}, u32[]{:S(2)}) collective-permute-start(f32[3,816,256]{2,1,0:T(8,128)} %collective-permute-done.24.rest_5_), channel_id=1, source_target_pairs={{0,1},{1,0},{2,3},{3,2},{4,5},{5,4},{6,7},{7,6},{8,9},{9,8},{10,11... | collective-permute-start | bytes 7520264 | tf_op jit(solution)/shard_map/ppermute | solution.py:724
  759.0 109.9 %collective-permute-start.35 = (f32[3,816,256]{2,1,0:T(8,128)}, f32[3,816,256]{2,1,0:T(8,128)}, u32[]{:S(2)}, u32[]{:S(2)}) collective-permute-start(f32[3,816,256]{2,1,0:T(8,128)} %copy-done.5), channel_id=1, source_target_pairs={{0,8},{4,12},{8,0},{12,4},{1,9},{5,13},{9,1},{13,5},{2,10},{6,14},... | collective-permute-start | bytes 7520264 | tf_op jit(solution)/shard_map/ppermute | solution.py:715
  759.5 109.9 %collective-permute-start.36 = (f32[3,816,256]{2,1,0:T(8,128)}, f32[3,816,256]{2,1,0:T(8,128)}, u32[]{:S(2)}, u32[]{:S(2)}) collective-permute-start(f32[3,816,256]{2,1,0:T(8,128)} %collective-permute-done.20.rest_1_), channel_id=1, source_target_pairs={{0,4},{4,0},{8,12},{12,8},{1,5},{5,1},{9,13},{13,9},{2,6},{6,2},{1... | collective-permute-start | bytes 7520264 | tf_op jit(solution)/shard_map/ppermute | solution.py:716
  761.0 108.8 %collective-permute-start.39 = (f32[3,816,256]{2,1,0:T(8,128)}, f32[3,816,256]{2,1,0:T(8,128)}, u32[]{:S(2)}, u32[]{:S(2)}) collective-permute-start(f32[3,816,256]{2,1,0:T(8,128)} %collective-permute-done.23.rest_4_), channel_id=1, source_target_pairs={{0,8},{4,12},{8,0},{12,4},{1,9},{5,13},{9,1},{13,5},{2,10},{6,14},... | collective-permute-start | bytes 7520264 | tf_op jit(solution)/shard_map/ppermute | solution.py:715
  762.6 107.4 %collective-permute-start.40 = (f32[3,816,256]{2,1,0:T(8,128)}, f32[3,816,256]{2,1,0:T(8,128)}, u32[]{:S(2)}, u32[]{:S(2)}) collective-permute-start(f32[3,816,256]{2,1,0:T(8,128)} %collective-permute-done.28.rest_9_), channel_id=1, source_target_pairs={{0,4},{4,0},{8,12},{12,8},{1,5},{5,1},{9,13},{13,9},{2,6},{6,2},{1... | collective-permute-start | bytes 7520264 | tf_op jit(solution)/shard_map/ppermute | solution.py:716
  763.1 107.8 %collective-permute-start.33 = (f32[3,816,256]{2,1,0:T(8,128)}, f32[3,816,256]{2,1,0:T(8,128)}, u32[]{:S(2)}, u32[]{:S(2)}) collective-permute-start(f32[3,816,256]{2,1,0:T(8,128)} %collective-permute-done.31.rest_0_), channel_id=1, source_target_pairs={{0,1},{1,0},{2,3},{3,2},{4,5},{5,4},{6,7},{7,6},{8,9},{9,8},{10,11... | collective-permute-start | bytes 7520264 | tf_op jit(solution)/shard_map/ppermute | solution.py:724
  868.9 1.6 collective-permute-start.43
  869.4 9.4 collective-permute-start.34
  869.8 10.2 collective-permute-start.37
  870.0 12.7 collective-permute-start.38
  870.6 6.6 copy-start
  870.6 15.9 %collective-permute-start.41 = (f32[3,816,256]{2,1,0:T(8,128)}, f32[3,816,256]{2,1,0:T(8,128)}, u32[]{:S(2)}, u32[]{:S(2)}) collective-permute-start(f32[3,816,256]{2,1,0:T(8,128)} %collective-permute-done.39.rest_8_), channel_id=1, source_target_pairs={{0,1},{1,0},{2,3},{3,2},{4,5},{5,4},{6,7},{7,6},{8,9},{9,8},{10,11... | collective-permute-start | bytes 7520264 | tf_op jit(solution)/shard_map/ppermute | solution.py:724
  871.0 19.2 %collective-permute-start.42 = (f32[3,816,256]{2,1,0:T(8,128)}, f32[3,816,256]{2,1,0:T(8,128)}, u32[]{:S(2)}, u32[]{:S(2)}) collective-permute-start(f32[3,816,256]{2,1,0:T(8,128)} %collective-permute-done.40.rest_9_), channel_id=1, source_target_pairs={{0,1},{1,0},{2,3},{3,2},{4,5},{5,4},{6,7},{7,6},{8,9},{9,8},{10,11... | collective-permute-start | bytes 7520264 | tf_op jit(solution)/shard_map/ppermute | solution.py:724
  878.8 215.2 %collective-permute-start.18 = (f32[3,32,768]{2,1,0:T(8,128)}, f32[3,32,768]{2,1,0:T(8,128)}, u32[]{:S(2)}, u32[]{:S(2)}) collective-permute-start(f32[3,32,768]{2,1,0:T(8,128)} %get-tuple-element.171), channel_id=1, source_target_pairs={{1,0},{2,1},{3,2},{5,4},{6,5},{7,6},{9,8},{10,9},{11,10},{13,12},{... | collective-permute-start | bytes 884744 | tf_op jit(solution)/shard_map/ppermute | solution.py:758
  880.1 116.0 %collective-permute-start.44 = (f32[3,32,256]{2,1,0:T(8,128)}, f32[3,32,256]{2,1,0:T(8,128)}, u32[]{:S(2)}, u32[]{:S(2)}) collective-permute-start(f32[3,32,256]{2,1,0:T(8,128)} %select_select_fusion.1), channel_id=1, source_target_pairs={{0,2},{1,3},{2,0},{3,1},{4,6},{5,7},{6,4},{7,5},{8,10},{9,11},{10,... | collective-permute-start | bytes 294920 | tf_op jit(solution)/shard_map/ppermute | solution.py:683
  995.7 2.2 collective-permute-start.46
  1000.3 46.3 %collective-permute-start.47 = (f32[3,32,256]{2,1,0:T(8,128)}, f32[3,32,256]{2,1,0:T(8,128)}, u32[]{:S(2)}, u32[]{:S(2)}) collective-permute-start(f32[3,32,256]{2,1,0:T(8,128)} %select_select_fusion), channel_id=1, source_target_pairs={{0,2},{1,3},{2,0},{3,1},{4,6},{5,7},{6,4},{7,5},{8,10},{9,11},{10,... | collective-permute-start | bytes 294920 | tf_op jit(solution)/shard_map/ppermute | solution.py:683
  1045.2 50.5 %collective-permute-start.45 = (f32[3,32,768]{2,1,0:T(8,128)}, f32[3,32,768]{2,1,0:T(8,128)}, u32[]{:S(2)}, u32[]{:S(2)}) collective-permute-start(f32[3,32,768]{2,1,0:T(8,128)} %get-tuple-element.185), channel_id=1, source_target_pairs={{1,0},{2,1},{3,2},{5,4},{6,5},{7,6},{9,8},{10,9},{11,10},{13,12},{... | collective-permute-start | bytes 884744 | tf_op jit(solution)/shard_map/ppermute | solution.py:758
  1092.7 4.8 collective-permute-start.48
  1299.6 14.6 collective-permute-start.51
  1303.4 12.0 collective-permute-start.50
  1312.9 2.5 collective-permute-start.49
  (2 other events, 1.7 us)
Sparse Core Ops, SparseCore 0:
  877.2 498.2 all-reduce.3

commit v3 on v2

--- a/solution.py
+++ b/solution.py
@@ -181,9 +181,16 @@
 
     @pl.when((step > 0) & (step < n_chunk))
     def _():
-        for blk in range(n_blk):
+        def both(blk, _):
             elementwise(blk)
             dots(blk)
+            return 0
+
+        if own:
+            for blk in range(n_blk):
+                both(blk, 0)
+        else:
+            lax.fori_loop(0, n_blk, both, 0)
 
     @pl.when(step == n_chunk)
     def _():
@@ -269,19 +276,19 @@
         gb_out[:, lane] += jnp.sum(gz_f.reshape(-1, SUB, LANES), axis=0)
 
 
-def row_specs(batch, n_tok):
-    per = batch // B_BLK
+def row_specs(batch, n_tok, b_blk=B_BLK):
+    per = batch // b_blk
     n_steps = (n_tok // TC) * per
     cur = lambda s: jnp.minimum(s, n_steps - 1)
     old = lambda s: jnp.maximum(s - 1, 0)
-    act = lambda lanes: pl.BlockSpec((TC, B_BLK, lanes), lambda s: (cur(s) // per, lax.rem(cur(s), per), 0))
-    native = lambda lag, lanes: pl.BlockSpec((B_BLK, TC, lanes), lambda s: (lax.rem(lag(s), per), lag(s) // per, 0))
+    act = lambda lanes: pl.BlockSpec((TC, b_blk, lanes), lambda s: (cur(s) // per, lax.rem(cur(s), per), 0))
+    native = lambda lag, lanes: pl.BlockSpec((b_blk, TC, lanes), lambda s: (lax.rem(lag(s), per), lag(s) // per, 0))
     return n_steps, cur, old, act, native
 
 
 def pre_pass(x_in, grad_z, scale):
     batch, n_tok, width = x_in.shape
-    n_steps, cur, _, act, native = row_specs(batch, n_tok)
+    n_steps, cur, _, act, native = row_specs(batch, n_tok, batch)
     const = lambda shape: pl.BlockSpec(shape, lambda s: (0,) * len(shape))
     return pl.pallas_call(
         pre_kernel, grid=(n_steps,),
@@ -703,6 +710,7 @@
     wg = jnp.concatenate([w_a, w_i], axis=-1).astype(F32).reshape(n_own, EXT_PAR, CB)
     ext = jnp.concatenate([wg, par, jnp.zeros((n_own, 6 * EXT_ROWS - EXT_PAR - PAR_ROWS, CB), F32)], axis=1)
 
+    x_halo = lax.ppermute(x_in[:, n_tok - HALO:].astype(F32).transpose(1, 0, 2), "cp", fwd_perm)
     core = jnp.full((1,), cp_index % 2, jnp.int32)
     mine = send_pass(core, w_x, w_y, w_out, ext)
     to_y, to_z = [[(k, k ^ m) for k in range(tp_size)] for m in (1, 2)]
@@ -725,7 +733,8 @@
         return lst
 
     normed, gz_t, inv_b, gb_part = pre_pass(after(x_in, *mine), grad_z, norm_scale.astype(F32).reshape(1, width))
-    n_halo = lax.ppermute(normed[n_tok - HALO:].astype(F32), "cp", fwd_perm).reshape(HALO * batch, width)
+    inv_h = lax.rsqrt(jnp.mean(x_halo * x_halo, axis=-1, keepdims=True) + NORM_EPS)
+    n_halo = (x_halo * inv_h * (1.0 + norm_scale.astype(F32))).reshape(HALO * batch, width)
     normed = normed.reshape(n_tok * batch, width)
     gz_t = gz_t.reshape(n_tok * batch, width)
     pos_b = jnp.broadcast_to(seg_pos.T[:, :, None], (n_tok, batch, LANES))

time: 1490 us -> 1480 us (level)
  Pallas kernels: 936 us -> 913 us
    pallas_call x4, Pallas kernels: 396 us -> 376 us  [first_pass(): pl.pallas_call(functools.partial(first_pass_kernel, n_blk=n_blk, n_chunk=...]
  transfers between devices with their start and end apart: 53 -> 53, of which waited for: 16 -> 14; matrix products, arithmetic and copies ran while one was open for 7% -> 8% of each run, Pallas kernels for 46% -> 50%
where the time goes in v3:
time: 1480 us; the launch traced here: 1470 us
  Pallas kernels  913 us (62%)
  waiting for transfers between devices  349 us (24%)
  matrix products  81 us (5%)
  starting transfers between devices  53.6 us (4%)
  other arithmetic  32.4 us (2%)
  local copies, waits for them, and re-layouts  27.4 us (2%)
  between operations  14.9 us (1%)
    pallas_call x4, Pallas kernels, first_pass(): pl.pallas_call(functools.partial(first_pass_kernel, n_blk=n_blk, n_chunk=...  376 us
    pallas_call x1, Pallas kernels, norm_back_pass(): pl.pallas_call(functools.partial(norm_back_kernel, n_part=n_part, n_steps...  200 us
    pallas_call x4, Pallas kernels, second_pass(): pl.pallas_call(functools.partial(second_pass_kernel, n_chunk=n_chunk, own...  187 us
    ppermute x6, waiting for transfers between devices, shard_body(): got['z', p, u] = lax.ppermute(mine[2 * p + u], 'tp', to_z)  107 us
    ppermute x6, waiting for transfers between devices, shard_body(): got['y', p, u] = lax.ppermute(mine[2 * p + u], 'tp', to_y)  102 us
    pallas_call x1, Pallas kernels, out_pass(): pl.pallas_call(functools.partial(out_kernel, n_part=n_part, n_steps=n_ste...  96.9 us
    dot_general x3, matrix products, dot_tn(): lax.dot_general(lhs, rhs, (((0,), (0,)), ((), ())), preferred_element_typ...  81 us
    psum x1, waiting for transfers between devices, shard_body(): lax.psum((g_w_x, g_w_y, g_w_out, packed), 'cp')  70.2 us
  transfers between devices with their start and end apart: 53, of which 14 were waited for; matrix products, arithmetic and copies ran while one was open for 8% of the time, Pallas kernels for 50%

profile of v3, /device:TPU:0, one launch (start us, length us, event | category | flops | bytes accessed | tf_op | source)
XLA Modules:
  0.0 1471.9 jit_solution(13954618420240514039)
XLA Ops:
  7.2 1.8 slice.255
  9.0 1.3 convert_bitcast_fusion
  10.3 3.7 collective-permute-start
  18.2 1.3 convert_element_type.20
  19.5 1.4 copy.86
  22.0 1.1 maximum_convert_fusion
  24.1 10.7 send_pass.1
  34.8 1.3 broadcast_add_fusion
  36.1 43.2 %pre_pass.1 = (bf16[128,32,3072]{2,1,0:T(8,128)(2,1)}, bf16[128,32,3072]{2,1,0:T(8,128)(2,1)}, f32[32,128,128]{2,1,0:T(8,128)}, f32[8,3072]{1,0:T(8,128)}) custom-call(bf16[32,128,3072]{2,1,0:T(8,128)(2,1)} %refs_11_.1, bf16[32,128,3072]{2,1,0:T(8,128)(2,1)} %refs_15_.1, f32[1,3072]{1,0:T(1,128)} %bitcast.205), custom_call_target="tpu_custom_call" | custom-call | flops 2516582400 | bytes 100663296 | tf_op jit(solution)/shard_map/pre_pass/pallas_call | solution.py:293
  79.3 1.4 multiply_reduce_fusion
  80.7 2.5 multiply_multiply_fusion
  83.2 3.0 broadcast_in_dim.30.pos_ref
  86.2 86.1 %first_pass_own.1 = (bf16[3,128,32,256]{3,2,1,0:T(8,128)(2,1)}, f32[3,128,32,256]{3,2,1,0:T(8,128)}, f32[3,128,32,256]{3,2,1,0:T(8,128)}, f32[3,128,32,256]{3,2,...) custom-call(bf16[4096,3072]{1,0:T(8,128)(2,1)} %bitcast.213, ...), custom_call_target="tpu_custom_call" | custom-call | flops 57982058496 | bytes 50331648 | tf_op jit(solution)/shard_map/first_pass_own/pallas_call | solution.py:242
  173.3 1.6 collective-permute-start.1
  174.9 1.2 collective-permute-done.1
  177.5 1.6 collective-permute-start.8
  179.0 1.5 collective-permute-start.4
  183.0 52.9 %second_pass_own.1 = (bf16[128,32,768]{2,1,0:T(8,128)(2,1)}, bf16[128,32,768]{2,1,0:T(8,128)(2,1)}, bf16[128,32,768]{2,1,0:T(8,128)(2,1)}, f32[3,32,768]{2,1,0:T...) custom-call(bf16[3,128,32,256]{3,2,1,0:T(8,128)(2,1)} %get-tuple-element.148.c_ref, ...), custom_call_target="tpu_custom_call" | custom-call | flops 37748736000 | bytes 62914560 | tf_op jit(solution)/shard_map/second_pass_own/pallas_call | solution.py:491
  235.9 1.3 collective-permute-start.3
  237.2 26.7 %convolution_bitcast_fusion = f32[3072,768]{1,0:T(8,128)} fusion(bf16[128,32,3072]{2,1,0:T(8,128)(2,1)} %get-tuple-element.146, bf16[128,32,768]{2,1,0:T(8,128)(2,1)} %get-tuple-element.159.refs_4_), kind=kOutput, calls=%fused_computation | convolution fusion | flops 19327352832 | bytes 40894464 | tf_op jit(solution)/shard_map/dot_general | solution.py:43
  264.0 1.5 collective-permute-start.12
  266.6 26.8 %convolution_bitcast_fusion.1 = f32[768,3072]{1,0:T(8,128)} fusion(bf16[128,32,768]{2,1,0:T(8,128)(2,1)} %get-tuple-element.204.refs_0_, bf16[128,32,3072]{2,1,0:T(8,128)(2,1)} %get-tuple-element.147), kind=kOutput, calls=%fused_computation.1 | convolution fusion | flops 19327352832 | bytes 40894464 | tf_op jit(solution)/shard_map/dot_general | solution.py:43
  294.6 49.4 %collective-permute-done.12.rest_8_ = f32[3,816,256]{2,1,0:T(8,128)S(1)} collective-permute-done((f32[3,816,256]{2,1,0:T(8,128)}, f32[3,816,256]{2,1,0:T(8,128)S(1)}, u32[]{:S(2)}, u32[]{:S(2)}) %collective-permute-start.12) | collective-permute-done | bytes 2506784 | tf_op jit(solution)/shard_map/ppermute | solution.py:720
  344.0 52.7 %collective-permute-done.13.rest_9_ = f32[3,816,256]{2,1,0:T(8,128)} collective-permute-done((f32[3,816,256]{2,1,0:T(8,128)}, f32[3,816,256]{2,1,0:T(8,128)}, u32[]{:S(2)}, u32[]{:S(2)}) %collective-permute-start.13) | collective-permute-done | bytes 2506784 | tf_op jit(solution)/shard_map/ppermute | solution.py:720
  397.2 27.5 %fusion.10 = f32[3072,768]{1,0:T(8,128)} fusion(bf16[4096,3072]{1,0:T(8,128)(2,1)S(1)} %bitcast.219, bf16[4096,768]{1,0:T(8,128)(2,1)} %bitcast.224), kind=kOutput, calls=%fused_computation.72 | convolution fusion | flops 19327352832 | bytes 40894464 | tf_op jit(solution)/shard_map/dot_general | solution.py:43
  425.3 1.5 collective-permute-start.20
  427.3 1.5 collective-permute-start.23
  428.8 96.6 %first_pass_far.3 = (bf16[3,128,32,256]{3,2,1,0:T(8,128)(2,1)}, f32[3,128,32,256]{3,2,1,0:T(8,128)}, f32[3,128,32,256]{3,2,1,0:T(8,128)}, f32[3,128,32,256]{3,2,...) custom-call(bf16[4096,3072]{1,0:T(8,128)(2,1)} %bitcast.214, ...), custom_call_target="tpu_custom_call" | custom-call | flops 57982058496 | bytes 50331648 | tf_op jit(solution)/shard_map/first_pass_far/pallas_call | solution.py:242
  526.4 1.6 collective-permute-done.16
  529.0 1.7 collective-permute-start.17
  530.8 1.6 collective-permute-start.28
  532.4 3.7 collective-permute-done.20.rest_1_
  536.1 1.6 collective-permute-start.24
  537.6 52.2 %collective-permute-done.27.rest_8_ = f32[3,816,256]{2,1,0:T(8,128)} collective-permute-done((f32[3,816,256]{2,1,0:T(8,128)}, f32[3,816,256]{2,1,0:T(8,128)}, u32[]{:S(2)}, u32[]{:S(2)}) %collective-permute-start.27) | collective-permute-done | bytes 2506784 | tf_op jit(solution)/shard_map/ppermute | solution.py:721
  590.3 1.5 collective-permute-start.32
  592.5 51.0 %collective-permute-done.28.rest_9_ = f32[3,816,256]{2,1,0:T(8,128)} collective-permute-done((f32[3,816,256]{2,1,0:T(8,128)}, f32[3,816,256]{2,1,0:T(8,128)}, u32[]{:S(2)}, u32[]{:S(2)}) %collective-permute-start.28) | collective-permute-done | bytes 2506784 | tf_op jit(solution)/shard_map/ppermute | solution.py:721
  644.0 52.3 %collective-permute-done.31.rest_0_ = f32[3,816,256]{2,1,0:T(8,128)} collective-permute-done((f32[3,816,256]{2,1,0:T(8,128)}, f32[3,816,256]{2,1,0:T(8,128)}, u32[]{:S(2)}, u32[]{:S(2)}) %collective-permute-start.31) | collective-permute-done | bytes 2506784 | tf_op jit(solution)/shard_map/ppermute | solution.py:723
  696.9 44.5 %second_pass_far.3 = (bf16[128,32,768]{2,1,0:T(8,128)(2,1)}, bf16[128,32,768]{2,1,0:T(8,128)(2,1)}, bf16[128,32,768]{2,1,0:T(8,128)(2,1)}, f32[3,32,768]{2,1,0:T(8,128)}, f32[3,32,768]{2,1,0:T(8,128)}) custom-call(bf16[3,128,32,256]{3,2,1,0:T(8,128)(2,1)} %get-tuple-element.164.c_ref, f32[3,128,32,256]{3,2,1,0:T(8,128)} %get-tuple-element.165.y_ref, ...), custom_call_target="tpu_custom_call" | custom-call | flops 37748736000 | bytes 62914560 | tf_op jit(solution)/shard_map/second_pass_far/pallas_call | solution.py:491
  741.9 1.5 collective-permute-start.36
  743.4 1.6 collective-permute-start.39
  745.5 96.8 %first_pass_far.4 = (bf16[3,128,32,256]{3,2,1,0:T(8,128)(2,1)}, f32[3,128,32,256]{3,2,1,0:T(8,128)}, f32[3,128,32,256]{3,2,1,0:T(8,128)}, f32[3,128,32,256]{3,2,...) custom-call(bf16[4096,3072]{1,0:T(8,128)(2,1)} %bitcast.215, ...), custom_call_target="tpu_custom_call" | custom-call | flops 57982058496 | bytes 50331648 | tf_op jit(solution)/shard_map/first_pass_far/pallas_call | solution.py:242
  844.0 8.2 collective-permute-done.39.rest_8_
  857.1 2.1 pad_maximum_fusion
  860.9 1.3 collective-permute-start.18
  862.2 2.5 collective-permute-start.44
  864.7 4.7 collective-permute-done.42.rest_11_
  869.3 96.8 %first_pass_far.5 = (bf16[3,128,32,256]{3,2,1,0:T(8,128)(2,1)}, f32[3,128,32,256]{3,2,1,0:T(8,128)}, f32[3,128,32,256]{3,2,1,0:T(8,128)}, f32[3,128,32,256]{3,2,...) custom-call(bf16[4096,3072]{1,0:T(8,128)(2,1)} %bitcast.216, ...), custom_call_target="tpu_custom_call" | custom-call | flops 57982058496 | bytes 50331648 | tf_op jit(solution)/shard_map/first_pass_far/pallas_call | solution.py:242
  970.0 1.7 select_select_fusion
  971.7 1.7 collective-permute-start.47
  973.4 44.8 %second_pass_far.4 = (bf16[128,32,768]{2,1,0:T(8,128)(2,1)}, bf16[128,32,768]{2,1,0:T(8,128)(2,1)}, bf16[128,32,768]{2,1,0:T(8,128)(2,1)}, f32[3,32,768]{2,1,0:T(8,128)}, f32[3,32,768]{2,1,0:T(8,128)}) custom-call(bf16[3,128,32,256]{3,2,1,0:T(8,128)(2,1)} %get-tuple-element.178.c_ref, f32[3,128,32,256]{3,2,1,0:T(8,128)} %get-tuple-element.179.y_ref, ...), custom_call_target="tpu_custom_call" | custom-call | flops 37748736000 | bytes 62914560 | tf_op jit(solution)/shard_map/second_pass_far/pallas_call | solution.py:491
  1018.3 1.3 collective-permute-start.45
  1021.3 44.5 %second_pass_far.5 = (bf16[128,32,768]{2,1,0:T(8,128)(2,1)}, bf16[128,32,768]{2,1,0:T(8,128)(2,1)}, bf16[128,32,768]{2,1,0:T(8,128)(2,1)}, f32[3,32,768]{2,1,0:T(8,128)}, f32[3,32,768]{2,1,0:T(8,128)}) custom-call(bf16[3,128,32,256]{3,2,1,0:T(8,128)(2,1)} %get-tuple-element.188.c_ref, f32[3,128,32,256]{3,2,1,0:T(8,128)} %get-tuple-element.189.y_ref, ...), custom_call_target="tpu_custom_call" | custom-call | flops 37748736000 | bytes 62914560 | tf_op jit(solution)/shard_map/second_pass_far/pallas_call | solution.py:491
  1065.9 1.3 collective-permute-start.48
  1067.2 1.7 fusion.1.refs_1_
  1068.9 1.8 fusion.2.refs_2_
  1070.7 1.7 fusion.3.refs_3_
  1072.3 199.6 %norm_back_pass.1 = (bf16[32,128,3072]{2,1,0:T(8,128)(2,1)}, f32[8,3072]{1,0:T(8,128)}) custom-call(bf16[128,32,768]{2,1,0:T(8,128)(2,1)} %fusion.refs_0_, bf16[128,32,768]{2,1,0:T(8,128)(2,1)} %fusion.1.refs_1_, bf16[128,32,768]{2,1,0:T(8,128)(2,1)} %fusion.2.refs_2_, bf16[128,32,768]{2,1,0:T(8,128)(2,1)} %fusion.3.refs_3_, ...), custom_call_target="tpu_custom_call" | custom-call | flops 154618822656 | bytes 125829120 | tf_op jit(solution)/shard_map/norm_back_pass/pallas_call | solution.py:666
  1272.8 3.0 collective-permute-start.51
  1275.8 10.0 collective-permute-start.50
  1285.8 1.3 reshape.290
  1287.1 1.2 collective-permute-done.50
  1288.9 70.2 %all-reduce.4.cloned.1.call-done = (f32[3072,768]{1,0:T(8,128)}, f32[3072,768]{1,0:T(8,128)}, f32[768,3072]{1,0:T(8,128)}, f32[816,256]{1,0:T(8,128)}) async-done(((f32[3072,768]{1,0:T(8,128)}, f32[3072,768]{1,0:T(8,128)}, f32[768,3072]{1,0:T(8,128)}, f32[816,256]{1,0:T(8,128)}), (f32[3072,768]{1,0:T(8,128)}, f32[3072,768]{1,0:T(8,128)}, f32[768,3072]{1,0:T(8,128)}, ...) | async-done | bytes 29147152 | tf_op jit(solution)/shard_map/psum | solution.py:779
  1360.7 1.2 slice.332
  1367.7 96.9 %out_pass.1 = (bf16[32,128,3072]{2,1,0:T(8,128)(2,1)}, f32[3072,768]{1,0:T(8,128)}, f32[3072,768]{1,0:T(8,128)}, f32[768,3072]{1,0:T(8,128)}) custom-call(bf16[128,32,768]{2,1,0:T(8,128)(2,1)} %get-tuple-element.204.refs_0_, bf16[128,32,768]{2,1,0:T(8,128)(2,1)} %get-tuple-element.172.refs_1_, bf16[128,32,768]{2,1,0:T(8,128)(2,1)} %get-tuple-element.187.refs_2_, ...), custom_call_target="tpu_custom_call" | custom-call | flops 77309411328 | bytes 100663296 | tf_op jit(solution)/shard_map/out_pass/pallas_call | solution.py:564
  (159 shorter events, 43.1 us)
Async XLA Ops:
  7.2 1351.8 %all-reduce.4.cloned.1.call-start = ((), (), s32[]{:S(2)}) async-start(), calls=%async_computation | async-start | bytes 58294272 | tf_op jit(solution)/shard_map/psum | solution.py:779
  10.3 68.9 %collective-permute-start = (f32[3,32,3072]{2,1,0:T(8,128)}, f32[3,32,3072]{2,1,0:T(8,128)}, u32[]{:S(2)}, u32[]{:S(2)}) collective-permute-start(f32[3,32,3072]{2,1,0:T(8,128)} %convert_bitcast_fusion), channel_id=1, source_target_pairs={{0,1},{1,2},{2,3},{4,5},{5,6},{6,7},{8,9},{9,10},{10,11},{12,13},{... | collective-permute-start | bytes 3538952 | tf_op jit(solution)/shard_map/ppermute | solution.py:713
  173.3 2.8 collective-permute-start.1
  177.2 5.1 collective-permute-start.2
  177.5 88.0 %collective-permute-start.8 = (f32[3,816,256]{2,1,0:T(8,128)}, f32[3,816,256]{2,1,0:T(8,128)}, u32[]{:S(2)}, u32[]{:S(2)}) collective-permute-start(f32[3,816,256]{2,1,0:T(8,128)} %get-tuple-element.139), channel_id=1, source_target_pairs={{0,8},{4,12},{8,0},{12,4},{1,9},{5,13},{9,1},{13,5},{2,10},{6,14},... | collective-permute-start | bytes 7520264 | tf_op jit(solution)/shard_map/ppermute | solution.py:721
  179.0 87.0 %collective-permute-start.4 = (f32[3,816,256]{2,1,0:T(8,128)}, f32[3,816,256]{2,1,0:T(8,128)}, u32[]{:S(2)}, u32[]{:S(2)}) collective-permute-start(f32[3,816,256]{2,1,0:T(8,128)} %get-tuple-element.139), channel_id=1, source_target_pairs={{0,4},{4,0},{8,12},{12,8},{1,5},{5,1},{9,13},{13,9},{2,6},{6,2},{1... | collective-permute-start | bytes 7520264 | tf_op jit(solution)/shard_map/ppermute | solution.py:720
  180.6 113.5 %collective-permute-start.9 = (f32[3,816,256]{2,1,0:T(8,128)}, f32[3,816,256]{2,1,0:T(8,128)}, u32[]{:S(2)}, u32[]{:S(2)}) collective-permute-start(f32[3,816,256]{2,1,0:T(8,128)} %get-tuple-element.140), channel_id=1, source_target_pairs={{0,8},{4,12},{8,0},{12,4},{1,9},{5,13},{9,1},{13,5},{2,10},{6,14},... | collective-permute-start | bytes 7520264 | tf_op jit(solution)/shard_map/ppermute | solution.py:721
  181.0 113.1 %collective-permute-start.5 = (f32[3,816,256]{2,1,0:T(8,128)}, f32[3,816,256]{2,1,0:T(8,128)}, u32[]{:S(2)}, u32[]{:S(2)}) collective-permute-start(f32[3,816,256]{2,1,0:T(8,128)} %get-tuple-element.140), channel_id=1, source_target_pairs={{0,4},{4,0},{8,12},{12,8},{1,5},{5,1},{9,13},{13,9},{2,6},{6,2},{1... | collective-permute-start | bytes 7520264 | tf_op jit(solution)/shard_map/ppermute | solution.py:720
  235.9 28.1 %collective-permute-start.3 = (f32[3,32,768]{2,1,0:T(8,128)}, f32[3,32,768]{2,1,0:T(8,128)S(1)}, u32[]{:S(2)}, u32[]{:S(2)}) collective-permute-start(f32[3,32,768]{2,1,0:T(8,128)} %get-tuple-element.158), channel_id=1, source_target_pairs={{1,0},{2,1},{3,2},{5,4},{6,5},{7,6},{9,8},{10,9},{11,10},{13,12},{... | collective-permute-start | bytes 884744 | tf_op jit(solution)/shard_map/ppermute | solution.py:746
  237.2 160.0 %slice-start = ((s8[25165824]{0:T(1024)(128)(4,1)}), s8[4194304]{0:T(1024)(128)(4,1)S(1)}, s32[]{:S(2)}) async-start(s8[25165824]{0:T(1024)(128)(4,1)} %bitcast.217), calls=%async_computation.1 | async-start | bytes 8388608
  237.2 160.0 %slice-start.1 = ((s8[25165824]{0:T(1024)(128)(4,1)}), s8[4194304]{0:T(1024)(128)(4,1)S(1)}, s32[]{:S(2)}) async-start(s8[25165824]{0:T(1024)(128)(4,1)} %bitcast.217), calls=%async_computation.2 | async-start | bytes 8388608
  237.2 160.0 %slice-start.2 = ((s8[25165824]{0:T(1024)(128)(4,1)}), s8[4194304]{0:T(1024)(128)(4,1)S(1)}, s32[]{:S(2)}) async-start(s8[25165824]{0:T(1024)(128)(4,1)} %bitcast.217), calls=%async_computation.3 | async-start | bytes 8388608
  264.0 29.4 %copy-start.3 = (f32[3,32,768]{2,1,0:T(8,128)}, f32[3,32,768]{2,1,0:T(8,128)S(1)}, u32[]{:S(2)}) copy-start(f32[3,32,768]{2,1,0:T(8,128)S(1)} %collective-permute-done.3) | copy-start | bytes 884740
  264.0 80.0 %collective-permute-start.12 = (f32[3,816,256]{2,1,0:T(8,128)}, f32[3,816,256]{2,1,0:T(8,128)S(1)}, u32[]{:S(2)}, u32[]{:S(2)}) collective-permute-start(f32[3,816,256]{2,1,0:T(8,128)} %get-tuple-element.141), channel_id=1, source_target_pairs={{0,4},{4,0},{8,12},{12,8},{1,5},{5,1},{9,13},{13,9},{2,6},{6,2},{1... | collective-permute-start | bytes 7520264 | tf_op jit(solution)/shard_map/ppermute | solution.py:720
  265.5 131.2 %collective-permute-start.13 = (f32[3,816,256]{2,1,0:T(8,128)}, f32[3,816,256]{2,1,0:T(8,128)}, u32[]{:S(2)}, u32[]{:S(2)}) collective-permute-start(f32[3,816,256]{2,1,0:T(8,128)} %get-tuple-element.142), channel_id=1, source_target_pairs={{0,4},{4,0},{8,12},{12,8},{1,5},{5,1},{9,13},{13,9},{2,6},{6,2},{1... | collective-permute-start | bytes 7520264 | tf_op jit(solution)/shard_map/ppermute | solution.py:720
  266.0 130.7 %collective-permute-start.10 = (f32[3,816,256]{2,1,0:T(8,128)}, f32[3,816,256]{2,1,0:T(8,128)}, u32[]{:S(2)}, u32[]{:S(2)}) collective-permute-start(f32[3,816,256]{2,1,0:T(8,128)} %collective-permute-done.8.rest_4_), channel_id=1, source_target_pairs={{0,1},{1,0},{2,3},{3,2},{4,5},{5,4},{6,7},{7,6},{8,9},{9,8},{10,11... | collective-permute-start | bytes 7520264 | tf_op jit(solution)/shard_map/ppermute | solution.py:732
  266.6 26.8 %copy-start.4 = (f32[3,32,768]{2,1,0:T(8,128)S(1)}, f32[3,32,768]{2,1,0:T(8,128)}, u32[]{:S(2)}) copy-start(f32[3,32,768]{2,1,0:T(8,128)} %get-tuple-element.157) | copy-start | bytes 884740
  266.6 130.6 %slice-start.3 = ((s8[25165824]{0:T(1024)(128)(4,1)}), s8[4194304]{0:T(1024)(128)(4,1)S(1)}, s32[]{:S(2)}) async-start(s8[25165824]{0:T(1024)(128)(4,1)} %bitcast.217), calls=%async_computation.4 | async-start | bytes 8388608
  266.6 130.6 %slice-start.4 = ((s8[25165824]{0:T(1024)(128)(4,1)}), s8[4194304]{0:T(1024)(128)(4,1)S(1)}, s32[]{:S(2)}) async-start(s8[25165824]{0:T(1024)(128)(4,1)} %bitcast.217), calls=%async_computation.5 | async-start | bytes 8388608
  266.6 130.6 %slice-start.5 = ((s8[25165824]{0:T(1024)(128)(4,1)}), s8[4194304]{0:T(1024)(128)(4,1)S(1)}, s32[]{:S(2)}) async-start(s8[25165824]{0:T(1024)(128)(4,1)} %bitcast.217), calls=%async_computation.6 | async-start | bytes 8388608
  294.0 130.7 %collective-permute-start.6 = (f32[3,816,256]{2,1,0:T(8,128)}, f32[3,816,256]{2,1,0:T(8,128)}, u32[]{:S(2)}, u32[]{:S(2)}) collective-permute-start(f32[3,816,256]{2,1,0:T(8,128)} %collective-permute-done.4.rest_0_), channel_id=1, source_target_pairs={{0,1},{1,0},{2,3},{3,2},{4,5},{5,4},{6,7},{7,6},{8,9},{9,8},{10,11... | collective-permute-start | bytes 7520264 | tf_op jit(solution)/shard_map/ppermute | solution.py:732
  294.1 131.2 %collective-permute-start.11 = (f32[3,816,256]{2,1,0:T(8,128)}, f32[3,816,256]{2,1,0:T(8,128)}, u32[]{:S(2)}, u32[]{:S(2)}) collective-permute-start(f32[3,816,256]{2,1,0:T(8,128)} %collective-permute-done.9.rest_5_), channel_id=1, source_target_pairs={{0,1},{1,0},{2,3},{3,2},{4,5},{5,4},{6,7},{7,6},{8,9},{9,8},{10,11... | collective-permute-start | bytes 7520264 | tf_op jit(solution)/shard_map/ppermute | solution.py:732
  344.0 80.8 %copy-start.5 = (f32[3,816,256]{2,1,0:T(8,128)}, f32[3,816,256]{2,1,0:T(8,128)S(1)}, u32[]{:S(2)}) copy-start(f32[3,816,256]{2,1,0:T(8,128)S(1)} %collective-permute-done.12.rest_8_) | copy-start | bytes 7520260
  344.0 82.8 %collective-permute-start.7 = (f32[3,816,256]{2,1,0:T(8,128)}, f32[3,816,256]{2,1,0:T(8,128)}, u32[]{:S(2)}, u32[]{:S(2)}) collective-permute-start(f32[3,816,256]{2,1,0:T(8,128)} %collective-permute-done.5.rest_1_), channel_id=1, source_target_pairs={{0,1},{1,0},{2,3},{3,2},{4,5},{5,4},{6,7},{7,6},{8,9},{9,8},{10,11... | collective-permute-start | bytes 7520264 | tf_op jit(solution)/shard_map/ppermute | solution.py:732
  396.7 30.6 %collective-permute-start.14 = (f32[3,816,256]{2,1,0:T(8,128)S(1)}, f32[3,816,256]{2,1,0:T(8,128)}, u32[]{:S(2)}, u32[]{:S(2)}) collective-permute-start(f32[3,816,256]{2,1,0:T(8,128)S(1)} %collective-permute-done.12.rest_8_), channel_id=1, source_target_pairs={{0,1},{1,0},{2,3},{3,2},{4,5},{5,4},{6,7},{7,6},{8,9},{9,8},{10,11... | collective-permute-start | bytes 7520264 | tf_op jit(solution)/shard_map/ppermute | solution.py:732
  396.7 32.1 %collective-permute-start.15 = (f32[3,816,256]{2,1,0:T(8,128)}, f32[3,816,256]{2,1,0:T(8,128)}, u32[]{:S(2)}, u32[]{:S(2)}) collective-permute-start(f32[3,816,256]{2,1,0:T(8,128)} %collective-permute-done.13.rest_9_), channel_id=1, source_target_pairs={{0,1},{1,0},{2,3},{3,2},{4,5},{5,4},{6,7},{7,6},{8,9},{9,8},{10,11... | collective-permute-start | bytes 7520264 | tf_op jit(solution)/shard_map/ppermute | solution.py:732
  424.8 106.0 %collective-permute-start.19 = (f32[3,816,256]{2,1,0:T(8,128)}, f32[3,816,256]{2,1,0:T(8,128)}, u32[]{:S(2)}, u32[]{:S(2)}) collective-permute-start(f32[3,816,256]{2,1,0:T(8,128)} %get-tuple-element.141), channel_id=1, source_target_pairs={{0,8},{4,12},{8,0},{12,4},{1,9},{5,13},{9,1},{13,5},{2,10},{6,14},... | collective-permute-start | bytes 7520264 | tf_op jit(solution)/shard_map/ppermute | solution.py:721
  425.3 110.8 %collective-permute-start.20 = (f32[3,816,256]{2,1,0:T(8,128)}, f32[3,816,256]{2,1,0:T(8,128)}, u32[]{:S(2)}, u32[]{:S(2)}) collective-permute-start(f32[3,816,256]{2,1,0:T(8,128)} %get-tuple-element.142), channel_id=1, source_target_pairs={{0,8},{4,12},{8,0},{12,4},{1,9},{5,13},{9,1},{13,5},{2,10},{6,14},... | collective-permute-start | bytes 7520264 | tf_op jit(solution)/shard_map/ppermute | solution.py:721
  426.8 163.0 %collective-permute-start.27 = (f32[3,816,256]{2,1,0:T(8,128)}, f32[3,816,256]{2,1,0:T(8,128)}, u32[]{:S(2)}, u32[]{:S(2)}) collective-permute-start(f32[3,816,256]{2,1,0:T(8,128)} %get-tuple-element.143), channel_id=1, source_target_pairs={{0,8},{4,12},{8,0},{12,4},{1,9},{5,13},{9,1},{13,5},{2,10},{6,14},... | collective-permute-start | bytes 7520264 | tf_op jit(solution)/shard_map/ppermute | solution.py:721
  427.3 163.0 %collective-permute-start.23 = (f32[3,816,256]{2,1,0:T(8,128)}, f32[3,816,256]{2,1,0:T(8,128)}, u32[]{:S(2)}, u32[]{:S(2)}) collective-permute-start(f32[3,816,256]{2,1,0:T(8,128)} %get-tuple-element.143), channel_id=1, source_target_pairs={{0,4},{4,0},{8,12},{12,8},{1,5},{5,1},{9,13},{13,9},{2,6},{6,2},{1... | collective-permute-start | bytes 7520264 | tf_op jit(solution)/shard_map/ppermute | solution.py:720
  526.4 1.6 collective-permute-start.16
  529.0 62.8 %collective-permute-start.17 = (f32[3,32,256]{2,1,0:T(8,128)S(1)}, f32[3,32,256]{2,1,0:T(8,128)S(1)}, u32[]{:S(2)}, u32[]{:S(2)}) collective-permute-start(f32[3,32,256]{2,1,0:T(8,128)S(1)} %select_select_fusion.2), channel_id=1, source_target_pairs={{0,2},{1,3},{2,0},{3,1},{4,6},{5,7},{6,4},{7,5},{8,10},{9,11},{10,... | collective-permute-start | bytes 294920 | tf_op jit(solution)/shard_map/ppermute | solution.py:690
  530.8 112.8 %collective-permute-start.28 = (f32[3,816,256]{2,1,0:T(8,128)}, f32[3,816,256]{2,1,0:T(8,128)}, u32[]{:S(2)}, u32[]{:S(2)}) collective-permute-start(f32[3,816,256]{2,1,0:T(8,128)} %get-tuple-element.144), channel_id=1, source_target_pairs={{0,8},{4,12},{8,0},{12,4},{1,9},{5,13},{9,1},{13,5},{2,10},{6,14},... | collective-permute-start | bytes 7520264 | tf_op jit(solution)/shard_map/ppermute | solution.py:721
  536.1 107.4 %collective-permute-start.24 = (f32[3,816,256]{2,1,0:T(8,128)}, f32[3,816,256]{2,1,0:T(8,128)}, u32[]{:S(2)}, u32[]{:S(2)}) collective-permute-start(f32[3,816,256]{2,1,0:T(8,128)} %get-tuple-element.144), channel_id=1, source_target_pairs={{0,4},{4,0},{8,12},{12,8},{1,5},{5,1},{9,13},{13,9},{2,6},{6,2},{1... | collective-permute-start | bytes 7520264 | tf_op jit(solution)/shard_map/ppermute | solution.py:720
  589.8 106.5 %collective-permute-start.31 = (f32[3,816,256]{2,1,0:T(8,128)}, f32[3,816,256]{2,1,0:T(8,128)}, u32[]{:S(2)}, u32[]{:S(2)}) collective-permute-start(f32[3,816,256]{2,1,0:T(8,128)} %collective-permute-done.4.rest_0_), channel_id=1, source_target_pairs={{0,8},{4,12},{8,0},{12,4},{1,9},{5,13},{9,1},{13,5},{2,10},{6,14},... | collective-permute-start | bytes 7520264 | tf_op jit(solution)/shard_map/ppermute | solution.py:723
  590.3 106.0 %collective-permute-start.32 = (f32[3,816,256]{2,1,0:T(8,128)}, f32[3,816,256]{2,1,0:T(8,128)}, u32[]{:S(2)}, u32[]{:S(2)}) collective-permute-start(f32[3,816,256]{2,1,0:T(8,128)} %collective-permute-done.9.rest_5_), channel_id=1, source_target_pairs={{0,4},{4,0},{8,12},{12,8},{1,5},{5,1},{9,13},{13,9},{2,6},{6,2},{1... | collective-permute-start | bytes 7520264 | tf_op jit(solution)/shard_map/ppermute | solution.py:724
  591.8 105.0 %collective-permute-start.21 = (f32[3,816,256]{2,1,0:T(8,128)}, f32[3,816,256]{2,1,0:T(8,128)}, u32[]{:S(2)}, u32[]{:S(2)}) collective-permute-start(f32[3,816,256]{2,1,0:T(8,128)} %collective-permute-done.19.rest_0_), channel_id=1, source_target_pairs={{0,1},{1,0},{2,3},{3,2},{4,5},{5,4},{6,7},{7,6},{8,9},{9,8},{10,11... | collective-permute-start | bytes 7520264 | tf_op jit(solution)/shard_map/ppermute | solution.py:732
  643.5 97.8 %collective-permute-start.22 = (f32[3,816,256]{2,1,0:T(8,128)}, f32[3,816,256]{2,1,0:T(8,128)}, u32[]{:S(2)}, u32[]{:S(2)}) collective-permute-start(f32[3,816,256]{2,1,0:T(8,128)} %collective-permute-done.20.rest_1_), channel_id=1, source_target_pairs={{0,1},{1,0},{2,3},{3,2},{4,5},{5,4},{6,7},{7,6},{8,9},{9,8},{10,11... | collective-permute-start | bytes 7520264 | tf_op jit(solution)/shard_map/ppermute | solution.py:732
  643.5 98.3 %collective-permute-start.29 = (f32[3,816,256]{2,1,0:T(8,128)}, f32[3,816,256]{2,1,0:T(8,128)}, u32[]{:S(2)}, u32[]{:S(2)}) collective-permute-start(f32[3,816,256]{2,1,0:T(8,128)} %collective-permute-done.27.rest_8_), channel_id=1, source_target_pairs={{0,1},{1,0},{2,3},{3,2},{4,5},{5,4},{6,7},{7,6},{8,9},{9,8},{10,11... | collective-permute-start | bytes 7520264 | tf_op jit(solution)/shard_map/ppermute | solution.py:732
  696.3 47.1 %collective-permute-start.25 = (f32[3,816,256]{2,1,0:T(8,128)}, f32[3,816,256]{2,1,0:T(8,128)}, u32[]{:S(2)}, u32[]{:S(2)}) collective-permute-start(f32[3,816,256]{2,1,0:T(8,128)} %collective-permute-done.23.rest_4_), channel_id=1, source_target_pairs={{0,1},{1,0},{2,3},{3,2},{4,5},{5,4},{6,7},{7,6},{8,9},{9,8},{10,11... | collective-permute-start | bytes 7520264 | tf_op jit(solution)/shard_map/ppermute | solution.py:732
  696.3 48.7 %collective-permute-start.30 = (f32[3,816,256]{2,1,0:T(8,128)}, f32[3,816,256]{2,1,0:T(8,128)}, u32[]{:S(2)}, u32[]{:S(2)}) collective-permute-start(f32[3,816,256]{2,1,0:T(8,128)} %collective-permute-done.28.rest_9_), channel_id=1, source_target_pairs={{0,1},{1,0},{2,3},{3,2},{4,5},{5,4},{6,7},{7,6},{8,9},{9,8},{10,11... | collective-permute-start | bytes 7520264 | tf_op jit(solution)/shard_map/ppermute | solution.py:732
  696.8 48.6 %collective-permute-start.26 = (f32[3,816,256]{2,1,0:T(8,128)}, f32[3,816,256]{2,1,0:T(8,128)}, u32[]{:S(2)}, u32[]{:S(2)}) collective-permute-start(f32[3,816,256]{2,1,0:T(8,128)} %collective-permute-done.24.rest_5_), channel_id=1, source_target_pairs={{0,1},{1,0},{2,3},{3,2},{4,5},{5,4},{6,7},{7,6},{8,9},{9,8},{10,11... | collective-permute-start | bytes 7520264 | tf_op jit(solution)/shard_map/ppermute | solution.py:732
  741.4 101.9 %collective-permute-start.35 = (f32[3,816,256]{2,1,0:T(8,128)}, f32[3,816,256]{2,1,0:T(8,128)}, u32[]{:S(2)}, u32[]{:S(2)}) collective-permute-start(f32[3,816,256]{2,1,0:T(8,128)} %copy-done.5), channel_id=1, source_target_pairs={{0,8},{4,12},{8,0},{12,4},{1,9},{5,13},{9,1},{13,5},{2,10},{6,14},... | collective-permute-start | bytes 7520264 | tf_op jit(solution)/shard_map/ppermute | solution.py:723
  741.9 102.0 %collective-permute-start.36 = (f32[3,816,256]{2,1,0:T(8,128)}, f32[3,816,256]{2,1,0:T(8,128)}, u32[]{:S(2)}, u32[]{:S(2)}) collective-permute-start(f32[3,816,256]{2,1,0:T(8,128)} %collective-permute-done.20.rest_1_), channel_id=1, source_target_pairs={{0,4},{4,0},{8,12},{12,8},{1,5},{5,1},{9,13},{13,9},{2,6},{6,2},{1... | collective-permute-start | bytes 7520264 | tf_op jit(solution)/shard_map/ppermute | solution.py:724
  743.4 108.8 %collective-permute-start.39 = (f32[3,816,256]{2,1,0:T(8,128)}, f32[3,816,256]{2,1,0:T(8,128)}, u32[]{:S(2)}, u32[]{:S(2)}) collective-permute-start(f32[3,816,256]{2,1,0:T(8,128)} %collective-permute-done.23.rest_4_), channel_id=1, source_target_pairs={{0,8},{4,12},{8,0},{12,4},{1,9},{5,13},{9,1},{13,5},{2,10},{6,14},... | collective-permute-start | bytes 7520264 | tf_op jit(solution)/shard_map/ppermute | solution.py:723
  745.0 107.4 %collective-permute-start.40 = (f32[3,816,256]{2,1,0:T(8,128)}, f32[3,816,256]{2,1,0:T(8,128)}, u32[]{:S(2)}, u32[]{:S(2)}) collective-permute-start(f32[3,816,256]{2,1,0:T(8,128)} %collective-permute-done.28.rest_9_), channel_id=1, source_target_pairs={{0,4},{4,0},{8,12},{12,8},{1,5},{5,1},{9,13},{13,9},{2,6},{6,2},{1... | collective-permute-start | bytes 7520264 | tf_op jit(solution)/shard_map/ppermute | solution.py:724
  745.5 107.5 %collective-permute-start.33 = (f32[3,816,256]{2,1,0:T(8,128)}, f32[3,816,256]{2,1,0:T(8,128)}, u32[]{:S(2)}, u32[]{:S(2)}) collective-permute-start(f32[3,816,256]{2,1,0:T(8,128)} %collective-permute-done.31.rest_0_), channel_id=1, source_target_pairs={{0,1},{1,0},{2,3},{3,2},{4,5},{5,4},{6,7},{7,6},{8,9},{9,8},{10,11... | collective-permute-start | bytes 7520264 | tf_op jit(solution)/shard_map/ppermute | solution.py:732
  843.3 9.5 collective-permute-start.43
  843.9 17.0 %collective-permute-start.34 = (f32[3,816,256]{2,1,0:T(8,128)}, f32[3,816,256]{2,1,0:T(8,128)}, u32[]{:S(2)}, u32[]{:S(2)}) collective-permute-start(f32[3,816,256]{2,1,0:T(8,128)} %collective-permute-done.32.rest_1_), channel_id=1, source_target_pairs={{0,1},{1,0},{2,3},{3,2},{4,5},{5,4},{6,7},{7,6},{8,9},{9,8},{10,11... | collective-permute-start | bytes 7520264 | tf_op jit(solution)/shard_map/ppermute | solution.py:732
  852.2 10.0 collective-permute-start.37
  852.4 12.3 collective-permute-start.38
  852.7 6.5 copy-start
  852.7 12.0 collective-permute-start.41
  852.9 16.4 %collective-permute-start.42 = (f32[3,816,256]{2,1,0:T(8,128)}, f32[3,816,256]{2,1,0:T(8,128)}, u32[]{:S(2)}, u32[]{:S(2)}) collective-permute-start(f32[3,816,256]{2,1,0:T(8,128)} %collective-permute-done.40.rest_9_), channel_id=1, source_target_pairs={{0,1},{1,0},{2,3},{3,2},{4,5},{5,4},{6,7},{7,6},{8,9},{9,8},{10,11... | collective-permute-start | bytes 7520264 | tf_op jit(solution)/shard_map/ppermute | solution.py:732
  859.2 1.0 copy-start.1
  860.9 206.3 %collective-permute-start.18 = (f32[3,32,768]{2,1,0:T(8,128)}, f32[3,32,768]{2,1,0:T(8,128)}, u32[]{:S(2)}, u32[]{:S(2)}) collective-permute-start(f32[3,32,768]{2,1,0:T(8,128)} %get-tuple-element.171), channel_id=1, source_target_pairs={{1,0},{2,1},{3,2},{5,4},{6,5},{7,6},{9,8},{10,9},{11,10},{13,12},{... | collective-permute-start | bytes 884744 | tf_op jit(solution)/shard_map/ppermute | solution.py:767
  862.2 105.4 %collective-permute-start.44 = (f32[3,32,256]{2,1,0:T(8,128)}, f32[3,32,256]{2,1,0:T(8,128)}, u32[]{:S(2)}, u32[]{:S(2)}) collective-permute-start(f32[3,32,256]{2,1,0:T(8,128)} %select_select_fusion.1), channel_id=1, source_target_pairs={{0,2},{1,3},{2,0},{3,1},{4,6},{5,7},{6,4},{7,5},{8,10},{9,11},{10,... | collective-permute-start | bytes 294920 | tf_op jit(solution)/shard_map/ppermute | solution.py:690
  967.2 2.1 collective-permute-start.46
  971.7 47.9 %collective-permute-start.47 = (f32[3,32,256]{2,1,0:T(8,128)}, f32[3,32,256]{2,1,0:T(8,128)}, u32[]{:S(2)}, u32[]{:S(2)}) collective-permute-start(f32[3,32,256]{2,1,0:T(8,128)} %select_select_fusion), channel_id=1, source_target_pairs={{0,2},{1,3},{2,0},{3,1},{4,6},{5,7},{6,4},{7,5},{8,10},{9,11},{10,... | collective-permute-start | bytes 294920 | tf_op jit(solution)/shard_map/ppermute | solution.py:690
  1018.3 50.6 %collective-permute-start.45 = (f32[3,32,768]{2,1,0:T(8,128)}, f32[3,32,768]{2,1,0:T(8,128)}, u32[]{:S(2)}, u32[]{:S(2)}) collective-permute-start(f32[3,32,768]{2,1,0:T(8,128)} %get-tuple-element.185), channel_id=1, source_target_pairs={{1,0},{2,1},{3,2},{5,4},{6,5},{7,6},{9,8},{10,9},{11,10},{13,12},{... | collective-permute-start | bytes 884744 | tf_op jit(solution)/shard_map/ppermute | solution.py:767
  1065.9 4.8 collective-permute-start.48
  1272.8 14.3 collective-permute-start.51
  1275.8 12.4 collective-permute-start.50
  1285.8 2.5 collective-permute-start.49
  (1 other events, 0.7 us)
Sparse Core Ops, SparseCore 0:
  859.4 499.6 all-reduce.3

commit v4 on v3

--- a/solution.py
+++ b/solution.py
@@ -63,7 +63,7 @@
     return gate_r, gate_i, decay, mult, inv_m
 
 
-def first_pass_kernel(n_ref, gz_ref, nh_ref, pos_ref, *rest, n_blk, n_chunk, own, batch):
+def first_pass_kernel(n_ref, gz_ref, nh_ref, pos_ref, *rest, n_blk, n_chunk, own, unroll, batch):
     if own:
         ext, rest = rest[0], rest[1:]
         w_hbm, rest = rest[:3], rest[3:]
@@ -186,7 +186,7 @@
             dots(blk)
             return 0
 
-        if own:
+        if unroll:
             for blk in range(n_blk):
                 both(blk, 0)
         else:
@@ -205,7 +205,7 @@
                     copy.wait()
 
 
-def first_pass(n_blk, normed, gz, n_halo, pos_b, weights, ext=None):
+def first_pass(n_blk, normed, gz, n_halo, pos_b, weights, ext=None, unroll=True):
     own = ext is not None
     n_rows, width = normed.shape
     n_tok, batch = pos_b.shape[0], pos_b.shape[1]
@@ -240,7 +240,7 @@
     in_specs += [any_spec] * len(weights)
     flops = 6 * n_rows * width * cols
     return pl.pallas_call(
-        functools.partial(first_pass_kernel, n_blk=n_blk, n_chunk=n_chunk, own=own, batch=batch),
+        functools.partial(first_pass_kernel, n_blk=n_blk, n_chunk=n_chunk, own=own, unroll=unroll, batch=batch),
         grid=(n_chunk + 1,), in_specs=in_specs, out_specs=out_specs, scratch_shapes=scratch, out_shape=out_shape,
         compiler_params=pltpu.CompilerParams(dimension_semantics=("arbitrary",), vmem_limit_bytes=VMEM_BYTES),
         cost_estimate=pl.CostEstimate(flops=flops, bytes_accessed=n_rows * width * 4, transcendentals=0),
@@ -388,7 +388,7 @@
         return hid
 
     pre_gates(0)
-    lax.fori_loop(0, n_chunk, forward, enter[0])
+    lax.fori_loop(0, n_chunk, forward, enter[0], unroll=True)
 
     def recur(j, carry):
         base = j * TC
@@ -459,7 +459,7 @@
         dgate[:] = dot_nt(dpai[:], wg)
         return (carry, *later)
 
-    vals = lax.fori_loop(0, n_chunk - 1, back, (carry, zero, zero, zero))
+    vals = lax.fori_loop(0, n_chunk - 1, back, (carry, zero, zero, zero), unroll=True)
     later = conv_back(0, vals[1:])
     for k in range(HALO):
         head_out[HALO - 1 - k] = later[k]
@@ -757,7 +757,7 @@
         if kind == "first":
             rows_n = after(normed, last)
             arrays = blocks(calls[idx])
-            *acts, last, ext_f, w16 = first_pass(len(calls[idx]), rows_n, gz_t, n_halo, pos_b, arrays)
+            *acts, last, ext_f, w16 = first_pass(len(calls[idx]), rows_n, gz_t, n_halo, pos_b, arrays, unroll=idx == len(calls) - 1)
             firsts[idx] = acts, entering(last, cp_index, swap_core, swap_x), ext_f
             w_far.append(w16)
             continue

time: 1480 us -> 1470 us (level)
  Pallas kernels: 913 us -> 877 us
  waiting for transfers between devices: 349 us -> 378 us
    pallas_call x4, Pallas kernels: 187 us -> 154 us  [second_pass(): pl.pallas_call(functools.partial(second_pass_kernel, n_chunk=n_chunk, own...]
    psum x1, waiting for transfers between devices: 70.2 us -> 91.5 us  [shard_body(): lax.psum((g_w_x, g_w_y, g_w_out, packed), 'cp')]
  transfers between devices with their start and end apart: 53 -> 53, of which waited for: 14 -> 16; matrix products, arithmetic and copies ran while one was open for 8% -> 8% of each run, Pallas kernels for 50% -> 47%
where the time goes in v4:
time: 1470 us; the launch traced here: 1460 us
  Pallas kernels  877 us (60%)
  waiting for transfers between devices  378 us (26%)
  matrix products  81.2 us (6%)
  starting transfers between devices  52.8 us (4%)
  other arithmetic  32.4 us (2%)
  local copies, waits for them, and re-layouts  27.4 us (2%)
  between operations  14.9 us (1%)
    pallas_call x4, Pallas kernels, first_pass(): pl.pallas_call(functools.partial(first_pass_kernel, n_blk=n_blk, n_chunk=...  372 us
    pallas_call x1, Pallas kernels, norm_back_pass(): pl.pallas_call(functools.partial(norm_back_kernel, n_part=n_part, n_steps...  200 us
    pallas_call x4, Pallas kernels, second_pass(): pl.pallas_call(functools.partial(second_pass_kernel, n_chunk=n_chunk, own...  154 us
    ppermute x6, waiting for transfers between devices, shard_body(): got['y', p, u] = lax.ppermute(mine[2 * p + u], 'tp', to_y)  109 us
    ppermute x6, waiting for transfers between devices, shard_body(): got['z', p, u] = lax.ppermute(mine[2 * p + u], 'tp', to_z)  108 us
    pallas_call x1, Pallas kernels, out_pass(): pl.pallas_call(functools.partial(out_kernel, n_part=n_part, n_steps=n_ste...  96.9 us
    psum x1, waiting for transfers between devices, shard_body(): lax.psum((g_w_x, g_w_y, g_w_out, packed), 'cp')  91.5 us
    dot_general x3, matrix products, dot_tn(): lax.dot_general(lhs, rhs, (((0,), (0,)), ((), ())), preferred_element_typ...  81.2 us
  transfers between devices with their start and end apart: 53, of which 16 were waited for; matrix products, arithmetic and copies ran while one was open for 8% of the time, Pallas kernels for 47%

profile of v4, /device:TPU:0, one launch (start us, length us, event | category | flops | bytes accessed | tf_op | source)
XLA Modules:
  0.0 1463.5 jit_solution(4155011264250259623)
XLA Ops:
  7.2 1.8 slice.255
  9.0 1.3 convert_bitcast_fusion
  10.3 3.7 collective-permute-start
  18.2 1.3 convert_element_type.20
  19.5 1.4 copy.86
  24.1 10.7 send_pass.1
  34.8 1.3 broadcast_add_fusion
  36.1 43.2 %pre_pass.1 = (bf16[128,32,3072]{2,1,0:T(8,128)(2,1)}, bf16[128,32,3072]{2,1,0:T(8,128)(2,1)}, f32[32,128,128]{2,1,0:T(8,128)}, f32[8,3072]{1,0:T(8,128)}) custom-call(bf16[32,128,3072]{2,1,0:T(8,128)(2,1)} %refs_11_.1, bf16[32,128,3072]{2,1,0:T(8,128)(2,1)} %refs_15_.1, f32[1,3072]{1,0:T(1,128)} %bitcast.205), custom_call_target="tpu_custom_call" | custom-call | flops 2516582400 | bytes 100663296 | tf_op jit(solution)/shard_map/pre_pass/pallas_call | solution.py:293
  79.3 1.4 multiply_reduce_fusion
  80.7 2.5 multiply_multiply_fusion
  83.2 3.0 broadcast_in_dim.30.pos_ref
  86.2 86.1 %first_pass_own.1 = (bf16[3,128,32,256]{3,2,1,0:T(8,128)(2,1)}, f32[3,128,32,256]{3,2,1,0:T(8,128)}, f32[3,128,32,256]{3,2,1,0:T(8,128)}, f32[3,128,32,256]{3,2,...) custom-call(bf16[4096,3072]{1,0:T(8,128)(2,1)} %bitcast.213, ...), custom_call_target="tpu_custom_call" | custom-call | flops 57982058496 | bytes 50331648 | tf_op jit(solution)/shard_map/first_pass_own/pallas_call | solution.py:242
  173.3 1.6 collective-permute-start.1
  174.9 1.2 collective-permute-done.1
  177.5 1.6 collective-permute-start.8
  179.0 1.5 collective-permute-start.4
  183.0 45.7 %second_pass_own.1 = (bf16[128,32,768]{2,1,0:T(8,128)(2,1)}, bf16[128,32,768]{2,1,0:T(8,128)(2,1)}, bf16[128,32,768]{2,1,0:T(8,128)(2,1)}, f32[3,32,768]{2,1,0:T...) custom-call(bf16[3,128,32,256]{3,2,1,0:T(8,128)(2,1)} %get-tuple-element.148.c_ref, ...), custom_call_target="tpu_custom_call" | custom-call | flops 37748736000 | bytes 62914560 | tf_op jit(solution)/shard_map/second_pass_own/pallas_call | solution.py:491
  228.7 1.3 collective-permute-start.3
  230.0 26.8 %convolution_bitcast_fusion = f32[3072,768]{1,0:T(8,128)} fusion(bf16[128,32,3072]{2,1,0:T(8,128)(2,1)} %get-tuple-element.146, bf16[128,32,768]{2,1,0:T(8,128)(2,1)} %get-tuple-element.159.refs_4_), kind=kOutput, calls=%fused_computation | convolution fusion | flops 19327352832 | bytes 40894464 | tf_op jit(solution)/shard_map/dot_general | solution.py:43
  256.8 1.5 collective-permute-start.12
  259.4 26.8 %convolution_bitcast_fusion.1 = f32[768,3072]{1,0:T(8,128)} fusion(bf16[128,32,768]{2,1,0:T(8,128)(2,1)} %get-tuple-element.204.refs_0_, bf16[128,32,3072]{2,1,0:T(8,128)(2,1)} %get-tuple-element.147), kind=kOutput, calls=%fused_computation.1 | convolution fusion | flops 19327352832 | bytes 40894464 | tf_op jit(solution)/shard_map/dot_general | solution.py:43
  288.0 2.4 collective-permute-done.5.rest_1_
  290.4 53.6 %collective-permute-done.12.rest_8_ = f32[3,816,256]{2,1,0:T(8,128)S(1)} collective-permute-done((f32[3,816,256]{2,1,0:T(8,128)}, f32[3,816,256]{2,1,0:T(8,128)S(1)}, u32[]{:S(2)}, u32[]{:S(2)}) %collective-permute-start.12) | collective-permute-done | bytes 2506784 | tf_op jit(solution)/shard_map/ppermute | solution.py:720
  344.0 52.7 %collective-permute-done.13.rest_9_ = f32[3,816,256]{2,1,0:T(8,128)} collective-permute-done((f32[3,816,256]{2,1,0:T(8,128)}, f32[3,816,256]{2,1,0:T(8,128)}, u32[]{:S(2)}, u32[]{:S(2)}) %collective-permute-start.13) | collective-permute-done | bytes 2506784 | tf_op jit(solution)/shard_map/ppermute | solution.py:720
  397.2 27.7 %fusion.10 = f32[3072,768]{1,0:T(8,128)} fusion(bf16[4096,3072]{1,0:T(8,128)(2,1)S(1)} %bitcast.219, bf16[4096,768]{1,0:T(8,128)(2,1)} %bitcast.224), kind=kOutput, calls=%fused_computation.72 | convolution fusion | flops 19327352832 | bytes 40894464 | tf_op jit(solution)/shard_map/dot_general | solution.py:43
  425.4 1.5 collective-permute-start.20
  427.5 1.5 collective-permute-start.23
  429.0 97.0 %first_pass_far.3 = (bf16[3,128,32,256]{3,2,1,0:T(8,128)(2,1)}, f32[3,128,32,256]{3,2,1,0:T(8,128)}, f32[3,128,32,256]{3,2,1,0:T(8,128)}, f32[3,128,32,256]{3,2,...) custom-call(bf16[4096,3072]{1,0:T(8,128)(2,1)} %bitcast.214, ...), custom_call_target="tpu_custom_call" | custom-call | flops 57982058496 | bytes 50331648 | tf_op jit(solution)/shard_map/first_pass_far/pallas_call | solution.py:242
  527.0 1.6 collective-permute-done.16
  529.6 1.7 collective-permute-start.17
  531.4 1.6 collective-permute-start.28
  533.0 3.3 collective-permute-done.20.rest_1_
  536.3 1.6 collective-permute-start.24
  537.8 52.2 %collective-permute-done.27.rest_8_ = f32[3,816,256]{2,1,0:T(8,128)} collective-permute-done((f32[3,816,256]{2,1,0:T(8,128)}, f32[3,816,256]{2,1,0:T(8,128)}, u32[]{:S(2)}, u32[]{:S(2)}) %collective-permute-start.27) | collective-permute-done | bytes 2506784 | tf_op jit(solution)/shard_map/ppermute | solution.py:721
  590.5 1.5 collective-permute-start.32
  592.7 51.0 %collective-permute-done.28.rest_9_ = f32[3,816,256]{2,1,0:T(8,128)} collective-permute-done((f32[3,816,256]{2,1,0:T(8,128)}, f32[3,816,256]{2,1,0:T(8,128)}, u32[]{:S(2)}, u32[]{:S(2)}) %collective-permute-start.28) | collective-permute-done | bytes 2506784 | tf_op jit(solution)/shard_map/ppermute | solution.py:721
  644.2 52.3 %collective-permute-done.31.rest_0_ = f32[3,816,256]{2,1,0:T(8,128)} collective-permute-done((f32[3,816,256]{2,1,0:T(8,128)}, f32[3,816,256]{2,1,0:T(8,128)}, u32[]{:S(2)}, u32[]{:S(2)}) %collective-permute-start.31) | collective-permute-done | bytes 2506784 | tf_op jit(solution)/shard_map/ppermute | solution.py:723
  697.0 36.0 %second_pass_far.3 = (bf16[128,32,768]{2,1,0:T(8,128)(2,1)}, bf16[128,32,768]{2,1,0:T(8,128)(2,1)}, bf16[128,32,768]{2,1,0:T(8,128)(2,1)}, f32[3,32,768]{2,1,0:T(8,128)}, f32[3,32,768]{2,1,0:T(8,128)}) custom-call(bf16[3,128,32,256]{3,2,1,0:T(8,128)(2,1)} %get-tuple-element.164.c_ref, f32[3,128,32,256]{3,2,1,0:T(8,128)} %get-tuple-element.165.y_ref, ...), custom_call_target="tpu_custom_call" | custom-call | flops 37748736000 | bytes 62914560 | tf_op jit(solution)/shard_map/second_pass_far/pallas_call | solution.py:491
  733.6 1.5 collective-permute-start.36
  735.1 1.6 collective-permute-start.39
  737.1 96.6 %first_pass_far.4 = (bf16[3,128,32,256]{3,2,1,0:T(8,128)(2,1)}, f32[3,128,32,256]{3,2,1,0:T(8,128)}, f32[3,128,32,256]{3,2,1,0:T(8,128)}, f32[3,128,32,256]{3,2,...) custom-call(bf16[4096,3072]{1,0:T(8,128)(2,1)} %bitcast.215, ...), custom_call_target="tpu_custom_call" | custom-call | flops 57982058496 | bytes 50331648 | tf_op jit(solution)/shard_map/first_pass_far/pallas_call | solution.py:242
  835.4 8.5 collective-permute-done.39.rest_8_
  848.8 2.1 pad_maximum_fusion
  852.6 1.3 collective-permute-start.18
  853.9 2.5 collective-permute-start.44
  856.4 4.7 collective-permute-done.42.rest_11_
  861.0 92.6 %first_pass_far.5 = (bf16[3,128,32,256]{3,2,1,0:T(8,128)(2,1)}, f32[3,128,32,256]{3,2,1,0:T(8,128)}, f32[3,128,32,256]{3,2,1,0:T(8,128)}, f32[3,128,32,256]{3,2,...) custom-call(bf16[4096,3072]{1,0:T(8,128)(2,1)} %bitcast.216, ...), custom_call_target="tpu_custom_call" | custom-call | flops 57982058496 | bytes 50331648 | tf_op jit(solution)/shard_map/first_pass_far/pallas_call | solution.py:242
  957.4 1.7 select_select_fusion
  959.1 1.7 collective-permute-start.47
  960.8 35.9 %second_pass_far.4 = (bf16[128,32,768]{2,1,0:T(8,128)(2,1)}, bf16[128,32,768]{2,1,0:T(8,128)(2,1)}, bf16[128,32,768]{2,1,0:T(8,128)(2,1)}, f32[3,32,768]{2,1,0:T(8,128)}, f32[3,32,768]{2,1,0:T(8,128)}) custom-call(bf16[3,128,32,256]{3,2,1,0:T(8,128)(2,1)} %get-tuple-element.178.c_ref, f32[3,128,32,256]{3,2,1,0:T(8,128)} %get-tuple-element.179.y_ref, ...), custom_call_target="tpu_custom_call" | custom-call | flops 37748736000 | bytes 62914560 | tf_op jit(solution)/shard_map/second_pass_far/pallas_call | solution.py:491
  996.7 1.3 collective-permute-start.45
  999.8 35.9 %second_pass_far.5 = (bf16[128,32,768]{2,1,0:T(8,128)(2,1)}, bf16[128,32,768]{2,1,0:T(8,128)(2,1)}, bf16[128,32,768]{2,1,0:T(8,128)(2,1)}, f32[3,32,768]{2,1,0:T(8,128)}, f32[3,32,768]{2,1,0:T(8,128)}) custom-call(bf16[3,128,32,256]{3,2,1,0:T(8,128)(2,1)} %get-tuple-element.188.c_ref, f32[3,128,32,256]{3,2,1,0:T(8,128)} %get-tuple-element.189.y_ref, ...), custom_call_target="tpu_custom_call" | custom-call | flops 37748736000 | bytes 62914560 | tf_op jit(solution)/shard_map/second_pass_far/pallas_call | solution.py:491
  1035.7 1.3 collective-permute-start.48
  1037.0 1.7 fusion.1.refs_1_
  1038.8 1.7 fusion.2.refs_2_
  1040.5 1.7 fusion.3.refs_3_
  1042.2 200.2 %norm_back_pass.1 = (bf16[32,128,3072]{2,1,0:T(8,128)(2,1)}, f32[8,3072]{1,0:T(8,128)}) custom-call(bf16[128,32,768]{2,1,0:T(8,128)(2,1)} %fusion.refs_0_, bf16[128,32,768]{2,1,0:T(8,128)(2,1)} %fusion.1.refs_1_, bf16[128,32,768]{2,1,0:T(8,128)(2,1)} %fusion.2.refs_2_, bf16[128,32,768]{2,1,0:T(8,128)(2,1)} %fusion.3.refs_3_, ...), custom_call_target="tpu_custom_call" | custom-call | flops 154618822656 | bytes 125829120 | tf_op jit(solution)/shard_map/norm_back_pass/pallas_call | solution.py:666
  1243.4 3.2 collective-permute-start.51
  1246.6 9.6 collective-permute-start.50
  1256.2 1.3 reshape.290
  1257.5 1.1 collective-permute-done.50
  1259.2 91.5 %all-reduce.4.cloned.1.call-done = (f32[3072,768]{1,0:T(8,128)}, f32[3072,768]{1,0:T(8,128)}, f32[768,3072]{1,0:T(8,128)}, f32[816,256]{1,0:T(8,128)}) async-done(((f32[3072,768]{1,0:T(8,128)}, f32[3072,768]{1,0:T(8,128)}, f32[768,3072]{1,0:T(8,128)}, f32[816,256]{1,0:T(8,128)}), (f32[3072,768]{1,0:T(8,128)}, f32[3072,768]{1,0:T(8,128)}, f32[768,3072]{1,0:T(8,128)}, ...) | async-done | bytes 29147152 | tf_op jit(solution)/shard_map/psum | solution.py:779
  1352.4 1.2 slice.332
  1359.3 96.9 %out_pass.1 = (bf16[32,128,3072]{2,1,0:T(8,128)(2,1)}, f32[3072,768]{1,0:T(8,128)}, f32[3072,768]{1,0:T(8,128)}, f32[768,3072]{1,0:T(8,128)}) custom-call(bf16[128,32,768]{2,1,0:T(8,128)(2,1)} %get-tuple-element.204.refs_0_, bf16[128,32,768]{2,1,0:T(8,128)(2,1)} %get-tuple-element.172.refs_1_, bf16[128,32,768]{2,1,0:T(8,128)(2,1)} %get-tuple-element.187.refs_2_, ...), custom_call_target="tpu_custom_call" | custom-call | flops 77309411328 | bytes 100663296 | tf_op jit(solution)/shard_map/out_pass/pallas_call | solution.py:564
  (159 shorter events, 44.7 us)
Async XLA Ops:
  7.2 1343.5 %all-reduce.4.cloned.1.call-start = ((), (), s32[]{:S(2)}) async-start(), calls=%async_computation | async-start | bytes 58294272 | tf_op jit(solution)/shard_map/psum | solution.py:779
  10.3 68.9 %collective-permute-start = (f32[3,32,3072]{2,1,0:T(8,128)}, f32[3,32,3072]{2,1,0:T(8,128)}, u32[]{:S(2)}, u32[]{:S(2)}) collective-permute-start(f32[3,32,3072]{2,1,0:T(8,128)} %convert_bitcast_fusion), channel_id=1, source_target_pairs={{0,1},{1,2},{2,3},{4,5},{5,6},{6,7},{8,9},{9,10},{10,11},{12,13},{... | collective-permute-start | bytes 3538952 | tf_op jit(solution)/shard_map/ppermute | solution.py:713
  173.3 2.8 collective-permute-start.1
  177.2 5.1 collective-permute-start.2
  177.5 80.8 %collective-permute-start.8 = (f32[3,816,256]{2,1,0:T(8,128)}, f32[3,816,256]{2,1,0:T(8,128)}, u32[]{:S(2)}, u32[]{:S(2)}) collective-permute-start(f32[3,816,256]{2,1,0:T(8,128)} %get-tuple-element.139), channel_id=1, source_target_pairs={{0,8},{4,12},{8,0},{12,4},{1,9},{5,13},{9,1},{13,5},{2,10},{6,14},... | collective-permute-start | bytes 7520264 | tf_op jit(solution)/shard_map/ppermute | solution.py:721
  179.0 79.8 %collective-permute-start.4 = (f32[3,816,256]{2,1,0:T(8,128)}, f32[3,816,256]{2,1,0:T(8,128)}, u32[]{:S(2)}, u32[]{:S(2)}) collective-permute-start(f32[3,816,256]{2,1,0:T(8,128)} %get-tuple-element.139), channel_id=1, source_target_pairs={{0,4},{4,0},{8,12},{12,8},{1,5},{5,1},{9,13},{13,9},{2,6},{6,2},{1... | collective-permute-start | bytes 7520264 | tf_op jit(solution)/shard_map/ppermute | solution.py:720
  180.6 107.4 %collective-permute-start.9 = (f32[3,816,256]{2,1,0:T(8,128)}, f32[3,816,256]{2,1,0:T(8,128)}, u32[]{:S(2)}, u32[]{:S(2)}) collective-permute-start(f32[3,816,256]{2,1,0:T(8,128)} %get-tuple-element.140), channel_id=1, source_target_pairs={{0,8},{4,12},{8,0},{12,4},{1,9},{5,13},{9,1},{13,5},{2,10},{6,14},... | collective-permute-start | bytes 7520264 | tf_op jit(solution)/shard_map/ppermute | solution.py:721
  181.0 109.3 %collective-permute-start.5 = (f32[3,816,256]{2,1,0:T(8,128)}, f32[3,816,256]{2,1,0:T(8,128)}, u32[]{:S(2)}, u32[]{:S(2)}) collective-permute-start(f32[3,816,256]{2,1,0:T(8,128)} %get-tuple-element.140), channel_id=1, source_target_pairs={{0,4},{4,0},{8,12},{12,8},{1,5},{5,1},{9,13},{13,9},{2,6},{6,2},{1... | collective-permute-start | bytes 7520264 | tf_op jit(solution)/shard_map/ppermute | solution.py:720
  228.7 28.1 %collective-permute-start.3 = (f32[3,32,768]{2,1,0:T(8,128)}, f32[3,32,768]{2,1,0:T(8,128)S(1)}, u32[]{:S(2)}, u32[]{:S(2)}) collective-permute-start(f32[3,32,768]{2,1,0:T(8,128)} %get-tuple-element.158), channel_id=1, source_target_pairs={{1,0},{2,1},{3,2},{5,4},{6,5},{7,6},{9,8},{10,9},{11,10},{13,12},{... | collective-permute-start | bytes 884744 | tf_op jit(solution)/shard_map/ppermute | solution.py:746
  230.0 167.2 %slice-start = ((s8[25165824]{0:T(1024)(128)(4,1)}), s8[4194304]{0:T(1024)(128)(4,1)S(1)}, s32[]{:S(2)}) async-start(s8[25165824]{0:T(1024)(128)(4,1)} %bitcast.217), calls=%async_computation.1 | async-start | bytes 8388608
  230.0 167.2 %slice-start.1 = ((s8[25165824]{0:T(1024)(128)(4,1)}), s8[4194304]{0:T(1024)(128)(4,1)S(1)}, s32[]{:S(2)}) async-start(s8[25165824]{0:T(1024)(128)(4,1)} %bitcast.217), calls=%async_computation.2 | async-start | bytes 8388608
  230.0 167.2 %slice-start.2 = ((s8[25165824]{0:T(1024)(128)(4,1)}), s8[4194304]{0:T(1024)(128)(4,1)S(1)}, s32[]{:S(2)}) async-start(s8[25165824]{0:T(1024)(128)(4,1)} %bitcast.217), calls=%async_computation.3 | async-start | bytes 8388608
  256.8 29.4 %copy-start.3 = (f32[3,32,768]{2,1,0:T(8,128)}, f32[3,32,768]{2,1,0:T(8,128)S(1)}, u32[]{:S(2)}) copy-start(f32[3,32,768]{2,1,0:T(8,128)S(1)} %collective-permute-done.3) | copy-start | bytes 884740
  256.8 87.2 %collective-permute-start.12 = (f32[3,816,256]{2,1,0:T(8,128)}, f32[3,816,256]{2,1,0:T(8,128)S(1)}, u32[]{:S(2)}, u32[]{:S(2)}) collective-permute-start(f32[3,816,256]{2,1,0:T(8,128)} %get-tuple-element.141), channel_id=1, source_target_pairs={{0,4},{4,0},{8,12},{12,8},{1,5},{5,1},{9,13},{13,9},{2,6},{6,2},{1... | collective-permute-start | bytes 7520264 | tf_op jit(solution)/shard_map/ppermute | solution.py:720
  258.3 138.4 %collective-permute-start.13 = (f32[3,816,256]{2,1,0:T(8,128)}, f32[3,816,256]{2,1,0:T(8,128)}, u32[]{:S(2)}, u32[]{:S(2)}) collective-permute-start(f32[3,816,256]{2,1,0:T(8,128)} %get-tuple-element.142), channel_id=1, source_target_pairs={{0,4},{4,0},{8,12},{12,8},{1,5},{5,1},{9,13},{13,9},{2,6},{6,2},{1... | collective-permute-start | bytes 7520264 | tf_op jit(solution)/shard_map/ppermute | solution.py:720
  258.8 137.8 %collective-permute-start.10 = (f32[3,816,256]{2,1,0:T(8,128)}, f32[3,816,256]{2,1,0:T(8,128)}, u32[]{:S(2)}, u32[]{:S(2)}) collective-permute-start(f32[3,816,256]{2,1,0:T(8,128)} %collective-permute-done.8.rest_4_), channel_id=1, source_target_pairs={{0,1},{1,0},{2,3},{3,2},{4,5},{5,4},{6,7},{7,6},{8,9},{9,8},{10,11... | collective-permute-start | bytes 7520264 | tf_op jit(solution)/shard_map/ppermute | solution.py:732
  259.4 26.8 %copy-start.4 = (f32[3,32,768]{2,1,0:T(8,128)S(1)}, f32[3,32,768]{2,1,0:T(8,128)}, u32[]{:S(2)}) copy-start(f32[3,32,768]{2,1,0:T(8,128)} %get-tuple-element.157) | copy-start | bytes 884740
  259.4 137.8 %slice-start.3 = ((s8[25165824]{0:T(1024)(128)(4,1)}), s8[4194304]{0:T(1024)(128)(4,1)S(1)}, s32[]{:S(2)}) async-start(s8[25165824]{0:T(1024)(128)(4,1)} %bitcast.217), calls=%async_computation.4 | async-start | bytes 8388608
  259.4 137.8 %slice-start.4 = ((s8[25165824]{0:T(1024)(128)(4,1)}), s8[4194304]{0:T(1024)(128)(4,1)S(1)}, s32[]{:S(2)}) async-start(s8[25165824]{0:T(1024)(128)(4,1)} %bitcast.217), calls=%async_computation.5 | async-start | bytes 8388608
  259.4 137.8 %slice-start.5 = ((s8[25165824]{0:T(1024)(128)(4,1)}), s8[4194304]{0:T(1024)(128)(4,1)S(1)}, s32[]{:S(2)}) async-start(s8[25165824]{0:T(1024)(128)(4,1)} %bitcast.217), calls=%async_computation.6 | async-start | bytes 8388608
  288.0 137.0 %collective-permute-start.6 = (f32[3,816,256]{2,1,0:T(8,128)}, f32[3,816,256]{2,1,0:T(8,128)}, u32[]{:S(2)}, u32[]{:S(2)}) collective-permute-start(f32[3,816,256]{2,1,0:T(8,128)} %collective-permute-done.4.rest_0_), channel_id=1, source_target_pairs={{0,1},{1,0},{2,3},{3,2},{4,5},{5,4},{6,7},{7,6},{8,9},{9,8},{10,11... | collective-permute-start | bytes 7520264 | tf_op jit(solution)/shard_map/ppermute | solution.py:732
  290.3 135.1 %collective-permute-start.11 = (f32[3,816,256]{2,1,0:T(8,128)}, f32[3,816,256]{2,1,0:T(8,128)}, u32[]{:S(2)}, u32[]{:S(2)}) collective-permute-start(f32[3,816,256]{2,1,0:T(8,128)} %collective-permute-done.9.rest_5_), channel_id=1, source_target_pairs={{0,1},{1,0},{2,3},{3,2},{4,5},{5,4},{6,7},{7,6},{8,9},{9,8},{10,11... | collective-permute-start | bytes 7520264 | tf_op jit(solution)/shard_map/ppermute | solution.py:732
  344.0 81.0 %copy-start.5 = (f32[3,816,256]{2,1,0:T(8,128)}, f32[3,816,256]{2,1,0:T(8,128)S(1)}, u32[]{:S(2)}) copy-start(f32[3,816,256]{2,1,0:T(8,128)S(1)} %collective-permute-done.12.rest_8_) | copy-start | bytes 7520260
  344.0 83.0 %collective-permute-start.7 = (f32[3,816,256]{2,1,0:T(8,128)}, f32[3,816,256]{2,1,0:T(8,128)}, u32[]{:S(2)}, u32[]{:S(2)}) collective-permute-start(f32[3,816,256]{2,1,0:T(8,128)} %collective-permute-done.5.rest_1_), channel_id=1, source_target_pairs={{0,1},{1,0},{2,3},{3,2},{4,5},{5,4},{6,7},{7,6},{8,9},{9,8},{10,11... | collective-permute-start | bytes 7520264 | tf_op jit(solution)/shard_map/ppermute | solution.py:732
  396.7 30.8 %collective-permute-start.14 = (f32[3,816,256]{2,1,0:T(8,128)S(1)}, f32[3,816,256]{2,1,0:T(8,128)}, u32[]{:S(2)}, u32[]{:S(2)}) collective-permute-start(f32[3,816,256]{2,1,0:T(8,128)S(1)} %collective-permute-done.12.rest_8_), channel_id=1, source_target_pairs={{0,1},{1,0},{2,3},{3,2},{4,5},{5,4},{6,7},{7,6},{8,9},{9,8},{10,11... | collective-permute-start | bytes 7520264 | tf_op jit(solution)/shard_map/ppermute | solution.py:732
  396.7 32.3 %collective-permute-start.15 = (f32[3,816,256]{2,1,0:T(8,128)}, f32[3,816,256]{2,1,0:T(8,128)}, u32[]{:S(2)}, u32[]{:S(2)}) collective-permute-start(f32[3,816,256]{2,1,0:T(8,128)} %collective-permute-done.13.rest_9_), channel_id=1, source_target_pairs={{0,1},{1,0},{2,3},{3,2},{4,5},{5,4},{6,7},{7,6},{8,9},{9,8},{10,11... | collective-permute-start | bytes 7520264 | tf_op jit(solution)/shard_map/ppermute | solution.py:732
  424.9 106.4 %collective-permute-start.19 = (f32[3,816,256]{2,1,0:T(8,128)}, f32[3,816,256]{2,1,0:T(8,128)}, u32[]{:S(2)}, u32[]{:S(2)}) collective-permute-start(f32[3,816,256]{2,1,0:T(8,128)} %get-tuple-element.141), channel_id=1, source_target_pairs={{0,8},{4,12},{8,0},{12,4},{1,9},{5,13},{9,1},{13,5},{2,10},{6,14},... | collective-permute-start | bytes 7520264 | tf_op jit(solution)/shard_map/ppermute | solution.py:721
  425.4 110.8 %collective-permute-start.20 = (f32[3,816,256]{2,1,0:T(8,128)}, f32[3,816,256]{2,1,0:T(8,128)}, u32[]{:S(2)}, u32[]{:S(2)}) collective-permute-start(f32[3,816,256]{2,1,0:T(8,128)} %get-tuple-element.142), channel_id=1, source_target_pairs={{0,8},{4,12},{8,0},{12,4},{1,9},{5,13},{9,1},{13,5},{2,10},{6,14},... | collective-permute-start | bytes 7520264 | tf_op jit(solution)/shard_map/ppermute | solution.py:721
  427.0 163.0 %collective-permute-start.27 = (f32[3,816,256]{2,1,0:T(8,128)}, f32[3,816,256]{2,1,0:T(8,128)}, u32[]{:S(2)}, u32[]{:S(2)}) collective-permute-start(f32[3,816,256]{2,1,0:T(8,128)} %get-tuple-element.143), channel_id=1, source_target_pairs={{0,8},{4,12},{8,0},{12,4},{1,9},{5,13},{9,1},{13,5},{2,10},{6,14},... | collective-permute-start | bytes 7520264 | tf_op jit(solution)/shard_map/ppermute | solution.py:721
  427.5 163.0 %collective-permute-start.23 = (f32[3,816,256]{2,1,0:T(8,128)}, f32[3,816,256]{2,1,0:T(8,128)}, u32[]{:S(2)}, u32[]{:S(2)}) collective-permute-start(f32[3,816,256]{2,1,0:T(8,128)} %get-tuple-element.143), channel_id=1, source_target_pairs={{0,4},{4,0},{8,12},{12,8},{1,5},{5,1},{9,13},{13,9},{2,6},{6,2},{1... | collective-permute-start | bytes 7520264 | tf_op jit(solution)/shard_map/ppermute | solution.py:720
  527.0 1.6 collective-permute-start.16
  529.6 62.3 %collective-permute-start.17 = (f32[3,32,256]{2,1,0:T(8,128)S(1)}, f32[3,32,256]{2,1,0:T(8,128)S(1)}, u32[]{:S(2)}, u32[]{:S(2)}) collective-permute-start(f32[3,32,256]{2,1,0:T(8,128)S(1)} %select_select_fusion.2), channel_id=1, source_target_pairs={{0,2},{1,3},{2,0},{3,1},{4,6},{5,7},{6,4},{7,5},{8,10},{9,11},{10,... | collective-permute-start | bytes 294920 | tf_op jit(solution)/shard_map/ppermute | solution.py:690
  531.4 112.3 %collective-permute-start.28 = (f32[3,816,256]{2,1,0:T(8,128)}, f32[3,816,256]{2,1,0:T(8,128)}, u32[]{:S(2)}, u32[]{:S(2)}) collective-permute-start(f32[3,816,256]{2,1,0:T(8,128)} %get-tuple-element.144), channel_id=1, source_target_pairs={{0,8},{4,12},{8,0},{12,4},{1,9},{5,13},{9,1},{13,5},{2,10},{6,14},... | collective-permute-start | bytes 7520264 | tf_op jit(solution)/shard_map/ppermute | solution.py:721
  536.3 107.4 %collective-permute-start.24 = (f32[3,816,256]{2,1,0:T(8,128)}, f32[3,816,256]{2,1,0:T(8,128)}, u32[]{:S(2)}, u32[]{:S(2)}) collective-permute-start(f32[3,816,256]{2,1,0:T(8,128)} %get-tuple-element.144), channel_id=1, source_target_pairs={{0,4},{4,0},{8,12},{12,8},{1,5},{5,1},{9,13},{13,9},{2,6},{6,2},{1... | collective-permute-start | bytes 7520264 | tf_op jit(solution)/shard_map/ppermute | solution.py:720
  590.0 106.5 %collective-permute-start.31 = (f32[3,816,256]{2,1,0:T(8,128)}, f32[3,816,256]{2,1,0:T(8,128)}, u32[]{:S(2)}, u32[]{:S(2)}) collective-permute-start(f32[3,816,256]{2,1,0:T(8,128)} %collective-permute-done.4.rest_0_), channel_id=1, source_target_pairs={{0,8},{4,12},{8,0},{12,4},{1,9},{5,13},{9,1},{13,5},{2,10},{6,14},... | collective-permute-start | bytes 7520264 | tf_op jit(solution)/shard_map/ppermute | solution.py:723
  590.5 106.0 %collective-permute-start.32 = (f32[3,816,256]{2,1,0:T(8,128)}, f32[3,816,256]{2,1,0:T(8,128)}, u32[]{:S(2)}, u32[]{:S(2)}) collective-permute-start(f32[3,816,256]{2,1,0:T(8,128)} %collective-permute-done.9.rest_5_), channel_id=1, source_target_pairs={{0,4},{4,0},{8,12},{12,8},{1,5},{5,1},{9,13},{13,9},{2,6},{6,2},{1... | collective-permute-start | bytes 7520264 | tf_op jit(solution)/shard_map/ppermute | solution.py:724
  592.0 105.0 %collective-permute-start.21 = (f32[3,816,256]{2,1,0:T(8,128)}, f32[3,816,256]{2,1,0:T(8,128)}, u32[]{:S(2)}, u32[]{:S(2)}) collective-permute-start(f32[3,816,256]{2,1,0:T(8,128)} %collective-permute-done.19.rest_0_), channel_id=1, source_target_pairs={{0,1},{1,0},{2,3},{3,2},{4,5},{5,4},{6,7},{7,6},{8,9},{9,8},{10,11... | collective-permute-start | bytes 7520264 | tf_op jit(solution)/shard_map/ppermute | solution.py:732
  643.7 89.3 %collective-permute-start.22 = (f32[3,816,256]{2,1,0:T(8,128)}, f32[3,816,256]{2,1,0:T(8,128)}, u32[]{:S(2)}, u32[]{:S(2)}) collective-permute-start(f32[3,816,256]{2,1,0:T(8,128)} %collective-permute-done.20.rest_1_), channel_id=1, source_target_pairs={{0,1},{1,0},{2,3},{3,2},{4,5},{5,4},{6,7},{7,6},{8,9},{9,8},{10,11... | collective-permute-start | bytes 7520264 | tf_op jit(solution)/shard_map/ppermute | solution.py:732
  643.7 89.9 %collective-permute-start.29 = (f32[3,816,256]{2,1,0:T(8,128)}, f32[3,816,256]{2,1,0:T(8,128)}, u32[]{:S(2)}, u32[]{:S(2)}) collective-permute-start(f32[3,816,256]{2,1,0:T(8,128)} %collective-permute-done.27.rest_8_), channel_id=1, source_target_pairs={{0,1},{1,0},{2,3},{3,2},{4,5},{5,4},{6,7},{7,6},{8,9},{9,8},{10,11... | collective-permute-start | bytes 7520264 | tf_op jit(solution)/shard_map/ppermute | solution.py:732
  696.5 38.6 %collective-permute-start.25 = (f32[3,816,256]{2,1,0:T(8,128)}, f32[3,816,256]{2,1,0:T(8,128)}, u32[]{:S(2)}, u32[]{:S(2)}) collective-permute-start(f32[3,816,256]{2,1,0:T(8,128)} %collective-permute-done.23.rest_4_), channel_id=1, source_target_pairs={{0,1},{1,0},{2,3},{3,2},{4,5},{5,4},{6,7},{7,6},{8,9},{9,8},{10,11... | collective-permute-start | bytes 7520264 | tf_op jit(solution)/shard_map/ppermute | solution.py:732
  696.5 40.2 %collective-permute-start.30 = (f32[3,816,256]{2,1,0:T(8,128)}, f32[3,816,256]{2,1,0:T(8,128)}, u32[]{:S(2)}, u32[]{:S(2)}) collective-permute-start(f32[3,816,256]{2,1,0:T(8,128)} %collective-permute-done.28.rest_9_), channel_id=1, source_target_pairs={{0,1},{1,0},{2,3},{3,2},{4,5},{5,4},{6,7},{7,6},{8,9},{9,8},{10,11... | collective-permute-start | bytes 7520264 | tf_op jit(solution)/shard_map/ppermute | solution.py:732
  697.0 40.1 %collective-permute-start.26 = (f32[3,816,256]{2,1,0:T(8,128)}, f32[3,816,256]{2,1,0:T(8,128)}, u32[]{:S(2)}, u32[]{:S(2)}) collective-permute-start(f32[3,816,256]{2,1,0:T(8,128)} %collective-permute-done.24.rest_5_), channel_id=1, source_target_pairs={{0,1},{1,0},{2,3},{3,2},{4,5},{5,4},{6,7},{7,6},{8,9},{9,8},{10,11... | collective-permute-start | bytes 7520264 | tf_op jit(solution)/shard_map/ppermute | solution.py:732
  733.0 101.7 %collective-permute-start.35 = (f32[3,816,256]{2,1,0:T(8,128)}, f32[3,816,256]{2,1,0:T(8,128)}, u32[]{:S(2)}, u32[]{:S(2)}) collective-permute-start(f32[3,816,256]{2,1,0:T(8,128)} %copy-done.5), channel_id=1, source_target_pairs={{0,8},{4,12},{8,0},{12,4},{1,9},{5,13},{9,1},{13,5},{2,10},{6,14},... | collective-permute-start | bytes 7520264 | tf_op jit(solution)/shard_map/ppermute | solution.py:723
  733.6 101.8 %collective-permute-start.36 = (f32[3,816,256]{2,1,0:T(8,128)}, f32[3,816,256]{2,1,0:T(8,128)}, u32[]{:S(2)}, u32[]{:S(2)}) collective-permute-start(f32[3,816,256]{2,1,0:T(8,128)} %collective-permute-done.20.rest_1_), channel_id=1, source_target_pairs={{0,4},{4,0},{8,12},{12,8},{1,5},{5,1},{9,13},{13,9},{2,6},{6,2},{1... | collective-permute-start | bytes 7520264 | tf_op jit(solution)/shard_map/ppermute | solution.py:724
  735.1 108.8 %collective-permute-start.39 = (f32[3,816,256]{2,1,0:T(8,128)}, f32[3,816,256]{2,1,0:T(8,128)}, u32[]{:S(2)}, u32[]{:S(2)}) collective-permute-start(f32[3,816,256]{2,1,0:T(8,128)} %collective-permute-done.23.rest_4_), channel_id=1, source_target_pairs={{0,8},{4,12},{8,0},{12,4},{1,9},{5,13},{9,1},{13,5},{2,10},{6,14},... | collective-permute-start | bytes 7520264 | tf_op jit(solution)/shard_map/ppermute | solution.py:723
  736.7 107.4 %collective-permute-start.40 = (f32[3,816,256]{2,1,0:T(8,128)}, f32[3,816,256]{2,1,0:T(8,128)}, u32[]{:S(2)}, u32[]{:S(2)}) collective-permute-start(f32[3,816,256]{2,1,0:T(8,128)} %collective-permute-done.28.rest_9_), channel_id=1, source_target_pairs={{0,4},{4,0},{8,12},{12,8},{1,5},{5,1},{9,13},{13,9},{2,6},{6,2},{1... | collective-permute-start | bytes 7520264 | tf_op jit(solution)/shard_map/ppermute | solution.py:724
  737.1 107.5 %collective-permute-start.33 = (f32[3,816,256]{2,1,0:T(8,128)}, f32[3,816,256]{2,1,0:T(8,128)}, u32[]{:S(2)}, u32[]{:S(2)}) collective-permute-start(f32[3,816,256]{2,1,0:T(8,128)} %collective-permute-done.31.rest_0_), channel_id=1, source_target_pairs={{0,1},{1,0},{2,3},{3,2},{4,5},{5,4},{6,7},{7,6},{8,9},{9,8},{10,11... | collective-permute-start | bytes 7520264 | tf_op jit(solution)/shard_map/ppermute | solution.py:732
  834.7 9.7 collective-permute-start.43
  835.4 17.2 %collective-permute-start.34 = (f32[3,816,256]{2,1,0:T(8,128)}, f32[3,816,256]{2,1,0:T(8,128)}, u32[]{:S(2)}, u32[]{:S(2)}) collective-permute-start(f32[3,816,256]{2,1,0:T(8,128)} %collective-permute-done.32.rest_1_), channel_id=1, source_target_pairs={{0,1},{1,0},{2,3},{3,2},{4,5},{5,4},{6,7},{7,6},{8,9},{9,8},{10,11... | collective-permute-start | bytes 7520264 | tf_op jit(solution)/shard_map/ppermute | solution.py:732
  843.9 10.0 collective-permute-start.37
  844.1 12.3 collective-permute-start.38
  844.4 6.5 copy-start
  844.4 12.0 collective-permute-start.41
  844.6 16.4 %collective-permute-start.42 = (f32[3,816,256]{2,1,0:T(8,128)}, f32[3,816,256]{2,1,0:T(8,128)}, u32[]{:S(2)}, u32[]{:S(2)}) collective-permute-start(f32[3,816,256]{2,1,0:T(8,128)} %collective-permute-done.40.rest_9_), channel_id=1, source_target_pairs={{0,1},{1,0},{2,3},{3,2},{4,5},{5,4},{6,7},{7,6},{8,9},{9,8},{10,11... | collective-permute-start | bytes 7520264 | tf_op jit(solution)/shard_map/ppermute | solution.py:732
  850.9 1.0 copy-start.1
  852.6 184.5 %collective-permute-start.18 = (f32[3,32,768]{2,1,0:T(8,128)}, f32[3,32,768]{2,1,0:T(8,128)}, u32[]{:S(2)}, u32[]{:S(2)}) collective-permute-start(f32[3,32,768]{2,1,0:T(8,128)} %get-tuple-element.171), channel_id=1, source_target_pairs={{1,0},{2,1},{3,2},{5,4},{6,5},{7,6},{9,8},{10,9},{11,10},{13,12},{... | collective-permute-start | bytes 884744 | tf_op jit(solution)/shard_map/ppermute | solution.py:767
  853.9 101.0 %collective-permute-start.44 = (f32[3,32,256]{2,1,0:T(8,128)}, f32[3,32,256]{2,1,0:T(8,128)}, u32[]{:S(2)}, u32[]{:S(2)}) collective-permute-start(f32[3,32,256]{2,1,0:T(8,128)} %select_select_fusion.1), channel_id=1, source_target_pairs={{0,2},{1,3},{2,0},{3,1},{4,6},{5,7},{6,4},{7,5},{8,10},{9,11},{10,... | collective-permute-start | bytes 294920 | tf_op jit(solution)/shard_map/ppermute | solution.py:690
  954.6 2.1 collective-permute-start.46
  959.1 38.9 %collective-permute-start.47 = (f32[3,32,256]{2,1,0:T(8,128)}, f32[3,32,256]{2,1,0:T(8,128)}, u32[]{:S(2)}, u32[]{:S(2)}) collective-permute-start(f32[3,32,256]{2,1,0:T(8,128)} %select_select_fusion), channel_id=1, source_target_pairs={{0,2},{1,3},{2,0},{3,1},{4,6},{5,7},{6,4},{7,5},{8,10},{9,11},{10,... | collective-permute-start | bytes 294920 | tf_op jit(solution)/shard_map/ppermute | solution.py:690
  996.7 42.1 %collective-permute-start.45 = (f32[3,32,768]{2,1,0:T(8,128)}, f32[3,32,768]{2,1,0:T(8,128)}, u32[]{:S(2)}, u32[]{:S(2)}) collective-permute-start(f32[3,32,768]{2,1,0:T(8,128)} %get-tuple-element.185), channel_id=1, source_target_pairs={{1,0},{2,1},{3,2},{5,4},{6,5},{7,6},{9,8},{10,9},{11,10},{13,12},{... | collective-permute-start | bytes 884744 | tf_op jit(solution)/shard_map/ppermute | solution.py:767
  1035.7 4.8 collective-permute-start.48
  1243.4 14.1 collective-permute-start.51
  1246.6 12.1 collective-permute-start.50
  1256.2 2.4 collective-permute-start.49
  (1 other events, 0.7 us)
Sparse Core Ops, SparseCore 0:
  851.1 499.5 all-reduce.3
